TPU v7x, 256 devices: a whole 4x4x8 slice. The times are simulated.
256 devices in a mesh: gx: 32 (over y, z), gy: 8 (over x, core).
Axes of the slice: x: 4, y: 4, z: 8, core: 2. Of those that a mesh axis runs over, the one named last changes fastest.
Arguments:
- right_side: float32 [64, 128, 4, 3, 128], P('gx', 'gy'), may hold values from -6 to 6
- stencil: float32 [27, 3, 3], replicated, as said below
- class_scale: float32 [8], replicated, may hold values from 0.5 to 4
- material: int32 [64, 128, 128], P('gx', 'gy'), may hold values from 0 to 7
- boundary: int32 [64, 128, 128], P('gx', 'gy'), may hold values 0 or 1
- sign_bits: int32 [64, 128, 3, 128], P('gx', 'gy'), may hold values from 0 to 1
- sample_rows: int32 [32, 8, 128], P('gx', 'gy'), may hold values from 0 to 12287
Outputs:
- solution: float32 [64, 128, 4, 3, 128], P('gx', 'gy')
- residual: float32 [64, 128, 4, 3, 128], P('gx', 'gy')
Inputs may be any that keep to these rules, and one draw needn't show every extreme that they name: In every row of the centre block stencil[13], the diagonal entry exceeds the sum of the magnitudes of all other entries of that row over all 27 blocks.
All inputs are finite; a program needn't handle non-finite values. No bound on the sum of `boundary` on one device may be relied on, other than what follows from the above.
Results may differ from a plain program's by a relative error of at most 0.0028.
Values sent between devices are 32-bit elements; how exact they have to be, the bound alone decides.
No kernel may reach another device: no remote copies, remote signals or barrier semaphores. Data moves between devices by JAX's collectives and lax.ppermute only.
A program may use at most 64 MiB of HBM per device.

v0:
```python
import math

import jax
import jax.numpy as jnp
from jax import lax
from jax.sharding import Mesh
from jax.sharding import PartitionSpec as P

STEPS = 8
GX_GY = ("gx_0", "gx_1", "gy_0", "gy_1")
GX = ("gx_0", "gx_1")
GY = ("gy_0", "gy_1")


exact_mode = lax.Precision.HIGHEST


def padded_2(cells, sides, width):
    for axis, dim in sides:
        count = lax.axis_size(axis)
        ends = count - 1
        head = lax.slice_in_dim(cells, 0, width, axis=dim)
        tail = lax.slice_in_dim(cells, cells.shape[dim] - width, cells.shape[dim], axis=dim)
        cells = jnp.concatenate(
            [
                lax.ppermute(tail, axis, [(i, (i + 1) % count) for i in range(ends)]),
                cells,
                lax.ppermute(head, axis, [((i + 1) % count, i) for i in range(ends)]),
            ],
            axis=dim,
        )
    return cells


def one_axis_at_a_time(shard, axes):
    for axis in axes:
        shard = lax.psum(shard, axis)
    return shard


def hadamard_table():
    lanes = jnp.arange(128, dtype=jnp.int32)
    common = lanes[:, None] & lanes[None, :]
    parity = jnp.zeros((128, 128), jnp.int32)
    for bit in range(7):
        parity = parity + (common >> bit & 1)
    return (1 - 2 * (parity % 2)).astype(jnp.float32) / math.sqrt(128.0)


def material_scale(material, class_scale):
    scale_field = jnp.zeros(material.shape, jnp.float32)
    for number in range(class_scale.shape[0]):
        scale_field = scale_field + jnp.where(
            material == number, class_scale[number], jnp.float32(0.0)
        )
    return scale_field


def extend(field):
    return padded_2(field, ((GX, 0), (GY, 1)), 1)


def operate(field, stencil, scale_field, boundary):
    padded = jnp.pad(extend(field), ((0, 0), (0, 0), (0, 0), (0, 0), (1, 1)))
    extent_x, extent_y, extent_z = (field.shape[0], field.shape[1], field.shape[4])
    summed = jnp.zeros(field.shape, jnp.float32)
    for offset_x in range(3):
        for offset_y in range(3):
            for offset_z in range(3):
                shifted = padded[
                    offset_x : offset_x + extent_x,
                    offset_y : offset_y + extent_y,
                    :,
                    :,
                    offset_z : offset_z + extent_z,
                ]
                coupling = stencil[offset_x * 9 + offset_y * 3 + offset_z]
                summed = summed + jnp.sum(
                    coupling[:, :, None] * shifted[:, :, :, None, :, :], axis=4
                )
    return jnp.where(
        boundary[:, :, None, None, :] == 1, field, scale_field[:, :, None, None, :] * summed
    )


def sketch_local(field, sign_field, picks, table):
    pick_x, pick_y, pick_comp, pick_block, pick_lane = picks
    signed = field * sign_field[:, :, None, :, :]
    tiled = signed.reshape(field.shape[:4] + (field.shape[4] // 128, 128))
    chosen = tiled[pick_x, pick_y, :, pick_comp, pick_block]
    return jnp.sum(chosen * table[pick_lane][:, None, :], axis=-1)


def back_substitute(triangle, projected):
    count = triangle.shape[0]

    def one_row(step, unknowns):
        row = count - 1 - step
        line = triangle[row]
        total = jnp.dot(line[None, :], unknowns, precision=exact_mode)[0]
        value = (projected[row] - total) / line[row]
        return unknowns.at[row].set(value)

    return lax.fori_loop(0, count, one_row, jnp.zeros(projected.shape, jnp.float32))


def solve_small(matrix, rhs):
    count = matrix.shape[1]
    columns = matrix.T

    def one_column(column, state_pair):
        orthonormal, triangle = state_pair
        vector = columns[column]
        first_pass = jnp.dot(orthonormal.T, vector, precision=exact_mode)
        vector = vector - jnp.dot(orthonormal, first_pass, precision=exact_mode)
        second_pass = jnp.dot(orthonormal.T, vector, precision=exact_mode)
        vector = vector - jnp.dot(orthonormal, second_pass, precision=exact_mode)
        length = jnp.sqrt(jnp.sum(vector * vector) + 1e-06)
        orthonormal = orthonormal.at[:, column].set(vector / length)
        triangle = triangle.at[:, column].set((first_pass + second_pass).at[column].set(length))
        return (orthonormal, triangle)

    start = (jnp.zeros(matrix.shape, jnp.float32), jnp.zeros((count, count), jnp.float32))
    orthonormal, triangle = lax.fori_loop(0, count, one_column, start)
    projected = jnp.dot(orthonormal.T, rhs, precision=exact_mode)
    return back_substitute(triangle, projected)


def shards(right_side, stencil, class_scale, material, boundary, sign_bits, sample_rows):
    table = hadamard_table()
    scale_field = material_scale(material, class_scale)
    sign_field = (2 * sign_bits - 1).astype(jnp.float32)
    depth = right_side.shape[4]
    plane = right_side.shape[1] * 3 * depth
    sampled = sample_rows[0, 0]
    rest_y = sampled % plane
    rest_c = rest_y % (3 * depth)
    pick_z = rest_c % depth
    picks = (sampled // plane, rest_y // (3 * depth), rest_c // depth, pick_z // 128, pick_z % 128)
    width = right_side.shape[2]
    local_rhs = sketch_local(right_side, sign_field, picks, table)
    sketch_rhs = one_axis_at_a_time(local_rhs, GX_GY)
    lengths = jnp.sqrt(jnp.sum(sketch_rhs * sketch_rhs, axis=0) + 1e-06)
    basis_block = right_side / lengths[None, None, :, None, None]
    sketch_basis = sketch_rhs / lengths
    blocks = []
    sketched_images = []
    for block_step in range(STEPS):
        operated = operate(basis_block, stencil, scale_field, boundary)
        local_image = sketch_local(operated, sign_field, picks, table)
        sketch_image = one_axis_at_a_time(local_image, GX_GY)
        blocks.append(basis_block)
        sketched_images.append(sketch_image)
        if block_step + 1 < STEPS:
            coupling = jnp.dot(sketch_basis.T, sketch_image, precision=exact_mode)
            remainder = operated - jnp.einsum(
                "xyicz,ij->xyjcz", basis_block, coupling, precision=exact_mode
            )
            sketch_remainder = sketch_image - jnp.dot(sketch_basis, coupling, precision=exact_mode)
            norms = jnp.sqrt(jnp.sum(sketch_remainder * sketch_remainder, axis=0) + 1e-06)
            basis_block = remainder / norms[None, None, :, None, None]
            sketch_basis = sketch_remainder / norms
    matrix = jnp.concatenate(sketched_images, axis=1)
    weights = solve_small(matrix, sketch_rhs)
    solution = jnp.zeros(right_side.shape, jnp.float32)
    for block_step in range(STEPS):
        part_weights = weights[block_step * width : (block_step + 1) * width]
        solution = solution + jnp.einsum(
            "xyicz,ij->xyjcz", blocks[block_step], part_weights, precision=exact_mode
        )
    residual = right_side - operate(solution, stencil, scale_field, boundary)
    return (solution, residual)


def solution(mesh):
    split = Mesh(mesh.devices.reshape(4, 8, 4, 2), ("gx_0", "gx_1", "gy_0", "gy_1"))
    return jax.shard_map(
        shards,
        mesh=split,
        in_specs=(
            P(GX, GY, None, None, None),
            P(),
            P(),
            P(GX, GY, None),
            P(GX, GY, None),
            P(GX, GY, None, None),
            P(GX, GY, None),
        ),
        out_specs=(P(GX, GY, None, None, None), P(GX, GY, None, None, None)),
        check_vma=False,
    )
```

profile of v0, /device:TPU:1, one launch (start us, length us, event | category | flops | bytes accessed | tf_op | source)
XLA Modules:
  0.0 820.1 jit_solution(13014205767853807181)
XLA Ops:
  6.1 9.5 %psum.252 = f32[128,4]{0,1:T(4,128)S(1)} all-reduce(f32[128,4]{0,1:T(4,128)S(1)} %copy.1897), channel_id=1, replica_groups=mesh['gx_0'=4,'gx_1'=8,'gy_0'=4,'gy_1'=2] {'gx_0'}, use_global_device_ids=true, to_apply=%region_1.2 | all-reduce | flops 512 | bytes 4096 | tf_op jit(solution)/shard_map/psum | solution.py:37
  15.6 16.2 %psum.253 = f32[128,4]{0,1:T(4,128)S(1)} all-reduce(f32[128,4]{0,1:T(4,128)S(1)} %psum.252), channel_id=1, replica_groups=mesh['gx_0'=4,'gx_1'=8,'gy_0'=4,'gy_1'=2] {'gx_1'}, use_global_device_ids=true, to_apply=%region_2.3 | all-reduce | flops 512 | bytes 4096 | tf_op jit(solution)/shard_map/psum | solution.py:37
  31.8 8.5 %psum.254 = f32[128,4]{0,1:T(4,128)S(1)} all-reduce(f32[128,4]{0,1:T(4,128)S(1)} %psum.253), channel_id=1, replica_groups=mesh['gx_0'=4,'gx_1'=8,'gy_0'=4,'gy_1'=2] {'gy_0'}, use_global_device_ids=true, to_apply=%region_3.4 | all-reduce | flops 512 | bytes 4096 | tf_op jit(solution)/shard_map/psum | solution.py:37
  40.3 10.6 %psum.255 = f32[128,4]{0,1:T(4,128)S(1)} all-reduce(f32[128,4]{0,1:T(4,128)S(1)} %psum.254), channel_id=1, replica_groups=mesh['gx_0'=4,'gx_1'=8,'gy_0'=4,'gy_1'=2] {'gy_1'}, use_global_device_ids=true, to_apply=%region_4.5 | all-reduce | flops 512 | bytes 4096 | tf_op jit(solution)/shard_map/psum | solution.py:37
  52.4 4.0 collective-permute-start
  57.5 5.0 select_add_fusion
  62.8 2.8 collective-permute-start.3
  65.7 2.8 collective-permute-start.2
  74.9 6.0 psum.256
  81.0 12.5 %psum.257 = f32[128,4]{0,1:T(4,128)S(1)} all-reduce(f32[128,4]{0,1:T(4,128)S(1)} %psum.256), channel_id=1, replica_groups=mesh['gx_0'=4,'gx_1'=8,'gy_0'=4,'gy_1'=2] {'gx_1'}, use_global_device_ids=true, to_apply=%region_35.36 | all-reduce | flops 512 | bytes 4096 | tf_op jit(solution)/shard_map/psum | solution.py:37
  93.5 6.0 psum.258
  99.5 11.7 %psum.259 = f32[128,4]{0,1:T(4,128)S(1)} all-reduce(f32[128,4]{0,1:T(4,128)S(1)} %psum.258), channel_id=1, replica_groups=mesh['gx_0'=4,'gx_1'=8,'gy_0'=4,'gy_1'=2] {'gy_1'}, use_global_device_ids=true, to_apply=%region_37.38 | all-reduce | flops 512 | bytes 4096 | tf_op jit(solution)/shard_map/psum | solution.py:37
  113.8 4.0 collective-permute-start.4
  119.4 3.4 collective-permute-start.7
  122.8 2.7 collective-permute-start.6
  132.0 10.7 %psum.260 = f32[128,4]{0,1:T(4,128)S(1)} all-reduce(f32[128,4]{0,1:T(4,128)S(1)} %copy.1905), channel_id=1, replica_groups=mesh['gx_0'=4,'gx_1'=8,'gy_0'=4,'gy_1'=2] {'gx_0'}, use_global_device_ids=true, to_apply=%region_67.68 | all-reduce | flops 512 | bytes 4096 | tf_op jit(solution)/shard_map/psum | solution.py:37
  142.7 10.7 %psum.261 = f32[128,4]{0,1:T(4,128)S(1)} all-reduce(f32[128,4]{0,1:T(4,128)S(1)} %psum.260), channel_id=1, replica_groups=mesh['gx_0'=4,'gx_1'=8,'gy_0'=4,'gy_1'=2] {'gx_1'}, use_global_device_ids=true, to_apply=%region_68.69 | all-reduce | flops 512 | bytes 4096 | tf_op jit(solution)/shard_map/psum | solution.py:37
  153.4 6.3 psum.262
  159.7 11.7 %psum.263 = f32[128,4]{0,1:T(4,128)S(1)} all-reduce(f32[128,4]{0,1:T(4,128)S(1)} %psum.262), channel_id=1, replica_groups=mesh['gx_0'=4,'gx_1'=8,'gy_0'=4,'gy_1'=2] {'gy_1'}, use_global_device_ids=true, to_apply=%region_70.71 | all-reduce | flops 512 | bytes 4096 | tf_op jit(solution)/shard_map/psum | solution.py:37
  174.0 4.3 collective-permute-start.8
  180.1 3.1 collective-permute-start.11
  183.2 2.4 collective-permute-start.10
  192.6 11.2 %psum.264 = f32[128,4]{0,1:T(4,128)S(1)} all-reduce(f32[128,4]{0,1:T(4,128)S(1)} %copy.1910), channel_id=1, replica_groups=mesh['gx_0'=4,'gx_1'=8,'gy_0'=4,'gy_1'=2] {'gx_0'}, use_global_device_ids=true, to_apply=%region_100.101 | all-reduce | flops 512 | bytes 4096 | tf_op jit(solution)/shard_map/psum | solution.py:37
  203.8 10.7 %psum.265 = f32[128,4]{0,1:T(4,128)S(1)} all-reduce(f32[128,4]{0,1:T(4,128)S(1)} %psum.264), channel_id=1, replica_groups=mesh['gx_0'=4,'gx_1'=8,'gy_0'=4,'gy_1'=2] {'gx_1'}, use_global_device_ids=true, to_apply=%region_101.102 | all-reduce | flops 512 | bytes 4096 | tf_op jit(solution)/shard_map/psum | solution.py:37
  214.5 6.0 psum.266
  220.5 11.7 %psum.267 = f32[128,4]{0,1:T(4,128)S(1)} all-reduce(f32[128,4]{0,1:T(4,128)S(1)} %psum.266), channel_id=1, replica_groups=mesh['gx_0'=4,'gx_1'=8,'gy_0'=4,'gy_1'=2] {'gy_1'}, use_global_device_ids=true, to_apply=%region_103.104 | all-reduce | flops 512 | bytes 4096 | tf_op jit(solution)/shard_map/psum | solution.py:37
  234.8 4.3 collective-permute-start.12
  240.9 3.1 collective-permute-start.15
  244.0 2.6 collective-permute-start.14
  253.4 11.2 %psum.268 = f32[128,4]{0,1:T(4,128)S(1)} all-reduce(f32[128,4]{0,1:T(4,128)S(1)} %copy.1915), channel_id=1, replica_groups=mesh['gx_0'=4,'gx_1'=8,'gy_0'=4,'gy_1'=2] {'gx_0'}, use_global_device_ids=true, to_apply=%region_133.134 | all-reduce | flops 512 | bytes 4096 | tf_op jit(solution)/shard_map/psum | solution.py:37
  264.6 10.7 %psum.269 = f32[128,4]{0,1:T(4,128)S(1)} all-reduce(f32[128,4]{0,1:T(4,128)S(1)} %psum.268), channel_id=1, replica_groups=mesh['gx_0'=4,'gx_1'=8,'gy_0'=4,'gy_1'=2] {'gx_1'}, use_global_device_ids=true, to_apply=%region_134.135 | all-reduce | flops 512 | bytes 4096 | tf_op jit(solution)/shard_map/psum | solution.py:37
  275.3 6.1 psum.270
  281.4 11.7 %psum.271 = f32[128,4]{0,1:T(4,128)S(1)} all-reduce(f32[128,4]{0,1:T(4,128)S(1)} %psum.270), channel_id=1, replica_groups=mesh['gx_0'=4,'gx_1'=8,'gy_0'=4,'gy_1'=2] {'gy_1'}, use_global_device_ids=true, to_apply=%region_136.137 | all-reduce | flops 512 | bytes 4096 | tf_op jit(solution)/shard_map/psum | solution.py:37
  295.6 4.3 collective-permute-start.16
  301.7 3.1 collective-permute-start.19
  314.2 11.2 %psum.272 = f32[128,4]{0,1:T(4,128)S(1)} all-reduce(f32[128,4]{0,1:T(4,128)S(1)} %copy.1920), channel_id=1, replica_groups=mesh['gx_0'=4,'gx_1'=8,'gy_0'=4,'gy_1'=2] {'gx_0'}, use_global_device_ids=true, to_apply=%region_166.167 | all-reduce | flops 512 | bytes 4096 | tf_op jit(solution)/shard_map/psum | solution.py:37
  325.4 10.7 %psum.273 = f32[128,4]{0,1:T(4,128)S(1)} all-reduce(f32[128,4]{0,1:T(4,128)S(1)} %psum.272), channel_id=1, replica_groups=mesh['gx_0'=4,'gx_1'=8,'gy_0'=4,'gy_1'=2] {'gx_1'}, use_global_device_ids=true, to_apply=%region_167.168 | all-reduce | flops 512 | bytes 4096 | tf_op jit(solution)/shard_map/psum | solution.py:37
  336.1 6.1 psum.274
  342.2 11.7 %psum.275 = f32[128,4]{0,1:T(4,128)S(1)} all-reduce(f32[128,4]{0,1:T(4,128)S(1)} %psum.274), channel_id=1, replica_groups=mesh['gx_0'=4,'gx_1'=8,'gy_0'=4,'gy_1'=2] {'gy_1'}, use_global_device_ids=true, to_apply=%region_169.170 | all-reduce | flops 512 | bytes 4096 | tf_op jit(solution)/shard_map/psum | solution.py:37
  356.4 4.3 collective-permute-start.20
  362.5 3.1 collective-permute-start.23
  365.6 2.7 collective-permute-start.22
  375.0 11.2 %psum.276 = f32[128,4]{0,1:T(4,128)S(1)} all-reduce(f32[128,4]{0,1:T(4,128)S(1)} %copy.1925), channel_id=1, replica_groups=mesh['gx_0'=4,'gx_1'=8,'gy_0'=4,'gy_1'=2] {'gx_0'}, use_global_device_ids=true, to_apply=%region_199.200 | all-reduce | flops 512 | bytes 4096 | tf_op jit(solution)/shard_map/psum | solution.py:37
  386.2 10.7 %psum.277 = f32[128,4]{0,1:T(4,128)S(1)} all-reduce(f32[128,4]{0,1:T(4,128)S(1)} %psum.276), channel_id=1, replica_groups=mesh['gx_0'=4,'gx_1'=8,'gy_0'=4,'gy_1'=2] {'gx_1'}, use_global_device_ids=true, to_apply=%region_200.201 | all-reduce | flops 512 | bytes 4096 | tf_op jit(solution)/shard_map/psum | solution.py:37
  396.9 6.1 psum.278
  403.0 11.7 %psum.279 = f32[128,4]{0,1:T(4,128)S(1)} all-reduce(f32[128,4]{0,1:T(4,128)S(1)} %psum.278), channel_id=1, replica_groups=mesh['gx_0'=4,'gx_1'=8,'gy_0'=4,'gy_1'=2] {'gy_1'}, use_global_device_ids=true, to_apply=%region_202.203 | all-reduce | flops 512 | bytes 4096 | tf_op jit(solution)/shard_map/psum | solution.py:37
  417.2 4.3 collective-permute-start.24
  423.3 3.1 collective-permute-start.27
  435.8 11.2 %psum.280 = f32[128,4]{0,1:T(4,128)S(1)} all-reduce(f32[128,4]{0,1:T(4,128)S(1)} %copy.1930), channel_id=1, replica_groups=mesh['gx_0'=4,'gx_1'=8,'gy_0'=4,'gy_1'=2] {'gx_0'}, use_global_device_ids=true, to_apply=%region_232.233 | all-reduce | flops 512 | bytes 4096 | tf_op jit(solution)/shard_map/psum | solution.py:37
  447.0 10.7 %psum.281 = f32[128,4]{0,1:T(4,128)S(1)} all-reduce(f32[128,4]{0,1:T(4,128)S(1)} %psum.280), channel_id=1, replica_groups=mesh['gx_0'=4,'gx_1'=8,'gy_0'=4,'gy_1'=2] {'gx_1'}, use_global_device_ids=true, to_apply=%region_233.234 | all-reduce | flops 512 | bytes 4096 | tf_op jit(solution)/shard_map/psum | solution.py:37
  457.7 6.1 psum.282
  463.7 11.7 %psum.283 = f32[128,4]{0,1:T(4,128)S(1)} all-reduce(f32[128,4]{0,1:T(4,128)S(1)} %psum.282), channel_id=1, replica_groups=mesh['gx_0'=4,'gx_1'=8,'gy_0'=4,'gy_1'=2] {'gy_1'}, use_global_device_ids=true, to_apply=%region_235.236 | all-reduce | flops 512 | bytes 4096 | tf_op jit(solution)/shard_map/psum | solution.py:37
  478.0 4.3 collective-permute-start.28
  484.1 3.1 collective-permute-start.31
  487.2 2.7 collective-permute-start.30
  496.6 11.2 %psum.284 = f32[128,4]{0,1:T(4,128)S(1)} all-reduce(f32[128,4]{0,1:T(4,128)S(1)} %copy.1935), channel_id=1, replica_groups=mesh['gx_0'=4,'gx_1'=8,'gy_0'=4,'gy_1'=2] {'gx_0'}, use_global_device_ids=true, to_apply=%region_265.266 | all-reduce | flops 512 | bytes 4096 | tf_op jit(solution)/shard_map/psum | solution.py:37
  507.8 10.7 %psum.285 = f32[128,4]{0,1:T(4,128)S(1)} all-reduce(f32[128,4]{0,1:T(4,128)S(1)} %psum.284), channel_id=1, replica_groups=mesh['gx_0'=4,'gx_1'=8,'gy_0'=4,'gy_1'=2] {'gx_1'}, use_global_device_ids=true, to_apply=%region_266.267 | all-reduce | flops 512 | bytes 4096 | tf_op jit(solution)/shard_map/psum | solution.py:37
  518.4 6.1 psum.286
  524.5 11.7 %psum.287 = f32[128,4]{0,1:T(4,128)S(1)} all-reduce(f32[128,4]{0,1:T(4,128)S(1)} %psum.286), channel_id=1, replica_groups=mesh['gx_0'=4,'gx_1'=8,'gy_0'=4,'gy_1'=2] {'gy_1'}, use_global_device_ids=true, to_apply=%region_268.269 | all-reduce | flops 512 | bytes 4096 | tf_op jit(solution)/shard_map/psum | solution.py:37
  536.3 173.4 %while.35 = (s32[]{:T(128)}, f32[128,32]{0,1:T(8,128)S(1)}, f32[32,32]{0,1:T(8,128)S(1)}, f32[32,128]{1,0:T(8,128)S(1)}, s32[]{:T(128)}, /*index=5*/s32[1]{0:T(128)}, f32[]{:T(128)}, s32[]{:T(128)}, s32[1]{0:T(128)}) while((s32[]{:T(128)}, f32[128,32]{0,1:T(8,128)S(1)}, f32[32,32]{0,1:T(8,128)S(1)}, f32[32,128]{1,0:T(8,128)S(1)}, ...), condition=%wide.region_272.273_spmd, body=%wide.region_269.272_spmd.sunk | while | flops 197457 | bytes 72798 | solution.py:124
  709.9 85.4 %while.36 = (s32[]{:T(128)}, f32[32,4]{1,0:T(8,128)S(1)}, f32[32,4]{1,0:T(8,128)S(1)}, f32[32,32]{1,0:T(8,128)S(1)}, s32[]{:T(128)}, /*index=5*/s32[2]{0:T(128)S(1)}, s32[1]{0:T(128)}, s32[]{:T(128)}, s32[]{:T(128)}, s32[]{:T(128)}) while((s32[]{:T(128)}, f32[32,4]{1,0:T(8,128)S(1)}, f32[32,4]{1,0:T(8,128)S(1)}, ...), condition=%wide.region_275.276_spmd, body=%wide.region_273.275_spmd.sunk | while | flops 1564 | bytes 20220 | solution.py:104
  801.7 4.3 collective-permute-start.32
  807.8 3.1 collective-permute-start.35
  810.9 2.7 collective-permute-start.34
  (953 shorter events, 324.1 us)
Async XLA Ops:
  1.5 49.5 %copy-start.1 = (f32[2,16,4,3,128]{4,2,3,1,0:T(4,128)S(1)}, f32[2,16,4,3,128]{4,2,3,1,0:T(4,128)}, u32[]{:S(2)}) copy-start(f32[2,16,4,3,128]{4,2,3,1,0:T(4,128)} %param.19) | copy-start | bytes 589828
  4.0 52.4 %copy-start = (f32[27,3,3]{0,2,1:T(4,128)S(1)}, f32[27,3,3]{0,2,1:T(4,128)}, u32[]{:S(2)}) copy-start(f32[27,3,3]{0,2,1:T(4,128)} %param.20) | copy-start | bytes 2920
  5.1 51.7 %copy-start.2 = (f32[8]{0:T(128)S(1)}, f32[8]{0:T(128)}, u32[]{:S(2)}) copy-start(f32[8]{0:T(128)} %param.21) | copy-start | bytes 100
  5.1 52.4 %copy-start.3 = (s32[2,16,128]{2,1,0:T(8,128)S(1)}, s32[2,16,128]{2,1,0:T(8,128)}, u32[]{:S(2)}) copy-start(s32[2,16,128]{2,1,0:T(8,128)} %param.23) | copy-start | bytes 49156
  5.1 52.4 %copy-start.4 = (s32[2,16,128]{2,1,0:T(8,128)S(1)}, s32[2,16,128]{2,1,0:T(8,128)}, u32[]{:S(2)}) copy-start(s32[2,16,128]{2,1,0:T(8,128)} %param.22) | copy-start | bytes 49156
  51.1 11.7 %collective-permute-start.1 = (f32[1,16,4,3,128]{4,1,3,2,0:T(8,128)S(1)}, f32[1,16,4,3,128]{4,1,3,2,0:T(8,128)S(1)}, u32[]{:S(2)}, u32[]{:S(2)}) collective-permute-start(f32[1,16,4,3,128]{4,1,3,2,0:T(8,128)S(1)} %get-tuple-element.683), channel_id=1, source_target_pairs={{8,0},{16,8},{24,16},{32,24},{40,32},{48,40},{56,48},{64,56},{72,6... | collective-permute-start | bytes 294920 | tf_op jit(solution)/shard_map/ppermute | solution.py:28
  52.4 10.4 %collective-permute-start = (f32[1,16,4,3,128]{4,1,3,2,0:T(8,128)S(1)}, f32[1,16,4,3,128]{4,1,3,2,0:T(8,128)S(1)}, u32[]{:S(2)}, u32[]{:S(2)}) collective-permute-start(f32[1,16,4,3,128]{4,1,3,2,0:T(8,128)S(1)} %get-tuple-element.682), channel_id=1, source_target_pairs={{0,8},{8,16},{16,24},{24,32},{32,40},{40,48},{48,56},{56,64},{64,7... | collective-permute-start | bytes 294920 | tf_op jit(solution)/shard_map/ppermute | solution.py:26
  62.8 5.6 collective-permute-start.3
  65.7 3.7 collective-permute-start.2
  112.5 5.9 collective-permute-start.5
  113.8 5.6 collective-permute-start.4
  119.4 6.4 collective-permute-start.7
  122.8 3.1 collective-permute-start.6
  172.7 6.5 collective-permute-start.9
  174.0 6.1 collective-permute-start.8
  180.1 5.8 collective-permute-start.11
  183.2 3.4 collective-permute-start.10
  233.5 6.5 collective-permute-start.13
  234.8 6.1 collective-permute-start.12
  240.9 6.0 collective-permute-start.15
  244.0 3.4 collective-permute-start.14
  294.3 6.5 collective-permute-start.17
  295.6 6.1 collective-permute-start.16
  301.7 5.8 collective-permute-start.19
  304.8 3.4 collective-permute-start.18
  355.1 6.5 collective-permute-start.21
  356.4 6.1 collective-permute-start.20
  362.5 6.1 collective-permute-start.23
  365.6 3.4 collective-permute-start.22
  415.9 6.5 collective-permute-start.25
  417.2 6.1 collective-permute-start.24
  423.3 5.8 collective-permute-start.27
  426.4 3.4 collective-permute-start.26
  476.7 6.5 collective-permute-start.29
  478.0 6.1 collective-permute-start.28
  484.1 6.1 collective-permute-start.31
  487.2 3.4 collective-permute-start.30
  495.1 214.7 %copy-start.5 = (s32[2]{0:T(128)S(1)}, s32[2]{0:T(128)}, u32[]{:S(2)}) copy-start(s32[2]{0:T(128)} %constant.394.clone.1) | copy-start | bytes 28
  800.4 6.5 collective-permute-start.33
  801.7 6.1 collective-permute-start.32
  807.8 6.1 collective-permute-start.35
  810.9 3.4 collective-permute-start.34
where the time goes:
time: 833 us; the launch traced here: 820 us
  blocking collectives  358 us (43%)
  other arithmetic  135 us (16%)
  starting transfers between devices  101 us (12%)
  matrix products  92.9 us (11%)
  local copies, waits for them, and re-layouts  67.1 us (8%)
  loops' own time  44.2 us (5%)
  waiting for transfers between devices  17.9 us (2%)
    psum x36, blocking collectives, one_axis_at_a_time(): shard = lax.psum(shard, axis)  358 us
    another operation x128, other arithmetic  87.4 us
    ppermute x18, starting transfers between devices, padded_2(): lax.ppermute(tail, axis, [(i, (i + 1) % count) for i in range(ends)])  61.4 us
    another operation x1, loops' own time, solve_small(): orthonormal, triangle = lax.fori_loop(0, count, one_column, start)  43.5 us
    dot_general x32, matrix products, one_row(): total = jnp.dot(line[None, :], unknowns, precision=exact_mode)[0]  42.8 us
    ppermute x18, starting transfers between devices, padded_2(): lax.ppermute(head, axis, [((i + 1) % count, i) for i in range(ends)])  39.6 us
    dot_general x32, matrix products, one_column(): vector = vector - jnp.dot(orthonormal, second_pass, precision=exact_mode)  25.2 us
    reduce_sum x230, other arithmetic, operate(): jnp.sum(coupling[:, :, None] * shifted[:, :, :, None, :, :], axis=4)  25 us
  transfers between devices with their start and end apart: 36, of which 25 were waited for; matrix products, arithmetic and copies ran while one was open for 1% of the time, Pallas kernels for 0%

commit v1 on v0

v1 whole, which is shorter than its diff:
```python
import math

import jax
import jax.numpy as jnp
from jax import lax
from jax.experimental import pallas as pl
from jax.experimental.pallas import tpu as pltpu
from jax.sharding import Mesh
from jax.sharding import PartitionSpec as P

STEPS = 8
AXES = ("gx_0", "gx_1", "gy_0", "gy_1")
GX = ("gx_0", "gx_1")
GY = ("gy_0", "gy_1")
REDUCE_STAGES = ((("gx_0", "gy_0"), 16), (("gx_1", "gy_1"), 16))

exact_mode = lax.Precision.HIGHEST
VMEM = pl.BlockSpec(memory_space=pltpu.VMEM)
SMEM = pl.BlockSpec(memory_space=pltpu.SMEM)
PARAMS = pltpu.CompilerParams(vmem_limit_bytes=48 * 1024 * 1024)


def tile_iota(axis):
    return lax.broadcasted_iota(jnp.int32, (8, 128), axis)


def stencil_rows(source, base, first, rows, component, coef):
    sums = [[None] * rows for _ in range(3)]
    for dx in range(3):
        for c in range(3):
            tiles = [source[first + r, base + dx, c] for r in range(rows + 2)]
            for dy in range(3):
                for dz in range(3):
                    weight = coef[(dx * 9 + dy * 3 + dz) * 9 + component * 3 + c]
                    for r in range(rows):
                        term = weight * tiles[r + dy]
                        old = sums[dz][r]
                        sums[dz][r] = term if old is None else old + term
    lane = tile_iota(1)
    out = []
    for r in range(rows):
        low = jnp.where(lane > 0, pltpu.roll(sums[0][r], 1, 1), 0.0)
        high = jnp.where(lane < 127, pltpu.roll(sums[2][r], 127, 1), 0.0)
        out.append(sums[1][r] + low + high)
    return out


def make_pair_kernel(first_round):
    rows_a, rows_b = 9, 8

    def kernel(coef, left, own, right, down, up, before, scale, scale_own, mid, last, work):
        half = tile_iota(0) < 4

        def put(row, t_left, t_own, t_right):
            for c in range(3):
                a, b, d = t_left(c), t_own(c), t_right(c)
                ra, rb, rd = pltpu.roll(a, 4, 0), pltpu.roll(b, 4, 0), pltpu.roll(d, 4, 0)
                work[row, 0, c] = a
                work[row, 1, c] = jnp.where(half, ra, rb)
                work[row, 2, c] = b
                work[row, 3, c] = jnp.where(half, rb, rd)
                work[row, 4, c] = d

        for row in range(2):
            put(row, *[(lambda c, s=s, row=row: down[s, row, c]) for s in range(3)])
            put(18 + row, *[(lambda c, s=s, row=row: up[s, row, c]) for s in range(3)])

        def inner(row, carry):
            put(
                row + 2,
                lambda c: left[row, c],
                lambda c: own[row, c],
                lambda c: right[row, c],
            )
            return carry

        lax.fori_loop(0, 16, inner, 0)
        shift, gain = coef[243], coef[244]

        def diagonal(tile):
            return jnp.where(tile == 0.0, gain - shift * gain, -shift * gain)

        def step_a(i, carry):
            side = i // 2
            first = (i % 2) * rows_a
            for component in range(3):
                total = stencil_rows(work, side * 2, first, rows_a, component, coef)
                for r in range(rows_a):
                    row = first + r
                    alpha = scale[row, side]
                    centre = work[row + 1, side * 2 + 1, component]
                    value = (alpha * gain) * total[r] + diagonal(alpha) * centre
                    if first_round:
                        value = value * 0.5
                    else:
                        value = value - before[row, side * 2, component]
                    mid[row, side * 2, component] = value
            return carry

        lax.fori_loop(0, 4, step_a, 0)

        def join(row, carry):
            for c in range(3):
                mid[row, 1, c] = jnp.where(
                    half, pltpu.roll(mid[row, 0, c], 4, 0), pltpu.roll(mid[row, 2, c], 4, 0)
                )
            return carry

        lax.fori_loop(0, 18, join, 0)

        def step_b(i, carry):
            first = i * rows_b
            for component in range(3):
                total = stencil_rows(mid, 0, first, rows_b, component, coef)
                for r in range(rows_b):
                    row = first + r
                    alpha = scale_own[row]
                    value = (alpha * gain) * total[r] + diagonal(alpha) * mid[row + 1, 1, component]
                    last[row, component] = value - own[row, component]
            return carry

        lax.fori_loop(0, 2, step_b, 0)

    return kernel


def two_steps(first_round, coef, left, own, right, down, up, before, scale, scale_own):
    return pl.pallas_call(
        make_pair_kernel(first_round),
        out_shape=(
            jax.ShapeDtypeStruct((18, 3, 3, 8, 128), jnp.float32),
            jax.ShapeDtypeStruct((16, 3, 8, 128), jnp.float32),
        ),
        in_specs=[SMEM] + [VMEM] * 8,
        out_specs=(VMEM, VMEM),
        scratch_shapes=[pltpu.VMEM((20, 5, 3, 8, 128), jnp.float32)],
        compiler_params=PARAMS,
        name="two_steps",
    )(coef, left, own, right, down, up, before, scale, scale_own)


def make_sketch_kernel(kinds):
    def kernel(where, signs, *refs):
        count = len(kinds)
        blocks, out = refs[:count], refs[count]
        both, products = refs[count + 1 :]
        half = tile_iota(0) < 4
        ones = jnp.ones((8, 128), jnp.float32)
        for n, kind in enumerate(kinds):
            ref = blocks[n]

            def spread(row, carry):
                for c in range(3):
                    tile = ref[row + 1, 1, c] if kind else ref[row, c]
                    both[row * 3 + c] = tile
                    both[48 + row * 3 + c] = pltpu.roll(tile, 4, 0)
                return carry

            lax.fori_loop(0, 16, spread, 0)

            def pick(group, carry):
                for k in range(8):
                    j = group * 8 + k
                    tile = jnp.where(half, both[where[j]], both[where[64 + j]]) * signs[j]
                    products[pl.ds(j, 4, stride=128), :] = tile[0:4]
                    products[pl.ds(j + 64, 4, stride=128), :] = tile[4:8]
                return carry

            lax.fori_loop(0, 8, pick, 0)
            sums = lax.dot_general(
                ones,
                products[...],
                (((1,), (1,)), ((), ())),
                precision=exact_mode,
                preferred_element_type=jnp.float32,
            )
            for b in range(4):
                out[pl.ds(n * 4 + b, 1), :] = sums[0:1, b * 128 : (b + 1) * 128]

    return kernel


def sketch(kinds, where, signs, *blocks):
    return pl.pallas_call(
        make_sketch_kernel(kinds),
        out_shape=jax.ShapeDtypeStruct((4 * len(kinds), 128), jnp.float32),
        in_specs=[SMEM] + [VMEM] * (1 + len(kinds)),
        out_specs=VMEM,
        scratch_shapes=[
            pltpu.VMEM((96, 8, 128), jnp.float32),
            pltpu.VMEM((512, 128), jnp.float32),
        ],
        compiler_params=PARAMS,
        name="sketch",
    )(where, signs, *blocks)


def fit_kernel(scalars, images, sketches, out):
    shift, reach = scalars[0], scalars[1]
    lane = tile_iota(1)
    row = tile_iota(0)
    tall_row = lax.broadcasted_iota(jnp.int32, (40, 128), 0)
    tall_lane = lax.broadcasted_iota(jnp.int32, (40, 128), 1)

    def dot(a, b):
        return jnp.dot(a, b, precision=exact_mode, preferred_element_type=jnp.float32)

    def sum_lanes(a):
        return jnp.sum(a, axis=1, keepdims=True)

    live = row < 4
    raise_by = jnp.where(lane < 4, reach, 0.5 * reach)
    lower_by = jnp.where(lane < 4, 0.0, 0.5 * reach)
    table = sketches[...]
    basis = jnp.where(live, images[32:40, :], 0.0)
    norms = jnp.sqrt(sum_lanes(basis * basis) + 1e-06)
    basis = basis / norms
    coords = jnp.where(live & (lane == row), 1.0, 0.0) / norms
    leading = jnp.sum(jnp.where(lane == row, coords, 0.0), axis=0, keepdims=True)
    for k in range(STEPS - 1):
        moved = (
            pltpu.roll(coords * raise_by, 4, 1)
            + shift * coords
            + pltpu.roll(coords * lower_by, 124, 1)
        )
        image = dot(moved, table)
        rest, next_coords = image, moved
        for i in range(4):
            weight = sum_lanes(image * basis[i : i + 1])
            rest = rest - weight * basis[i : i + 1]
            next_coords = next_coords - weight * coords[i : i + 1]
        norms = jnp.sqrt(sum_lanes(rest * rest) + 1e-06)
        basis = rest / norms
        coords = next_coords / norms
        leading = leading + jnp.sum(
            jnp.where(live & (lane == row + 4 * (k + 1)), coords, 0.0), axis=0, keepdims=True
        )

    vectors = images[...]
    combos = jnp.where(tall_row == tall_lane, 1.0, 0.0)
    found = jnp.zeros((8, 128), jnp.float32)
    sizes = jnp.zeros((1, 128), jnp.float32)
    for j in range(4 * STEPS):
        pivot = vectors[j : j + 1]
        products = sum_lanes(vectors * pivot)
        size = products[j : j + 1]
        ratio = products / (size + 1e-37)
        found = jnp.where(lane == j, ratio[32:40], found)
        sizes = jnp.where(lane[0:1] == j, size, sizes)
        later = jnp.where(tall_row > j, ratio, 0.0)
        vectors = vectors - later * pivot
        combos = combos - later * combos[j : j + 1]
    scaled = sizes * leading * leading
    found = found * (scaled / (scaled + 1e-06))
    out[...] = dot(found[:, 0:40], combos)


def fit(scalars, images, sketches):
    return pl.pallas_call(
        fit_kernel,
        out_shape=jax.ShapeDtypeStruct((8, 128), jnp.float32),
        in_specs=[SMEM, VMEM, VMEM],
        out_specs=VMEM,
        compiler_params=PARAMS,
        name="fit",
    )(scalars, images, sketches)


def combine_kernel(mix, first, m0, l0, m1, l1, m2, l2, m3, l3, iterate, remainder):
    sub = tile_iota(0) % 4
    refs = [(first, 0), (m0, 1), (l0, 0), (m1, 1), (l1, 0), (m2, 1), (l2, 0), (m3, 1), (l3, 0)]

    def one_row(y, carry):
        for c in range(3):
            start = first[y, c]
            total = None
            image = start
            for k, (ref, kind) in enumerate(refs):
                tile = ref[y + 1, 1, c] if kind else ref[y, c]
                for r in range(4):
                    if r:
                        turned = jnp.where(
                            sub < 4 - r, pltpu.roll(tile, 8 - r, 0), pltpu.roll(tile, 4 - r, 0)
                        )
                    else:
                        turned = tile
                    if k < STEPS:
                        part = mix[k * 4 + r] * turned
                        total = part if total is None else total + part
                    image = image - mix[(STEPS + k) * 4 + r] * turned
            iterate[y, c] = total
            remainder[y, c] = image
        return carry

    lax.fori_loop(0, 16, one_row, 0)


def combine(mix, blocks):
    shape = jax.ShapeDtypeStruct((16, 3, 8, 128), jnp.float32)
    return pl.pallas_call(
        combine_kernel,
        out_shape=(shape, shape),
        in_specs=[VMEM] * 10,
        out_specs=(VMEM, VMEM),
        compiler_params=PARAMS,
        name="combine",
    )(mix, *blocks)


def hadamard_table():
    lanes = jnp.arange(128, dtype=jnp.int32)
    common = lanes[:, None] & lanes[None, :]
    parity = jnp.zeros((128, 128), jnp.int32)
    for bit in range(7):
        parity = parity + (common >> bit & 1)
    return (1 - 2 * (parity % 2)).astype(jnp.float32) / math.sqrt(128.0)


def material_scale(material, class_scale):
    scale_field = jnp.zeros(material.shape, jnp.float32)
    for number in range(class_scale.shape[0]):
        scale_field = scale_field + jnp.where(
            material == number, class_scale[number], jnp.float32(0.0)
        )
    return scale_field


def neighbours(low, high, axis):
    count = lax.axis_size(axis)
    before = lax.ppermute(high, axis, [(i, i + 1) for i in range(count - 1)])
    after = lax.ppermute(low, axis, [(i + 1, i) for i in range(count - 1)])
    return before, after


def spectrum(stencil, class_scale):
    centre = jnp.diagonal(stencil[13])
    middle = jnp.mean(centre)
    spread = jnp.sqrt(
        jnp.maximum(jnp.sum(stencil * stencil) - jnp.sum(centre * centre), 0.0) / 3.0
    )
    low = jnp.minimum(jnp.min(class_scale) * (middle - spread), 1.0)
    high = jnp.maximum(jnp.max(class_scale) * (middle + spread), 1.0)
    shift = 0.5 * (low + high)
    return shift, jnp.maximum(0.5 * (high - low), 0.05 * shift)


def shards(right_side, stencil, class_scale, material, boundary, sign_bits, sample_rows):
    shift, reach = spectrum(stencil, class_scale)
    coef = jnp.concatenate(
        [stencil.reshape(-1), shift[None], (2.0 / reach)[None], jnp.zeros((11,), jnp.float32)]
    )
    own = right_side.transpose(1, 3, 0, 2, 4).reshape(16, 3, 8, 128)
    masked = jnp.where(boundary == 1, 0.0, material_scale(material, class_scale))

    sampled = sample_rows[0, 0]
    pick_x = sampled // 6144
    pick_y = sampled % 6144 // 384
    pick_c = sampled % 384 // 128
    pick_z = sampled % 128
    tile = pick_y * 3 + pick_c
    where = tile + 48 * jnp.concatenate([pick_x[:64], 1 - pick_x[64:]])
    sign_rows = (2 * sign_bits - 1).astype(jnp.float32)[pick_x, pick_y, pick_c]
    sign_rows = sign_rows * hadamard_table()[pick_z]
    signs = jnp.broadcast_to(
        sign_rows.reshape(2, 64, 1, 128).transpose(1, 0, 2, 3), (64, 2, 4, 128)
    ).reshape(64, 8, 128)

    blocks = [own]
    sketches = []
    before = None
    flat = (16 * 3 * 8, 128)
    for turn in range(STEPS // 2):
        if turn == 0:
            packed = own.reshape(flat)
            low, high = neighbours(
                jnp.concatenate([packed, masked[0]]), jnp.concatenate([packed, masked[1]]), GX
            )
            left, right = low[:384].reshape(own.shape), high[:384].reshape(own.shape)
            planes = jnp.concatenate([low[None, 384:], masked, high[None, 384:]])
        else:
            left, right = neighbours(own, own, GX)
        bottom = jnp.stack([left[:2], own[:2], right[:2]])
        top = jnp.stack([left[14:], own[14:], right[14:]])
        if turn == 0:
            flat_y = (3 * 2 * 3 * 8, 128)
            down, up = neighbours(
                jnp.concatenate([bottom.reshape(flat_y), planes[:, 0], planes[:, 0]]),
                jnp.concatenate([top.reshape(flat_y), planes[:, 15], planes[:, 15]]),
                GY,
            )
            planes = jnp.concatenate([down[144:148, None], planes, up[144:148, None]], axis=1)
            down, up = down[:144].reshape(bottom.shape), up[:144].reshape(top.shape)
            scale = jnp.broadcast_to(
                planes.reshape(2, 2, 18, 128).transpose(2, 0, 1, 3)[:, :, :, None], (18, 2, 2, 4, 128)
            ).reshape(18, 2, 8, 128)
            scale_own = jnp.broadcast_to(
                masked.transpose(1, 0, 2)[:, :, None], (16, 2, 4, 128)
            ).reshape(16, 8, 128)
        else:
            down, up = neighbours(bottom, top, GY)
        if turn == 0:
            sketches.append(sketch((0,), where, signs, own))
            before = jnp.zeros((8, 128), jnp.float32)
        else:
            sketches.append(sketch((1, 0), where, signs, blocks[-2], blocks[-1]))
        mid, last = two_steps(
            turn == 0, coef, left, own, right, down, up, before, scale, scale_own
        )
        blocks += [mid, last]
        before, own = mid, last
    sketches.append(sketch((1, 0), where, signs, blocks[-2], blocks[-1]))

    table = jnp.concatenate(sketches)
    for axes, count in REDUCE_STAGES:
        copies = jnp.broadcast_to(table, (count,) + table.shape)
        table = jnp.sum(lax.all_to_all(copies, axes, 0, 0, tiled=True), axis=0)

    by_block = table.reshape(9, 4, 128)
    half_reach = 0.5 * reach
    images = shift * by_block[:8] + half_reach * by_block[1:]
    images = images + jnp.concatenate(
        [half_reach * by_block[1:2], half_reach * by_block[:7]]
    )
    images = jnp.concatenate(
        [images.reshape(32, 128), by_block[0], jnp.zeros((4, 128), jnp.float32)]
    )
    padded = jnp.concatenate([table, jnp.zeros((92, 128), jnp.float32)])
    weights = fit(jnp.stack([shift, reach]), images, padded)

    weights = weights[:4, :32].reshape(4, 8, 4).transpose(1, 2, 0)
    none = jnp.zeros((1, 4, 4), jnp.float32)
    rising = jnp.concatenate([none, weights[:1], 0.5 * weights[1:]]) * reach
    level = jnp.concatenate([weights, none]) * shift
    falling = jnp.concatenate([weights[1:], none, none]) * half_reach
    image_weights = rising + level + falling
    both = jnp.concatenate([weights, image_weights])
    column = jnp.arange(4)
    choose = (column[None, :, None] == (column[None, None, :] + column[:, None, None]) % 4)
    mix = jnp.sum(both[:, None] * choose[None].astype(jnp.float32), axis=2)
    mix = jnp.broadcast_to(mix.reshape(68, 1, 4, 1), (68, 2, 4, 128)).reshape(68, 8, 128)
    iterate, remainder = combine(mix, blocks)

    def unpack(block):
        return block.reshape(16, 3, 2, 4, 128).transpose(2, 0, 3, 1, 4)

    return unpack(iterate), unpack(remainder)


def solution(mesh):
    split = Mesh(mesh.devices.reshape(4, 8, 4, 2), AXES)
    return jax.shard_map(
        shards,
        mesh=split,
        in_specs=(
            P(GX, GY, None, None, None),
            P(),
            P(),
            P(GX, GY, None),
            P(GX, GY, None),
            P(GX, GY, None, None),
            P(GX, GY, None),
        ),
        out_specs=(P(GX, GY, None, None, None), P(GX, GY, None, None, None)),
        check_vma=False,
    )
```

time: 833 us -> 181 us (0.22); the launches traced: 820 us -> 179 us
  blocking collectives: 358 us -> 16.8 us
  other arithmetic: 135 us -> 12.3 us
  matrix products: 92.9 us -> 0 us
  local copies, waits for them, and re-layouts: 67.1 us -> 17.2 us
  loops' own time: 44.2 us -> 0 us
  starting transfers between devices: 101 us -> 57.2 us
  Pallas kernels: 0 us -> 37.7 us
  waiting for transfers between devices: 17.9 us -> 33.7 us
    psum x36 -> x0, blocking collectives: 358 us -> none  [one_axis_at_a_time(): shard = lax.psum(shard, axis)]
    dot_general x190 -> x0, matrix products: 92.9 us -> none  [the longest x32 42.8 us: one_row(): total = jnp.dot(line[None, :], unknowns, precision=exact_mode)[0]]
    another operation x128 -> x9, other arithmetic: 87.4 us -> 1.42 us  [the longest x4 0.68 us: shards(): bottom = jnp.stack([left[:2], own[:2], right[:2]])]
    ppermute x36 -> x16, starting transfers between devices: 101 us -> 50.1 us  [the longest x8 34.4 us: neighbours(): before = lax.ppermute(high, axis, [(i, i + 1) for i in range(count - 1)])]
    another operation x2 -> x0, loops' own time: 44.2 us -> none  [the longest x1 43.5 us: solve_small(): orthonormal, triangle = lax.fori_loop(0, count, one_column, start)]
    pallas_call x0 -> x11, Pallas kernels: none -> 37.7 us  [the longest x4 22.6 us: two_steps(): pl.pallas_call(make_pair_kernel(first_round), out_shape=(jax.ShapeDtypeSt...]
    reduce_sum x240 -> x5, other arithmetic: 27 us -> 3.38 us  [the longest x2 2 us: shards(): table = jnp.sum(lax.all_to_all(copies, axes, 0, 0, tiled=True), axis=0)]
    another operation x32 -> x10, local copies, waits for them, and re-layouts: 20.9 us -> 0.05 us  [the longest x9 0.04 us: shards(): bottom = jnp.stack([left[:2], own[:2], right[:2]])]
  transfers between devices with their start and end apart: 36 -> 17, of which waited for: 25 -> 10; matrix products, arithmetic and copies ran while one was open for 1% -> 5% of each run, Pallas kernels for 0% -> 4%
where the time goes in v1:
time: 181 us; the launch traced here: 179 us
  starting transfers between devices  57.2 us (32%)
  Pallas kernels  37.7 us (21%)
  waiting for transfers between devices  33.7 us (19%)
  local copies, waits for them, and re-layouts  17.2 us (10%)
  blocking collectives  16.8 us (9%)
  other arithmetic  12.3 us (7%)
  between operations  4.61 us (3%)
    ppermute x8, starting transfers between devices, neighbours(): before = lax.ppermute(high, axis, [(i, i + 1) for i in range(count - 1)])  34.4 us
    pallas_call x4, Pallas kernels, two_steps(): pl.pallas_call(make_pair_kernel(first_round), out_shape=(jax.ShapeDtypeSt...  22.6 us
    all_to_all x1, blocking collectives, shards(): table = jnp.sum(lax.all_to_all(copies, axes, 0, 0, tiled=True), axis=0)  16.8 us
    ppermute x8, starting transfers between devices, neighbours(): after = lax.ppermute(low, axis, [(i + 1, i) for i in range(count - 1)])  15.7 us
    all_to_all x1, waiting for transfers between devices, shards(): table = jnp.sum(lax.all_to_all(copies, axes, 0, 0, tiled=True), axis=0)  12.9 us
    ppermute x8, waiting for transfers between devices, neighbours(): after = lax.ppermute(low, axis, [(i + 1, i) for i in range(count - 1)])  12.1 us
    pallas_call x5, Pallas kernels, sketch(): pl.pallas_call(make_sketch_kernel(kinds), out_shape=jax.ShapeDtypeStruct(...  8.8 us
    ppermute x8, waiting for transfers between devices, neighbours(): before = lax.ppermute(high, axis, [(i, i + 1) for i in range(count - 1)])  8.63 us
  transfers between devices with their start and end apart: 17, of which 10 were waited for; matrix products, arithmetic and copies ran while one was open for 5% of the time, Pallas kernels for 4%

profile of v1, /device:TPU:1, one launch (start us, length us, event | category | flops | bytes accessed | tf_op | source)
XLA Modules:
  0.0 179.5 jit_solution(16174454260891943456)
XLA Ops:
  0.6 1.6 fusion.31
  2.3 0.7 copy-done.15
  3.0 5.0 %add_select_fusion.1 = f32[2,16,128]{2,1,0:T(8,128)S(1)} fusion(s32[2,16,128]{2,1,0:T(8,128)S(1)} %copy-done.15, s32[2,16,128]{2,1,0:T(8,128)S(1)} %copy-done.16, f32[]{:T(128)} %bitcast.25, f32[]{:T(128)} %bitcast.24, f32[]{:T(128)} %bitcast.23, f32[]{:T(128)} %bitcast.22, f32[]{:T(128)} %bitcast.21, f32[]{:T(128)} %bitcast.20, f32[]{:T(128)} %bitcast.19, ...), kind=kLoop, calls=%fused_computation.58 | loop fusion | flops 102400 | bytes 49184 | tf_op jit(solution)/shard_map/jit(_where)/select_n | solution.py:353
  8.0 1.0 copy.68
  9.0 1.3 collective-permute-start.1
  10.3 5.0 %collective-permute-start = (f32[400,128]{1,0:T(8,128)S(1)}, f32[400,128]{1,0:T(8,128)S(1)}, u32[]{:S(2)}, u32[]{:S(2)}) collective-permute-start(f32[400,128]{1,0:T(8,128)S(1)} %get-tuple-element.51), channel_id=1, source_target_pairs={{0,8},{8,16},{16,24},{24,32},{32,40},{40,48},{48,56},{56,64},{64,7... | collective-permute-start | bytes 614408 | tf_op jit(solution)/shard_map/ppermute | solution.py:330
  15.3 0.8 fusion.28
  16.3 0.6 multiply_reduce_fusion.1
  16.9 0.6 fusion.25
  17.5 0.7 gather_fusion
  18.2 0.7 multiply_reduce_fusion.2
  23.6 0.6 add_convert_fusion
  24.5 4.7 %collective-permute-start.3 = (f32[152,128]{1,0:T(8,128)S(1)}, f32[152,128]{1,0:T(8,128)S(1)}, u32[]{:S(2)}, u32[]{:S(2)}) collective-permute-start(f32[152,128]{1,0:T(8,128)S(1)} %pad_maximum_fusion.3), channel_id=1, source_target_pairs={{1,0},{2,1},{3,2},{4,3},{5,4},{6,5},{7,6},{9,8},{10,9},{11,10},{12... | collective-permute-start | bytes 233480 | tf_op jit(solution)/shard_map/ppermute | solution.py:331
  29.2 1.9 %collective-permute-start.2 = (f32[152,128]{1,0:T(8,128)S(1)}, f32[152,128]{1,0:T(8,128)S(1)}, u32[]{:S(2)}, u32[]{:S(2)}) collective-permute-start(f32[152,128]{1,0:T(8,128)S(1)} %pad_maximum_fusion.2), channel_id=1, source_target_pairs={{0,1},{1,2},{2,3},{3,4},{4,5},{5,6},{6,7},{8,9},{9,10},{10,11},{11... | collective-permute-start | bytes 233480 | tf_op jit(solution)/shard_map/ppermute | solution.py:330
  31.2 1.3 collective-permute-done.2
  32.7 5.6 %two_steps.4 = (f32[18,3,3,8,128]{4,3,2,1,0:T(8,128)S(1)}, f32[16,3,8,128]{3,2,1,0:T(8,128)S(1)}) custom-call(f32[256]{0:T(256)S(1)} %pad_maximum_fusion.15.coef, f32[16,3,8,128]{3,2,1,0:T(8,128)S(1)} %bitcast.164, f32[16,3,8,128]{3,2,1,0:T(8,128)S(1)} %bitcast.153, f32[16,3,8,128]{3,2,1,0:T(8,128)S(1)} %bitcast.165, f32[3,2,3,8,128]{4,3,2,1,0:T(8,128)S(1)} %bitcast.167, ...), custom_call_target="tpu_custom_call" | custom-call | tf_op jit(solution)/shard_map/two_steps/pallas_call | solution.py:128
  38.3 2.9 %collective-permute-start.4 = (f32[16,3,8,128]{3,2,1,0:T(8,128)S(1)}, f32[16,3,8,128]{3,2,1,0:T(8,128)S(1)}, u32[]{:S(2)}, u32[]{:S(2)}) collective-permute-start(f32[16,3,8,128]{3,2,1,0:T(8,128)S(1)} %get-tuple-element.13.refs_1_.own.l0), channel_id=1, source_target_pairs={{0,8},{8,16},{16,24},{24,32},{32,40},{40,48},{48,56},{56,64},{64,7... | collective-permute-start | bytes 589832 | tf_op jit(solution)/shard_map/ppermute | solution.py:330
  41.2 1.3 collective-permute-start.5
  42.6 2.7 %collective-permute-done.4.left = f32[16,3,8,128]{3,2,1,0:T(8,128)S(1)} collective-permute-done((f32[16,3,8,128]{3,2,1,0:T(8,128)S(1)}, f32[16,3,8,128]{3,2,1,0:T(8,128)S(1)}, u32[]{:S(2)}, u32[]{:S(2)}) %collective-permute-start.4) | collective-permute-done | bytes 196640 | tf_op jit(solution)/shard_map/ppermute | solution.py:330
  45.3 4.1 %collective-permute-done.5.right = f32[16,3,8,128]{3,2,1,0:T(8,128)S(1)} collective-permute-done((f32[16,3,8,128]{3,2,1,0:T(8,128)S(1)}, f32[16,3,8,128]{3,2,1,0:T(8,128)S(1)}, u32[]{:S(2)}, u32[]{:S(2)}) %collective-permute-start.5) | collective-permute-done | bytes 196640 | tf_op jit(solution)/shard_map/ppermute | solution.py:331
  49.4 2.0 %collective-permute-start.7 = (f32[3,2,3,8,128]{4,3,2,1,0:T(8,128)S(1)}, f32[3,2,3,8,128]{4,3,2,1,0:T(8,128)S(1)}, u32[]{:S(2)}, u32[]{:S(2)}) collective-permute-start(f32[3,2,3,8,128]{4,3,2,1,0:T(8,128)S(1)} %pad_maximum_fusion.7), channel_id=1, source_target_pairs={{1,0},{2,1},{3,2},{4,3},{5,4},{6,5},{7,6},{9,8},{10,9},{11,10},{12... | collective-permute-start | bytes 221192 | tf_op jit(solution)/shard_map/ppermute | solution.py:331
  51.4 4.1 %collective-permute-start.6 = (f32[3,2,3,8,128]{4,3,2,1,0:T(8,128)S(1)}, f32[3,2,3,8,128]{4,3,2,1,0:T(8,128)S(1)}, u32[]{:S(2)}, u32[]{:S(2)}) collective-permute-start(f32[3,2,3,8,128]{4,3,2,1,0:T(8,128)S(1)} %pad_maximum_fusion.6), channel_id=1, source_target_pairs={{0,1},{1,2},{2,3},{3,4},{4,5},{5,6},{6,7},{8,9},{9,10},{10,11},{11... | collective-permute-start | bytes 221192 | tf_op jit(solution)/shard_map/ppermute | solution.py:330
  55.7 1.3 collective-permute-done.6.down
  57.0 5.7 %two_steps.5 = (f32[18,3,3,8,128]{4,3,2,1,0:T(8,128)S(1)}, f32[16,3,8,128]{3,2,1,0:T(8,128)S(1)}) custom-call(f32[256]{0:T(256)S(1)} %pad_maximum_fusion.15.coef, f32[16,3,8,128]{3,2,1,0:T(8,128)S(1)} %collective-permute-done.4.left, f32[16,3,8,128]{3,2,1,0:T(8,128)S(1)} %get-tuple-element.13.refs_1_.own.l0, ...), custom_call_target="tpu_custom_call" | custom-call | tf_op jit(solution)/shard_map/two_steps/pallas_call | solution.py:128
  62.7 4.8 %collective-permute-start.8 = (f32[16,3,8,128]{3,2,1,0:T(8,128)S(1)}, f32[16,3,8,128]{3,2,1,0:T(8,128)S(1)}, u32[]{:S(2)}, u32[]{:S(2)}) collective-permute-start(f32[16,3,8,128]{3,2,1,0:T(8,128)S(1)} %get-tuple-element.15.refs_1_.own.l1), channel_id=1, source_target_pairs={{0,8},{8,16},{16,24},{24,32},{32,40},{40,48},{48,56},{56,64},{64,7... | collective-permute-start | bytes 589832 | tf_op jit(solution)/shard_map/ppermute | solution.py:330
  67.4 1.3 collective-permute-start.9
  68.8 1.4 collective-permute-done.8.left
  70.2 4.2 %collective-permute-done.9.right = f32[16,3,8,128]{3,2,1,0:T(8,128)S(1)} collective-permute-done((f32[16,3,8,128]{3,2,1,0:T(8,128)S(1)}, f32[16,3,8,128]{3,2,1,0:T(8,128)S(1)}, u32[]{:S(2)}, u32[]{:S(2)}) %collective-permute-start.9) | collective-permute-done | bytes 196640 | tf_op jit(solution)/shard_map/ppermute | solution.py:331
  74.4 1.9 %collective-permute-start.11 = (f32[3,2,3,8,128]{4,3,2,1,0:T(8,128)S(1)}, f32[3,2,3,8,128]{4,3,2,1,0:T(8,128)S(1)}, u32[]{:S(2)}, u32[]{:S(2)}) collective-permute-start(f32[3,2,3,8,128]{4,3,2,1,0:T(8,128)S(1)} %pad_maximum_fusion.9), channel_id=1, source_target_pairs={{1,0},{2,1},{3,2},{4,3},{5,4},{6,5},{7,6},{9,8},{10,9},{11,10},{12... | collective-permute-start | bytes 221192 | tf_op jit(solution)/shard_map/ppermute | solution.py:331
  76.3 5.2 %collective-permute-start.10 = (f32[3,2,3,8,128]{4,3,2,1,0:T(8,128)S(1)}, f32[3,2,3,8,128]{4,3,2,1,0:T(8,128)S(1)}, u32[]{:S(2)}, u32[]{:S(2)}) collective-permute-start(f32[3,2,3,8,128]{4,3,2,1,0:T(8,128)S(1)} %pad_maximum_fusion.8), channel_id=1, source_target_pairs={{0,1},{1,2},{2,3},{3,4},{4,5},{5,6},{6,7},{8,9},{9,10},{10,11},{11... | collective-permute-start | bytes 221192 | tf_op jit(solution)/shard_map/ppermute | solution.py:330
  81.5 0.7 fusion.4
  82.3 0.7 collective-permute-done.10.down
  82.9 5.7 %two_steps.6 = (f32[18,3,3,8,128]{4,3,2,1,0:T(8,128)S(1)}, f32[16,3,8,128]{3,2,1,0:T(8,128)S(1)}) custom-call(f32[256]{0:T(256)S(1)} %pad_maximum_fusion.15.coef, f32[16,3,8,128]{3,2,1,0:T(8,128)S(1)} %collective-permute-done.8.left, f32[16,3,8,128]{3,2,1,0:T(8,128)S(1)} %get-tuple-element.15.refs_1_.own.l1, ...), custom_call_target="tpu_custom_call" | custom-call | tf_op jit(solution)/shard_map/two_steps/pallas_call | solution.py:128
  88.6 4.8 %collective-permute-start.12 = (f32[16,3,8,128]{3,2,1,0:T(8,128)S(1)}, f32[16,3,8,128]{3,2,1,0:T(8,128)S(1)}, u32[]{:S(2)}, u32[]{:S(2)}) collective-permute-start(f32[16,3,8,128]{3,2,1,0:T(8,128)S(1)} %get-tuple-element.17.refs_1_.own.l2), channel_id=1, source_target_pairs={{0,8},{8,16},{16,24},{24,32},{32,40},{40,48},{48,56},{56,64},{64,7... | collective-permute-start | bytes 589832 | tf_op jit(solution)/shard_map/ppermute | solution.py:330
  93.4 1.3 collective-permute-start.13
  94.7 1.3 collective-permute-done.12.left
  96.0 3.8 %collective-permute-done.13.right = f32[16,3,8,128]{3,2,1,0:T(8,128)S(1)} collective-permute-done((f32[16,3,8,128]{3,2,1,0:T(8,128)S(1)}, f32[16,3,8,128]{3,2,1,0:T(8,128)S(1)}, u32[]{:S(2)}, u32[]{:S(2)}) %collective-permute-start.13) | collective-permute-done | bytes 196640 | tf_op jit(solution)/shard_map/ppermute | solution.py:331
  99.8 0.7 pad_maximum_fusion.11
  100.5 1.9 %collective-permute-start.15 = (f32[3,2,3,8,128]{4,3,2,1,0:T(8,128)}, f32[3,2,3,8,128]{4,3,2,1,0:T(8,128)S(1)}, u32[]{:S(2)}, u32[]{:S(2)}) collective-permute-start(f32[3,2,3,8,128]{4,3,2,1,0:T(8,128)} %pad_maximum_fusion.11), channel_id=1, source_target_pairs={{1,0},{2,1},{3,2},{4,3},{5,4},{6,5},{7,6},{9,8},{10,9},{11,10},{12... | collective-permute-start | bytes 221192 | tf_op jit(solution)/shard_map/ppermute | solution.py:331
  102.4 0.6 pad_maximum_fusion.10
  103.0 5.7 %collective-permute-start.14 = (f32[3,2,3,8,128]{4,3,2,1,0:T(8,128)}, f32[3,2,3,8,128]{4,3,2,1,0:T(8,128)S(1)}, u32[]{:S(2)}, u32[]{:S(2)}) collective-permute-start(f32[3,2,3,8,128]{4,3,2,1,0:T(8,128)} %pad_maximum_fusion.10), channel_id=1, source_target_pairs={{0,1},{1,2},{2,3},{3,4},{4,5},{5,6},{6,7},{8,9},{9,10},{10,11},{11... | collective-permute-start | bytes 221192 | tf_op jit(solution)/shard_map/ppermute | solution.py:330
  108.8 1.5 gather_fusion.2
  110.3 1.4 gather_fusion.1
  111.8 1.2 sketch.5
  113.0 1.9 %sketch.6 = f32[8,128]{1,0:T(8,128)S(1)} custom-call(s32[128]{0:T(128)S(1)} %fusion.23.where, f32[64,8,128]{2,1,0:T(8,128)S(1)} %bitcast.148, f32[18,3,3,8,128]{4,3,2,1,0:T(8,128)S(1)} %get-tuple-element.12.refs_0_.before.m0, f32[16,3,8,128]{3,2,1,0:T(8,128)S(1)} %get-tuple-element.13.refs_1_.own.l0), custom_call_target="tpu_custom_call" | custom-call | tf_op jit(solution)/shard_map/sketch/pallas_call | solution.py:184
  114.9 1.9 %sketch.7 = f32[8,128]{1,0:T(8,128)S(1)} custom-call(s32[128]{0:T(128)S(1)} %fusion.23.where, f32[64,8,128]{2,1,0:T(8,128)S(1)} %bitcast.149, f32[18,3,3,8,128]{4,3,2,1,0:T(8,128)S(1)} %get-tuple-element.14.refs_0_.before.m1, f32[16,3,8,128]{3,2,1,0:T(8,128)S(1)} %get-tuple-element.15.refs_1_.own.l1), custom_call_target="tpu_custom_call" | custom-call | tf_op jit(solution)/shard_map/sketch/pallas_call | solution.py:184
  116.9 1.9 %sketch.8 = f32[8,128]{1,0:T(8,128)S(1)} custom-call(s32[128]{0:T(128)S(1)} %fusion.23.where, f32[64,8,128]{2,1,0:T(8,128)S(1)} %bitcast.150, f32[18,3,3,8,128]{4,3,2,1,0:T(8,128)S(1)} %get-tuple-element.16.refs_0_.before.m2, f32[16,3,8,128]{3,2,1,0:T(8,128)S(1)} %get-tuple-element.17.refs_1_.own.l2), custom_call_target="tpu_custom_call" | custom-call | tf_op jit(solution)/shard_map/sketch/pallas_call | solution.py:184
  118.8 0.6 copy-done.9
  119.4 0.9 copy-done.1
  120.4 0.9 copy-done.10
  121.3 5.6 %two_steps.7 = (f32[18,3,3,8,128]{4,3,2,1,0:T(8,128)S(1)}, f32[16,3,8,128]{3,2,1,0:T(8,128)S(1)}) custom-call(f32[256]{0:T(256)S(1)} %pad_maximum_fusion.15.coef, f32[16,3,8,128]{3,2,1,0:T(8,128)S(1)} %copy-done.6, f32[16,3,8,128]{3,2,1,0:T(8,128)S(1)} %copy-done.1, f32[16,3,8,128]{3,2,1,0:T(8,128)S(1)} %copy-done.8, f32[3,2,3,8,128]{4,3,2,1,0:T(8,128)S(1)} %copy-done.10, ...), custom_call_target="tpu_custom_call" | custom-call | tf_op jit(solution)/shard_map/two_steps/pallas_call | solution.py:128
  126.9 1.9 %sketch.9 = f32[8,128]{1,0:T(8,128)S(1)} custom-call(s32[128]{0:T(128)S(1)} %fusion.23.where, f32[64,8,128]{2,1,0:T(8,128)S(1)} %bitcast.151, f32[18,3,3,8,128]{4,3,2,1,0:T(8,128)S(1)} %get-tuple-element.18.refs_0_.m3, f32[16,3,8,128]{3,2,1,0:T(8,128)S(1)} %get-tuple-element.19.refs_1_.l3), custom_call_target="tpu_custom_call" | custom-call | tf_op jit(solution)/shard_map/sketch/pallas_call | solution.py:184
  128.8 0.7 copy-done.3
  129.9 16.8 %all_to_all.10 = f32[16,36,128]{2,1,0:T(8,128)} all-to-all(f32[16,36,128]{2,1,0:T(8,128)S(1)} %broadcast_in_dim.125), channel_id=1, replica_groups=mesh['gx_0'=4,'gx_1'=8,'gy_0'=4,'gy_1'=2] {'gx_0','gy_0'}, dimensions={0} | all-to-all | bytes 589824 | tf_op jit(solution)/shard_map/all_to_all | solution.py:416
  146.7 1.0 reduce_sum.57
  147.7 0.8 broadcast_in_dim.126
  148.4 7.1 %all-to-all-start.1 = ((f32[16,36,128]{2,1,0:T(8,128)}), f32[16,36,128]{2,1,0:T(8,128)}, u32[]{:S(2)}, u32[]{:S(2)}) async-start(f32[16,36,128]{2,1,0:T(8,128)} %broadcast_in_dim.126), calls=%async_computation.1 | async-start | bytes 655360 | tf_op jit(solution)/shard_map/all_to_all | solution.py:416
  155.7 12.9 %all-to-all-done.1 = f32[16,36,128]{2,1,0:T(8,128)} async-done(((f32[16,36,128]{2,1,0:T(8,128)}), f32[16,36,128]{2,1,0:T(8,128)}, u32[]{:S(2)}, u32[]{:S(2)}) %all-to-all-start.1) | async-done | bytes 294944 | tf_op jit(solution)/shard_map/all_to_all | solution.py:416
  168.6 1.0 reduce_sum.58
  169.7 4.6 %fit.1 = f32[8,128]{1,0:T(8,128)S(1)} custom-call(f32[2]{0:T(128)S(1)} %pad_maximum_fusion.16.scalars, f32[40,128]{1,0:T(8,128)S(1)} %maximum_maximum_fusion.images, f32[128,128]{1,0:T(8,128)S(1)} %concatenate.82.sketches), custom_call_target="tpu_custom_call" | custom-call | tf_op jit(solution)/shard_map/fit/pallas_call | solution.py:259
  175.3 0.9 copy-done.2
  176.2 0.9 copy-done.4
  177.1 1.6 combine.1
  178.7 0.8 copy_bitcast_fusion
  (117 shorter events, 3.9 us)
Async XLA Ops:
  0.6 1.6 copy-start.16
  2.3 0.7 copy-start.15
  9.0 15.4 %collective-permute-start.1 = (f32[400,128]{1,0:T(8,128)S(1)}, f32[400,128]{1,0:T(8,128)S(1)}, u32[]{:S(2)}, u32[]{:S(2)}) collective-permute-start(f32[400,128]{1,0:T(8,128)S(1)} %get-tuple-element.50), channel_id=1, source_target_pairs={{8,0},{16,8},{24,16},{32,24},{40,32},{48,40},{56,48},{64,56},{72,6... | collective-permute-start | bytes 614408 | tf_op jit(solution)/shard_map/ppermute | solution.py:331
  10.3 14.1 %collective-permute-start = (f32[400,128]{1,0:T(8,128)S(1)}, f32[400,128]{1,0:T(8,128)S(1)}, u32[]{:S(2)}, u32[]{:S(2)}) collective-permute-start(f32[400,128]{1,0:T(8,128)S(1)} %get-tuple-element.51), channel_id=1, source_target_pairs={{0,8},{8,16},{16,24},{24,32},{32,40},{40,48},{48,56},{56,64},{64,7... | collective-permute-start | bytes 614408 | tf_op jit(solution)/shard_map/ppermute | solution.py:330
  15.3 0.8 copy-start.12
  16.3 0.7 copy-start.14
  22.1 0.7 copy-start.17
  22.8 0.8 copy-start.13
  24.5 6.8 %collective-permute-start.3 = (f32[152,128]{1,0:T(8,128)S(1)}, f32[152,128]{1,0:T(8,128)S(1)}, u32[]{:S(2)}, u32[]{:S(2)}) collective-permute-start(f32[152,128]{1,0:T(8,128)S(1)} %pad_maximum_fusion.3), channel_id=1, source_target_pairs={{1,0},{2,1},{3,2},{4,3},{5,4},{6,5},{7,6},{9,8},{10,9},{11,10},{12... | collective-permute-start | bytes 233480 | tf_op jit(solution)/shard_map/ppermute | solution.py:331
  29.2 3.4 %collective-permute-start.2 = (f32[152,128]{1,0:T(8,128)S(1)}, f32[152,128]{1,0:T(8,128)S(1)}, u32[]{:S(2)}, u32[]{:S(2)}) collective-permute-start(f32[152,128]{1,0:T(8,128)S(1)} %pad_maximum_fusion.2), channel_id=1, source_target_pairs={{0,1},{1,2},{2,3},{3,4},{4,5},{5,6},{6,7},{8,9},{9,10},{10,11},{11... | collective-permute-start | bytes 233480 | tf_op jit(solution)/shard_map/ppermute | solution.py:330
  38.3 7.0 %collective-permute-start.4 = (f32[16,3,8,128]{3,2,1,0:T(8,128)S(1)}, f32[16,3,8,128]{3,2,1,0:T(8,128)S(1)}, u32[]{:S(2)}, u32[]{:S(2)}) collective-permute-start(f32[16,3,8,128]{3,2,1,0:T(8,128)S(1)} %get-tuple-element.13.refs_1_.own.l0), channel_id=1, source_target_pairs={{0,8},{8,16},{16,24},{24,32},{32,40},{40,48},{48,56},{56,64},{64,7... | collective-permute-start | bytes 589832 | tf_op jit(solution)/shard_map/ppermute | solution.py:330
  41.2 8.1 %collective-permute-start.5 = (f32[16,3,8,128]{3,2,1,0:T(8,128)S(1)}, f32[16,3,8,128]{3,2,1,0:T(8,128)S(1)}, u32[]{:S(2)}, u32[]{:S(2)}) collective-permute-start(f32[16,3,8,128]{3,2,1,0:T(8,128)S(1)} %get-tuple-element.13.refs_1_.own.l0), channel_id=1, source_target_pairs={{8,0},{16,8},{24,16},{32,24},{40,32},{48,40},{56,48},{64,56},{72,6... | collective-permute-start | bytes 589832 | tf_op jit(solution)/shard_map/ppermute | solution.py:331
  49.4 6.3 %collective-permute-start.7 = (f32[3,2,3,8,128]{4,3,2,1,0:T(8,128)S(1)}, f32[3,2,3,8,128]{4,3,2,1,0:T(8,128)S(1)}, u32[]{:S(2)}, u32[]{:S(2)}) collective-permute-start(f32[3,2,3,8,128]{4,3,2,1,0:T(8,128)S(1)} %pad_maximum_fusion.7), channel_id=1, source_target_pairs={{1,0},{2,1},{3,2},{4,3},{5,4},{6,5},{7,6},{9,8},{10,9},{11,10},{12... | collective-permute-start | bytes 221192 | tf_op jit(solution)/shard_map/ppermute | solution.py:331
  51.4 5.5 %collective-permute-start.6 = (f32[3,2,3,8,128]{4,3,2,1,0:T(8,128)S(1)}, f32[3,2,3,8,128]{4,3,2,1,0:T(8,128)S(1)}, u32[]{:S(2)}, u32[]{:S(2)}) collective-permute-start(f32[3,2,3,8,128]{4,3,2,1,0:T(8,128)S(1)} %pad_maximum_fusion.6), channel_id=1, source_target_pairs={{0,1},{1,2},{2,3},{3,4},{4,5},{5,6},{6,7},{8,9},{9,10},{10,11},{11... | collective-permute-start | bytes 221192 | tf_op jit(solution)/shard_map/ppermute | solution.py:330
  62.7 7.5 %collective-permute-start.8 = (f32[16,3,8,128]{3,2,1,0:T(8,128)S(1)}, f32[16,3,8,128]{3,2,1,0:T(8,128)S(1)}, u32[]{:S(2)}, u32[]{:S(2)}) collective-permute-start(f32[16,3,8,128]{3,2,1,0:T(8,128)S(1)} %get-tuple-element.15.refs_1_.own.l1), channel_id=1, source_target_pairs={{0,8},{8,16},{16,24},{24,32},{32,40},{40,48},{48,56},{56,64},{64,7... | collective-permute-start | bytes 589832 | tf_op jit(solution)/shard_map/ppermute | solution.py:330
  67.4 6.9 %collective-permute-start.9 = (f32[16,3,8,128]{3,2,1,0:T(8,128)S(1)}, f32[16,3,8,128]{3,2,1,0:T(8,128)S(1)}, u32[]{:S(2)}, u32[]{:S(2)}) collective-permute-start(f32[16,3,8,128]{3,2,1,0:T(8,128)S(1)} %get-tuple-element.15.refs_1_.own.l1), channel_id=1, source_target_pairs={{8,0},{16,8},{24,16},{32,24},{40,32},{48,40},{56,48},{64,56},{72,6... | collective-permute-start | bytes 589832 | tf_op jit(solution)/shard_map/ppermute | solution.py:331
  74.4 7.9 %collective-permute-start.11 = (f32[3,2,3,8,128]{4,3,2,1,0:T(8,128)S(1)}, f32[3,2,3,8,128]{4,3,2,1,0:T(8,128)S(1)}, u32[]{:S(2)}, u32[]{:S(2)}) collective-permute-start(f32[3,2,3,8,128]{4,3,2,1,0:T(8,128)S(1)} %pad_maximum_fusion.9), channel_id=1, source_target_pairs={{1,0},{2,1},{3,2},{4,3},{5,4},{6,5},{7,6},{9,8},{10,9},{11,10},{12... | collective-permute-start | bytes 221192 | tf_op jit(solution)/shard_map/ppermute | solution.py:331
  76.3 6.6 %collective-permute-start.10 = (f32[3,2,3,8,128]{4,3,2,1,0:T(8,128)S(1)}, f32[3,2,3,8,128]{4,3,2,1,0:T(8,128)S(1)}, u32[]{:S(2)}, u32[]{:S(2)}) collective-permute-start(f32[3,2,3,8,128]{4,3,2,1,0:T(8,128)S(1)} %pad_maximum_fusion.8), channel_id=1, source_target_pairs={{0,1},{1,2},{2,3},{3,4},{4,5},{5,6},{6,7},{8,9},{9,10},{10,11},{11... | collective-permute-start | bytes 221192 | tf_op jit(solution)/shard_map/ppermute | solution.py:330
  88.6 28.2 %copy-start = (f32[16,3,8,128]{3,2,1,0:T(8,128)}, f32[16,3,8,128]{3,2,1,0:T(8,128)S(1)}, u32[]{:S(2)}) copy-start(f32[16,3,8,128]{3,2,1,0:T(8,128)S(1)} %get-tuple-element.17.refs_1_.own.l2) | copy-start | bytes 589828
  88.6 7.4 %collective-permute-start.12 = (f32[16,3,8,128]{3,2,1,0:T(8,128)S(1)}, f32[16,3,8,128]{3,2,1,0:T(8,128)S(1)}, u32[]{:S(2)}, u32[]{:S(2)}) collective-permute-start(f32[16,3,8,128]{3,2,1,0:T(8,128)S(1)} %get-tuple-element.17.refs_1_.own.l2), channel_id=1, source_target_pairs={{0,8},{8,16},{16,24},{24,32},{32,40},{40,48},{48,56},{56,64},{64,7... | collective-permute-start | bytes 589832 | tf_op jit(solution)/shard_map/ppermute | solution.py:330
  93.4 6.4 %collective-permute-start.13 = (f32[16,3,8,128]{3,2,1,0:T(8,128)S(1)}, f32[16,3,8,128]{3,2,1,0:T(8,128)S(1)}, u32[]{:S(2)}, u32[]{:S(2)}) collective-permute-start(f32[16,3,8,128]{3,2,1,0:T(8,128)S(1)} %get-tuple-element.17.refs_1_.own.l2), channel_id=1, source_target_pairs={{8,0},{16,8},{24,16},{32,24},{40,32},{48,40},{56,48},{64,56},{72,6... | collective-permute-start | bytes 589832 | tf_op jit(solution)/shard_map/ppermute | solution.py:331
  96.0 7.1 %copy-start.5 = (f32[16,3,8,128]{3,2,1,0:T(8,128)}, f32[16,3,8,128]{3,2,1,0:T(8,128)S(1)}, u32[]{:S(2)}) copy-start(f32[16,3,8,128]{3,2,1,0:T(8,128)S(1)} %collective-permute-done.12.left) | copy-start | bytes 589828
  99.8 3.2 %copy-start.7 = (f32[16,3,8,128]{3,2,1,0:T(8,128)}, f32[16,3,8,128]{3,2,1,0:T(8,128)S(1)}, u32[]{:S(2)}) copy-start(f32[16,3,8,128]{3,2,1,0:T(8,128)S(1)} %collective-permute-done.13.right) | copy-start | bytes 589828
  100.5 18.3 %collective-permute-start.15 = (f32[3,2,3,8,128]{4,3,2,1,0:T(8,128)}, f32[3,2,3,8,128]{4,3,2,1,0:T(8,128)S(1)}, u32[]{:S(2)}, u32[]{:S(2)}) collective-permute-start(f32[3,2,3,8,128]{4,3,2,1,0:T(8,128)} %pad_maximum_fusion.11), channel_id=1, source_target_pairs={{1,0},{2,1},{3,2},{4,3},{5,4},{6,5},{7,6},{9,8},{10,9},{11,10},{12... | collective-permute-start | bytes 221192 | tf_op jit(solution)/shard_map/ppermute | solution.py:331
  103.0 15.7 %collective-permute-start.14 = (f32[3,2,3,8,128]{4,3,2,1,0:T(8,128)}, f32[3,2,3,8,128]{4,3,2,1,0:T(8,128)S(1)}, u32[]{:S(2)}, u32[]{:S(2)}) collective-permute-start(f32[3,2,3,8,128]{4,3,2,1,0:T(8,128)} %pad_maximum_fusion.10), channel_id=1, source_target_pairs={{0,1},{1,2},{2,3},{3,4},{4,5},{5,6},{6,7},{8,9},{9,10},{10,11},{11... | collective-permute-start | bytes 221192 | tf_op jit(solution)/shard_map/ppermute | solution.py:330
  108.8 1.5 copy-start.11
  116.9 2.6 %copy-start.6 = (f32[16,3,8,128]{3,2,1,0:T(8,128)S(1)}, f32[16,3,8,128]{3,2,1,0:T(8,128)}, u32[]{:S(2)}) copy-start(f32[16,3,8,128]{3,2,1,0:T(8,128)} %copy-done.5) | copy-start | bytes 589828
  116.9 2.6 %copy-start.8 = (f32[16,3,8,128]{3,2,1,0:T(8,128)S(1)}, f32[16,3,8,128]{3,2,1,0:T(8,128)}, u32[]{:S(2)}) copy-start(f32[16,3,8,128]{3,2,1,0:T(8,128)} %copy-done.7) | copy-start | bytes 589828
  118.8 0.6 copy-start.9
  119.4 0.9 copy-start.1
  120.4 0.9 copy-start.10
  128.8 0.7 copy-start.3
  148.4 20.2 %all-to-all-start.1 = ((f32[16,36,128]{2,1,0:T(8,128)}), f32[16,36,128]{2,1,0:T(8,128)}, u32[]{:S(2)}, u32[]{:S(2)}) async-start(f32[16,36,128]{2,1,0:T(8,128)} %broadcast_in_dim.126), calls=%async_computation.1 | async-start | bytes 655360 | tf_op jit(solution)/shard_map/all_to_all | solution.py:416
  175.3 0.9 copy-start.2
  176.2 0.9 copy-start.4

commit v2 on v1

v2 whole, which is shorter than its diff:
```python
import math

import jax
import jax.numpy as jnp
from jax import lax
from jax.experimental import pallas as pl
from jax.experimental.pallas import tpu as pltpu
from jax.sharding import Mesh
from jax.sharding import PartitionSpec as P

STEPS = 8
AXES = ("gx_0", "gx_1", "gy_0", "gy_1")
GX = ("gx_0", "gx_1")
GY = ("gy_0", "gy_1")

VMEM = pl.BlockSpec(memory_space=pltpu.VMEM)
SMEM = pl.BlockSpec(memory_space=pltpu.SMEM)
FAR = pl.BlockSpec(memory_space=pltpu.HBM)
PARAMS = pltpu.CompilerParams(vmem_limit_bytes=16 * 1024 * 1024)
F32 = jnp.float32


def tile_iota(axis):
    return lax.broadcasted_iota(jnp.int32, (8, 128), axis)


def shaped(*shape):
    return jax.ShapeDtypeStruct(shape, F32)


def prepare_kernel(class_scale, far_side, far_material, far_boundary, own, low, high, masked, *scratch):
    right_side, material, boundary, sems = scratch
    copies = [
        pltpu.make_async_copy(far_material, material, sems.at[0]),
        pltpu.make_async_copy(far_boundary, boundary, sems.at[1]),
        pltpu.make_async_copy(far_side, right_side, sems.at[2]),
    ]
    for copy in copies:
        copy.start()
    copies[0].wait()
    copies[1].wait()
    for x in range(2):
        for half in range(2):
            rows = pl.ds(half * 8, 8)
            field = jnp.zeros((8, 128), F32)
            kinds = material[x, rows]
            for number in range(8):
                field = field + jnp.where(kinds == number, class_scale[number], 0.0)
            field = jnp.where(boundary[x, rows] == 1, 0.0, field)
            masked[x, rows] = field
            (low, high)[x][pl.ds(384 + half * 8, 8)] = field

    copies[2].wait()

    def one_row(y, carry):
        for c in range(3):
            tile = jnp.concatenate([right_side[0, y, c], right_side[1, y, c]], axis=0)
            own[y, c] = tile
            low[pl.ds((y * 3 + c) * 8, 8)] = tile
            high[pl.ds((y * 3 + c) * 8, 8)] = tile
        return carry

    lax.fori_loop(0, 16, one_row, 0)


def prepare(class_scale, right_side, material, boundary):
    return pl.pallas_call(
        prepare_kernel,
        out_shape=(shaped(16, 3, 8, 128), shaped(400, 128), shaped(400, 128), shaped(2, 16, 128)),
        in_specs=[SMEM, FAR, FAR, FAR],
        out_specs=(VMEM,) * 4,
        scratch_shapes=[
            pltpu.VMEM((2, 16, 3, 4, 128), F32),
            pltpu.VMEM((2, 16, 128), jnp.int32),
            pltpu.VMEM((2, 16, 128), jnp.int32),
            pltpu.SemaphoreType.DMA((3,)),
        ],
        compiler_params=PARAMS,
        name="prepare",
    )(class_scale, right_side, material, boundary)


def setup_kernel(stencil, class_scale, rows, sign_bits, coef, interval, signs):
    def fill(n, total):
        tile = jnp.full((8, 128), stencil[n])
        coef[n] = tile
        return total + tile * tile

    total = lax.fori_loop(0, 243, fill, jnp.zeros((8, 128), F32))
    centre = [jnp.full((8, 128), stencil[13 * 9 + n]) for n in (0, 4, 8)]
    middle = (centre[0] + centre[1] + centre[2]) / 3.0
    for tile in centre:
        total = total - tile * tile
    spread = jnp.sqrt(jnp.maximum(total, 0.0) / 3.0)
    least = most = jnp.full((8, 128), class_scale[0])
    for number in range(1, 8):
        value = jnp.full((8, 128), class_scale[number])
        least, most = jnp.minimum(least, value), jnp.maximum(most, value)
    bottom = jnp.minimum(least * (middle - spread), 1.0)
    top = jnp.maximum(most * (middle + spread), 1.0)
    shift = 0.5 * (bottom + top)
    interval[0] = shift
    interval[1] = jnp.maximum(0.5 * (top - bottom), 0.05 * shift)

    lanes = lax.broadcasted_iota(jnp.int32, (1, 128), 1)
    size = 1.0 / math.sqrt(128.0)

    def sample(n, carry):
        for part in range(2):
            spot = rows[n + 64 * part]
            tile = lax.shift_right_logical(spot, 7)
            x = (tile >= 48).astype(jnp.int32)
            place = tile - 48 * x
            y = lax.shift_right_logical(place * 171, 9)
            bits = sign_bits[x, place - 3 * y, pl.ds(y, 1), :]
            common = (spot & 127) & lanes
            for by in (4, 2, 1):
                common = common ^ lax.shift_right_logical(common, by)
            row = jnp.where(((common ^ bits) & 1) == 1, size, -size)
            signs[n, pl.ds(4 * part, 4), :] = jnp.broadcast_to(row, (4, 128))
        return carry

    lax.fori_loop(0, 64, sample, 0, unroll=4)


def setup(stencil, class_scale, rows, sign_bits):
    return pl.pallas_call(
        setup_kernel,
        out_shape=(shaped(243, 8, 128), shaped(2, 8, 128), shaped(64, 8, 128)),
        in_specs=[SMEM, SMEM, SMEM, VMEM],
        out_specs=(VMEM,) * 3,
        compiler_params=PARAMS,
        name="setup",
    )(stencil, class_scale, rows, sign_bits)


def stencil_rows(coef, component, rows, terms):
    sums = [[None] * rows for _ in range(3)]
    for dx, tile in terms:
        for c in range(3):
            tiles = [tile(r, c) for r in range(rows + 2)]
            for dy in range(3):
                for dz in range(3):
                    weight = coef[(dx * 9 + dy * 3 + dz) * 9 + component * 3 + c]
                    for r in range(rows):
                        term = weight * tiles[r + dy]
                        old = sums[dz][r]
                        sums[dz][r] = term if old is None else old + term
    lane = tile_iota(1)
    out = []
    for r in range(rows):
        low = jnp.where(lane > 0, pltpu.roll(sums[0][r], 1, 1), 0.0)
        high = jnp.where(lane < 127, pltpu.roll(sums[2][r], 127, 1), 0.0)
        out.append(sums[1][r] + low + high)
    return out


def five_pairs(put, left, own, right):
    half = tile_iota(0) < 4
    turned = [pltpu.roll(tile, 4, 0) for tile in (left, own, right)]
    put(0, left)
    put(1, jnp.where(half, turned[0], turned[1]))
    put(2, own)
    put(3, jnp.where(half, turned[1], turned[2]))
    put(4, right)


def recurrence(interval):
    shift = interval[0]
    gain = 2.0 / interval[1]
    inside, fixed = -shift * gain, gain - shift * gain

    def value(alpha, total, centre):
        return (alpha * gain) * total + jnp.where(alpha == 0.0, fixed, inside) * centre

    return value


SEVEN = 7


def inner_kernel(coef, own, part):
    def body(i, carry):
        component, first, side = i % 3, i // 3 % 2 * SEVEN, i // 6
        terms = [(2 - 2 * side, lambda r, c: own[first + r, c])]
        for r, total in enumerate(stencil_rows(coef, component, SEVEN, terms)):
            part[first + r, side, component] = total
        return carry

    lax.fori_loop(0, 12, body, 0)


def inner(coef, own):
    return pl.pallas_call(
        inner_kernel,
        out_shape=shaped(14, 2, 3, 8, 128),
        in_specs=[VMEM, VMEM],
        out_specs=VMEM,
        compiler_params=PARAMS,
        name="inner",
    )(coef, own)


def make_middle_kernel(first_round):
    def kernel(coef, interval, left, own, right, part, before, scale, mid, work):
        def fill(y, carry):
            for c in range(3):

                def put(n, tile):
                    work[y, n, c] = tile

                five_pairs(put, left[y, c], own[y, c], right[y, c])
            return carry

        lax.fori_loop(0, 16, fill, 0)
        value_of = recurrence(interval)

        def body(i, carry):
            component, first, side = i % 3, i // 3 % 2 * SEVEN, i // 6
            terms = [
                (side + n, lambda r, c, n=n: work[first + r, 3 * side + n, c]) for n in range(2)
            ]
            for r, total in enumerate(stencil_rows(coef, component, SEVEN, terms)):
                row = first + r
                value = value_of(
                    scale[row + 1, side],
                    total + part[row, side, component],
                    work[row + 1, side * 2 + 1, component],
                )
                if first_round:
                    value = value * 0.5
                else:
                    value = value - before[row + 2, side * 2, component]
                mid[row + 2, side * 2, component] = value
            return carry

        lax.fori_loop(0, 12, body, 0)

    return kernel


def middle(first_round, *operands):
    return pl.pallas_call(
        make_middle_kernel(first_round),
        out_shape=shaped(18, 3, 3, 8, 128),
        in_specs=[VMEM] * 8,
        out_specs=VMEM,
        scratch_shapes=[pltpu.VMEM((16, 5, 3, 8, 128), F32)],
        compiler_params=PARAMS,
        name="middle",
    )(*operands)


def make_outer_kernel(first_round):
    def kernel(
        coef, interval, left, own, right, down, up, before, scale, scale_own, started, mid, last, work
    ):
        del started
        half = tile_iota(0) < 4
        value_of = recurrence(interval)
        for edge in range(2):
            for row in range(4):
                for c in range(3):

                    def put(n, tile):
                        work[edge, row, n, c] = tile

                    far = (down, up)[edge]
                    near = row - 2 + 14 * edge if edge == 0 else row + 14
                    if (row < 2) == (edge == 0):
                        five_pairs(put, *[far[n, row % 2, c] for n in range(3)])
                    else:
                        five_pairs(put, left[near, c], own[near, c], right[near, c])

        def edges(i, carry):
            component, edge = i % 3, i // 3
            for side in range(2):
                terms = [
                    (dx, lambda r, c, dx=dx: work[edge, r, side * 2 + dx, c]) for dx in range(3)
                ]
                for r, total in enumerate(stencil_rows(coef, component, 2, terms)):
                    row = edge * 16 + r
                    value = value_of(
                        scale[row, side], total, work[edge, r + 1, side * 2 + 1, component]
                    )
                    if first_round:
                        value = value * 0.5
                    else:
                        value = value - before[row, side * 2, component]
                    mid[row, side * 2, component] = value
            return carry

        lax.fori_loop(0, 6, edges, 0)

        def join(row, carry):
            for c in range(3):
                mid[row, 1, c] = jnp.where(
                    half, pltpu.roll(mid[row, 0, c], 4, 0), pltpu.roll(mid[row, 2, c], 4, 0)
                )
            return carry

        lax.fori_loop(0, 18, join, 0)

        def second(i, carry):
            component, first = i % 3, i // 3 * 8
            terms = [(dx, lambda r, c, dx=dx: mid[first + r, dx, c]) for dx in range(3)]
            for r, total in enumerate(stencil_rows(coef, component, 8, terms)):
                row = first + r
                value = value_of(scale_own[row], total, mid[row + 1, 1, component])
                last[row, component] = value - own[row, component]
            return carry

        lax.fori_loop(0, 6, second, 0)

    return kernel


def outer(first_round, *operands):
    return pl.pallas_call(
        make_outer_kernel(first_round),
        out_shape=(shaped(18, 3, 3, 8, 128), shaped(16, 3, 8, 128)),
        in_specs=[VMEM] * 11,
        out_specs=(VMEM, VMEM),
        scratch_shapes=[pltpu.VMEM((2, 4, 5, 3, 8, 128), F32)],
        input_output_aliases={10: 0},
        compiler_params=PARAMS,
        name="outer",
    )(*operands)


def make_sketch_kernel(kinds, earlier):
    def kernel(rows, signs, *refs):
        count = len(kinds)
        blocks, out, both = refs[:count], refs[-2], refs[-1]
        base = 0
        for part in refs[count : count + earlier]:
            size = part.shape[0]
            out[pl.ds(base, size), :] = part[...]
            base += size
        half = tile_iota(0) < 4
        lane = tile_iota(1)

        def spread(y, carry):
            for n, kind in enumerate(kinds):
                for c in range(3):
                    tile = blocks[n][y + 1, 1, c] if kind else blocks[n][y, c]
                    both[n, y * 3 + c] = tile
                    both[n, 48 + y * 3 + c] = pltpu.roll(tile, 4, 0)
            return carry

        lax.fori_loop(0, 16, spread, 0)

        def pick(group, sums):
            sums = list(sums)
            for k in range(8):
                j = group * 8 + k
                first = lax.shift_right_logical(rows[j], 7)
                second = lax.shift_right_logical(rows[64 + j], 7)
                second = jnp.where(second < 48, second + 48, second - 48)
                sign = signs[j]
                for n in range(count):
                    tile = jnp.where(half, both[n, first], both[n, second]) * sign
                    sums[n] = jnp.where(lane == j, jnp.sum(tile, axis=1, keepdims=True), sums[n])
            return tuple(sums)

        sums = lax.fori_loop(0, 8, pick, tuple(jnp.zeros((8, 128), F32) for _ in kinds))
        for n in range(count):
            folded = jnp.where(lane < 64, sums[n], pltpu.roll(pltpu.roll(sums[n], 64, 1), 4, 0))
            out[pl.ds(base + n * 4, 4), :] = folded[0:4]

    return kernel


def sketch(kinds, rows, signs, blocks, earlier=()):
    size = 4 * len(kinds) + sum(part.shape[0] for part in earlier)
    return pl.pallas_call(
        make_sketch_kernel(kinds, len(earlier)),
        out_shape=shaped(size, 128),
        in_specs=[SMEM] + [VMEM] * (1 + len(kinds) + len(earlier)),
        out_specs=VMEM,
        scratch_shapes=[pltpu.VMEM((len(kinds), 96, 8, 128), F32)],
        compiler_params=PARAMS,
        name="sketch",
    )(rows, signs, *blocks, *earlier)


def dot(a, b):
    return jnp.dot(a, b, precision=lax.Precision.HIGHEST, preferred_element_type=F32)


def sum_lanes(a):
    return jnp.sum(a, axis=1, keepdims=True)


def fit(table, shift, reach):
    lane = tile_iota(1)
    row = tile_iota(0)
    live = row < 4
    raise_by = jnp.where(lane < 4, reach, 0.5 * reach)
    lower_by = jnp.where(lane < 4, 0.0, 0.5 * reach)

    def move(coords):
        return (
            pltpu.roll(coords * raise_by, 4, 1)
            + shift * coords
            + pltpu.roll(coords * lower_by, 124, 1)
        )

    rhs = jnp.where(live, table[0:8], 0.0)
    norms = jnp.sqrt(sum_lanes(rhs * rhs) + 1e-06)
    basis = rhs / norms
    coords = jnp.where(live & (lane == row), 1.0, 0.0) / norms
    leading = jnp.sum(jnp.where(lane == row, coords, 0.0), axis=0, keepdims=True)
    for k in range(STEPS - 1):
        moved = move(coords)
        image = dot(moved[:, 0:40], table)
        rest, next_coords = image, moved
        for i in range(4):
            weight = sum_lanes(image * basis[i : i + 1])
            rest = rest - weight * basis[i : i + 1]
            next_coords = next_coords - weight * coords[i : i + 1]
        norms = jnp.sqrt(sum_lanes(rest * rest) + 1e-06)
        basis = rest / norms
        coords = next_coords / norms
        leading = leading + jnp.sum(
            jnp.where(live & (lane == row + 4 * (k + 1)), coords, 0.0), axis=0, keepdims=True
        )

    tall_row = lax.broadcasted_iota(jnp.int32, (40, 128), 0)
    tall_lane = lax.broadcasted_iota(jnp.int32, (40, 128), 1)
    wide = shift[0:1]
    part = 0.5 * reach[0:1]
    lower = jnp.concatenate([table[4:8], table[0:36]], axis=0)
    upper = jnp.concatenate([table[4:40], table[0:4]], axis=0)
    vectors = wide * table + part * (lower + upper)
    rhs_rows = jnp.concatenate([rhs, rhs, rhs, rhs, rhs], axis=0)
    vectors = jnp.where(tall_row < 32, vectors, rhs_rows)

    combos = jnp.where(tall_row == tall_lane, 1.0, 0.0)
    found = jnp.zeros((8, 128), F32)
    sizes = jnp.zeros((1, 128), F32)
    for j in range(4 * STEPS):
        pivot = vectors[j : j + 1]
        products = sum_lanes(vectors * pivot)
        size = products[j : j + 1]
        ratio = products / (size + 1e-37)
        found = jnp.where(lane == j, ratio[32:40], found)
        sizes = jnp.where(lane[0:1] == j, size, sizes)
        later = jnp.where(tall_row > j, ratio, 0.0)
        vectors = vectors - later * pivot
        combos = combos - later * combos[j : j + 1]
    scaled = sizes * leading * leading
    found = jnp.where(live, found * (scaled / (scaled + 1e-06)), 0.0)
    return move, dot(found[:, 0:40], combos)


def finish_kernel(table, interval, first, m0, l0, m1, l1, m2, l2, m3, l3, iterate, remainder, mix):
    shift, reach = interval[0], interval[1]
    lane = tile_iota(1)
    row = tile_iota(0)
    sub = row % 4
    total = table[0]
    for n in range(1, table.shape[0]):
        total = total + table[n]
    tall = jnp.concatenate([total, jnp.zeros((4, 128), F32)], axis=0)
    move, weights = fit(tall, shift, reach)
    weights = jnp.where(lane < 4 * STEPS, weights, 0.0)
    images = move(weights)
    weights = jnp.where(row < 4, weights, pltpu.roll(weights, 4, 0))
    images = jnp.where(row < 4, images, pltpu.roll(images, 4, 0))
    for k in range(STEPS + 1):
        for r in range(4):
            spot = lane == 4 * k + (sub + r) % 4
            if k < STEPS:
                mix[0, k * 4 + r] = jnp.broadcast_to(
                    sum_lanes(jnp.where(spot, weights, 0.0)), (8, 128)
                )
            mix[1, k * 4 + r] = jnp.broadcast_to(
                sum_lanes(jnp.where(spot, images, 0.0)), (8, 128)
            )

    refs = [(first, 0), (m0, 1), (l0, 0), (m1, 1), (l1, 0), (m2, 1), (l2, 0), (m3, 1), (l3, 0)]

    def one_row(y, carry):
        for c in range(3):
            total = None
            image = first[y, c]
            for k, (ref, kind) in enumerate(refs):
                tile = ref[y + 1, 1, c] if kind else ref[y, c]
                for r in range(4):
                    if r:
                        turned = jnp.where(
                            sub < 4 - r, pltpu.roll(tile, 8 - r, 0), pltpu.roll(tile, 4 - r, 0)
                        )
                    else:
                        turned = tile
                    if k < STEPS:
                        part = mix[0, k * 4 + r] * turned
                        total = part if total is None else total + part
                    image = image - mix[1, k * 4 + r] * turned
            for x in range(2):
                iterate[x, y, c] = total[4 * x : 4 * x + 4]
                remainder[x, y, c] = image[4 * x : 4 * x + 4]
        return carry

    lax.fori_loop(0, 16, one_row, 0)


def finish(table, interval, blocks):
    return pl.pallas_call(
        finish_kernel,
        out_shape=(shaped(2, 16, 3, 4, 128), shaped(2, 16, 3, 4, 128)),
        in_specs=[VMEM] * 11,
        out_specs=(VMEM, VMEM),
        scratch_shapes=[pltpu.VMEM((2, 36, 8, 128), F32)],
        compiler_params=PARAMS,
        name="finish",
    )(table, interval, *blocks)


def neighbours(low, high, axis):
    count = lax.axis_size(axis)
    after = lax.ppermute(low, axis, [(i + 1, i) for i in range(count - 1)])
    before = lax.ppermute(high, axis, [(i, i + 1) for i in range(count - 1)])
    return before, after


def fold(copies, count):
    def kernel(parts, out):
        total = parts[0]
        for n in range(1, copies.shape[0]):
            total = total + parts[n]
        for n in range(count):
            out[n] = total

    return pl.pallas_call(
        kernel,
        out_shape=shaped(count, *copies.shape[1:]),
        in_specs=[VMEM],
        out_specs=VMEM,
        compiler_params=PARAMS,
        name="fold",
    )(copies)


def cycle(right_side, stencil, class_scale, material, boundary, sign_bits, sample_rows):
    rows = sample_rows.reshape(-1)
    own, low, high, masked = prepare(
        class_scale, right_side.transpose(0, 1, 3, 2, 4), material, boundary
    )
    blocks = [own]
    sketches = []

    def spread(planes, count):
        pairs = planes.reshape(2, 2, count, 128).transpose(2, 0, 1, 3)
        return jnp.broadcast_to(pairs[:, :, :, None], (count, 2, 2, 4, 128)).reshape(
            count, 2, 8, 128
        )

    for turn in range(STEPS // 2):
        first_round = turn == 0
        if first_round:
            low, high = neighbours(low, high, GX)
            coef, interval, signs = setup(
                stencil.reshape(-1), class_scale, rows, sign_bits.transpose(0, 2, 1, 3)
            )
        else:
            left, right = neighbours(own, own, GX)
        part = sketch((0,) if first_round else (1, 0), rows, signs, blocks[-2:])
        started = inner(coef, own)
        if first_round:
            low, high, part, started, masked = lax.optimization_barrier(
                (low, high, part, started, masked)
            )
            left, right = low[:384].reshape(own.shape), high[:384].reshape(own.shape)
            planes = jnp.concatenate([low[None, 384:], masked, high[None, 384:]])
        else:
            left, right, part, started = lax.optimization_barrier((left, right, part, started))
        sketches.append(part)
        bottom = jnp.stack([left[:2], own[:2], right[:2]])
        top = jnp.stack([left[14:], own[14:], right[14:]])
        if first_round:
            flat_y = (3 * 2 * 3 * 8, 128)
            down, up = neighbours(
                jnp.concatenate([bottom.reshape(flat_y), planes[:, 0], planes[:, 0]]),
                jnp.concatenate([top.reshape(flat_y), planes[:, 15], planes[:, 15]]),
                GY,
            )
            scale_mid = spread(planes, 16)
            scale_own = jnp.broadcast_to(
                masked.transpose(1, 0, 2)[:, :, None], (16, 2, 4, 128)
            ).reshape(16, 8, 128)
            before = interval
        else:
            down, up = neighbours(bottom, top, GY)
            before = blocks[-2]
        started = middle(first_round, coef, interval, left, own, right, started, before, scale_mid)
        if first_round:
            down, up, started, scale_own = lax.optimization_barrier((down, up, started, scale_own))
            planes = jnp.concatenate([down[144:148, None], planes, up[144:148, None]], axis=1)
            down, up = down[:144].reshape(bottom.shape), up[:144].reshape(top.shape)
            scale = spread(planes, 18)
        mid, own = outer(
            first_round,
            *(coef, interval, left, own, right, down, up, before, scale, scale_own, started),
        )
        blocks += [mid, own]

    table = lax.psum(sketch((1, 0), rows, signs, blocks[-2:], sketches), "gy_1")
    copies = jnp.broadcast_to(table, (16,) + table.shape)
    copies = lax.all_to_all(copies, ("gx_0", "gy_0"), 0, 0, tiled=True)
    copies = lax.all_to_all(fold(copies, 8), ("gx_1",), 0, 0, tiled=True)
    iterate, remainder = finish(copies, interval, blocks)
    return iterate.transpose(0, 1, 3, 2, 4), remainder.transpose(0, 1, 3, 2, 4)


def solution(mesh):
    split = Mesh(mesh.devices.reshape(4, 8, 4, 2), AXES)
    return jax.shard_map(
        cycle,
        mesh=split,
        in_specs=(
            P(GX, GY, None, None, None),
            P(),
            P(),
            P(GX, GY, None),
            P(GX, GY, None),
            P(GX, GY, None, None),
            P(GX, GY, None),
        ),
        out_specs=(P(GX, GY, None, None, None), P(GX, GY, None, None, None)),
        check_vma=False,
    )
```

time: 181 us -> 144 us (0.80)
  waiting for transfers between devices: 33.7 us -> 6.53 us
  blocking collectives: 16.8 us -> 39.1 us
  other arithmetic: 12.3 us -> 0.1 us
  local copies, waits for them, and re-layouts: 17.2 us -> 6.14 us
  starting transfers between devices: 57.2 us -> 48.2 us
  Pallas kernels: 37.7 us -> 41.6 us
  between operations: 4.61 us -> 1.21 us
    all_to_all x1 -> x2, blocking collectives: 16.8 us -> 35.7 us  [the longest x1 24.9 us: cycle(): copies = lax.all_to_all(copies, ('gx_0', 'gy_0'), 0, 0, tiled=True)]
    all_to_all x1 -> x0, waiting for transfers between devices: 12.9 us -> none  [shards(): table = jnp.sum(lax.all_to_all(copies, axes, 0, 0, tiled=True), axis=0)]
    ppermute x8, waiting for transfers between devices: 12.1 us -> 4.91 us  [neighbours(): after = lax.ppermute(low, axis, [(i + 1, i) for i in range(count - 1)])]
    all_to_all x1 -> x0, starting transfers between devices: 7.08 us -> none  [shards(): table = jnp.sum(lax.all_to_all(copies, axes, 0, 0, tiled=True), axis=0)]
    ppermute x8, waiting for transfers between devices: 8.63 us -> 1.62 us  [neighbours(): before = lax.ppermute(high, axis, [(i, i + 1) for i in range(count - 1)])]
    select_n x4 -> x0, other arithmetic: 5.05 us -> none  [the longest x1 5 us: shards(): jnp.where(boundary == 1, 0.0, material_scale(material, class_scale))]
    pallas_call x11 -> x21, Pallas kernels: 37.7 us -> 41.6 us  [the longest x4 9.67 us: outer(): pl.pallas_call(make_outer_kernel(first_round), out_shape=(shaped(18, 3, 3...]
    gather x3 -> x0, local copies, waits for them, and re-layouts: 3.58 us -> none  [the longest x1 1.5 us: shards(): sign_rows = sign_rows * hadamard_table()[pick_z]]
  transfers between devices with their start and end apart: 17 -> 16, of which waited for: 10 -> 4; matrix products, arithmetic and copies ran while one was open for 5% -> 0% of each run, Pallas kernels for 4% -> 16%
where the time goes in v2:
time: 144 us; the launch traced here: 143 us
  starting transfers between devices  48.2 us (33%)
  Pallas kernels  41.6 us (29%)
  blocking collectives  39.1 us (27%)
  waiting for transfers between devices  6.53 us (5%)
  local copies, waits for them, and re-layouts  6.14 us (4%)
    ppermute x8, starting transfers between devices, neighbours(): before = lax.ppermute(high, axis, [(i, i + 1) for i in range(count - 1)])  33.9 us
    all_to_all x1, blocking collectives, cycle(): copies = lax.all_to_all(copies, ('gx_0', 'gy_0'), 0, 0, tiled=True)  24.9 us
    ppermute x8, starting transfers between devices, neighbours(): after = lax.ppermute(low, axis, [(i + 1, i) for i in range(count - 1)])  14.3 us
    all_to_all x1, blocking collectives, cycle(): copies = lax.all_to_all(fold(copies, 8), ('gx_1',), 0, 0, tiled=True)  10.9 us
    pallas_call x4, Pallas kernels, outer(): pl.pallas_call(make_outer_kernel(first_round), out_shape=(shaped(18, 3, 3...  9.67 us
    pallas_call x4, Pallas kernels, middle(): pl.pallas_call(make_middle_kernel(first_round), out_shape=shaped(18, 3, 3...  8.42 us
    pallas_call x5, Pallas kernels, sketch(): pl.pallas_call(make_sketch_kernel(kinds, len(earlier)), out_shape=shaped(...  7.66 us
    pallas_call x1, Pallas kernels, finish(): pl.pallas_call(finish_kernel, out_shape=(shaped(2, 16, 3, 4, 128), shaped...  6.19 us
  transfers between devices with their start and end apart: 16, of which 4 were waited for; matrix products, arithmetic and copies ran while one was open for 0% of the time, Pallas kernels for 16%

profile of v2, /device:TPU:1, one launch (start us, length us, event | category | flops | bytes accessed | tf_op | source)
XLA Modules:
  0.0 142.9 jit_solution(6087739791280284537)
XLA Ops:
  0.6 0.6 copy-done.7
  1.3 0.9 copy-done.2
  2.2 0.7 copy-done.5
  2.9 0.7 copy-done.6
  3.7 1.0 prepare.1
  4.7 4.4 %collective-permute-start = (f32[400,128]{1,0:T(8,128)S(1)}, f32[400,128]{1,0:T(8,128)S(1)}, u32[]{:S(2)}, u32[]{:S(2)}) collective-permute-start(f32[400,128]{1,0:T(8,128)S(1)} %get-tuple-element.43), channel_id=1, source_target_pairs={{0,8},{8,16},{16,24},{24,32},{32,40},{40,48},{48,56},{56,64},{64,7... | collective-permute-start | bytes 614408 | tf_op jit(solution)/shard_map/ppermute | solution.py:524
  9.0 0.0 copy-start.3
  9.0 1.4 collective-permute-start.1
  10.5 0.1 copy.18
  10.6 0.2 reshape.58.stencil
  10.8 0.0 copy-start.4
  10.8 0.6 copy-done.4
  11.4 3.0 %setup.1 = (f32[243,8,128]{2,1,0:T(8,128)S(1)}, f32[2,8,128]{2,1,0:T(8,128)S(1)}, f32[64,8,128]{2,1,0:T(8,128)S(1)}) custom-call(f32[243]{0:T(256)S(1)} %reshape.58.stencil, f32[8]{0:T(128)S(1)} %copy-done.7, s32[128]{0:T(128)S(1)} %bitcast.97, s32[2,3,16,128]{3,2,1,0:T(8,128)S(1)} %bitcast.96), custom_call_target="tpu_custom_call" | custom-call | tf_op jit(solution)/shard_map/setup/pallas_call | solution.py:127
  14.4 1.5 %sketch.5.refs_2_ = f32[4,128]{1,0:T(4,128)S(1)} custom-call(s32[128]{0:T(128)S(1)} %bitcast.98, f32[64,8,128]{2,1,0:T(8,128)S(1)} %get-tuple-element.40.signs, f32[16,3,8,128]{3,2,1,0:T(8,128)S(1)} %get-tuple-element.45.refs_0_.own.first), custom_call_target="tpu_custom_call" | custom-call | tf_op jit(solution)/shard_map/sketch/pallas_call | solution.py:376
  15.9 1.4 inner.4.part
  17.3 0.0 collective-permute-done
  17.4 0.0 collective-permute-done.1
  17.5 3.3 %collective-permute-start.3 = (f32[152,128]{1,0:T(8,128)S(1)}, f32[152,128]{1,0:T(8,128)S(1)}, u32[]{:S(2)}, u32[]{:S(2)}) collective-permute-start(f32[152,128]{1,0:T(8,128)S(1)} %pad_maximum_fusion.1), channel_id=1, source_target_pairs={{1,0},{2,1},{3,2},{4,3},{5,4},{6,5},{7,6},{9,8},{10,9},{11,10},{12... | collective-permute-start | bytes 233480 | tf_op jit(solution)/shard_map/ppermute | solution.py:523
  20.8 3.0 %collective-permute-start.2 = (f32[152,128]{1,0:T(8,128)S(1)}, f32[152,128]{1,0:T(8,128)S(1)}, u32[]{:S(2)}, u32[]{:S(2)}) collective-permute-start(f32[152,128]{1,0:T(8,128)S(1)} %pad_maximum_fusion), channel_id=1, source_target_pairs={{0,1},{1,2},{2,3},{3,4},{4,5},{5,6},{6,7},{8,9},{9,10},{10,11},{11... | collective-permute-start | bytes 233480 | tf_op jit(solution)/shard_map/ppermute | solution.py:524
  23.9 2.1 %middle.4.started = f32[18,3,3,8,128]{4,3,2,1,0:T(8,128)S(1)} custom-call(f32[243,8,128]{2,1,0:T(8,128)S(1)} %get-tuple-element.41.coef, f32[2,8,128]{2,1,0:T(8,128)S(1)} %get-tuple-element.42.interval.before, f32[16,3,8,128]{3,2,1,0:T(8,128)S(1)} %bitcast.86, f32[16,3,8,128]{3,2,1,0:T(8,128)S(1)} %get-tuple-element.45.refs_0_.own.first, ...), custom_call_target="tpu_custom_call" | custom-call | tf_op jit(solution)/shard_map/middle/pallas_call | solution.py:243
  26.0 0.0 collective-permute-done.3
  26.0 0.0 copy-start.8
  26.0 0.0 collective-permute-done.2
  26.1 0.6 copy-done.8
  26.7 0.7 slice-done
  27.4 2.4 %outer.4 = (f32[18,3,3,8,128]{4,3,2,1,0:T(8,128)S(1)}, f32[16,3,8,128]{3,2,1,0:T(8,128)S(1)}) custom-call(f32[243,8,128]{2,1,0:T(8,128)S(1)} %get-tuple-element.41.coef, f32[2,8,128]{2,1,0:T(8,128)S(1)} %get-tuple-element.42.interval.before, f32[16,3,8,128]{3,2,1,0:T(8,128)S(1)} %bitcast.87, ...), custom_call_target="tpu_custom_call", output_to_operand_aliasing={{0}: (10, {})} | custom-call | tf_op jit(solution)/shard_map/outer/pallas_call | solution.py:319
  29.8 1.3 collective-permute-start.5
  31.1 4.5 %collective-permute-start.4 = (f32[16,3,8,128]{3,2,1,0:T(8,128)S(1)}, f32[16,3,8,128]{3,2,1,0:T(8,128)S(1)}, u32[]{:S(2)}, u32[]{:S(2)}) collective-permute-start(f32[16,3,8,128]{3,2,1,0:T(8,128)S(1)} %get-tuple-element.55.refs_1_.own.l0), channel_id=1, source_target_pairs={{0,8},{8,16},{16,24},{24,32},{32,40},{40,48},{48,56},{56,64},{64,7... | collective-permute-start | bytes 589832 | tf_op jit(solution)/shard_map/ppermute | solution.py:524
  35.6 1.4 inner.5.part
  37.0 1.5 %sketch.6.refs_3_ = f32[8,128]{1,0:T(8,128)S(1)} custom-call(s32[128]{0:T(128)S(1)} %bitcast.99, f32[64,8,128]{2,1,0:T(8,128)S(1)} %get-tuple-element.40.signs, f32[18,3,3,8,128]{4,3,2,1,0:T(8,128)S(1)} %get-tuple-element.56.refs_0_.before.m0, f32[16,3,8,128]{3,2,1,0:T(8,128)S(1)} %get-tuple-element.55.refs_1_.own.l0), custom_call_target="tpu_custom_call" | custom-call | tf_op jit(solution)/shard_map/sketch/pallas_call | solution.py:376
  38.6 1.6 %collective-permute-done.4.left = f32[16,3,8,128]{3,2,1,0:T(8,128)S(1)} collective-permute-done((f32[16,3,8,128]{3,2,1,0:T(8,128)S(1)}, f32[16,3,8,128]{3,2,1,0:T(8,128)S(1)}, u32[]{:S(2)}, u32[]{:S(2)}) %collective-permute-start.4) | collective-permute-done | bytes 196640 | tf_op jit(solution)/shard_map/ppermute | solution.py:524
  40.2 3.5 %collective-permute-start.6 = (f32[3,2,3,8,128]{4,3,2,1,0:T(8,128)S(1)}, f32[3,2,3,8,128]{4,3,2,1,0:T(8,128)S(1)}, u32[]{:S(2)}, u32[]{:S(2)}) collective-permute-start(f32[3,2,3,8,128]{4,3,2,1,0:T(8,128)S(1)} %pad_maximum_fusion.4), channel_id=1, source_target_pairs={{0,1},{1,2},{2,3},{3,4},{4,5},{5,6},{6,7},{8,9},{9,10},{10,11},{11... | collective-permute-start | bytes 221192 | tf_op jit(solution)/shard_map/ppermute | solution.py:524
  43.8 1.9 %collective-permute-start.7 = (f32[3,2,3,8,128]{4,3,2,1,0:T(8,128)S(1)}, f32[3,2,3,8,128]{4,3,2,1,0:T(8,128)S(1)}, u32[]{:S(2)}, u32[]{:S(2)}) collective-permute-start(f32[3,2,3,8,128]{4,3,2,1,0:T(8,128)S(1)} %pad_maximum_fusion.5), channel_id=1, source_target_pairs={{1,0},{2,1},{3,2},{4,3},{5,4},{6,5},{7,6},{9,8},{10,9},{11,10},{12... | collective-permute-start | bytes 221192 | tf_op jit(solution)/shard_map/ppermute | solution.py:523
  45.7 2.1 %middle.5.started = f32[18,3,3,8,128]{4,3,2,1,0:T(8,128)S(1)} custom-call(f32[243,8,128]{2,1,0:T(8,128)S(1)} %get-tuple-element.41.coef, f32[2,8,128]{2,1,0:T(8,128)S(1)} %get-tuple-element.42.interval.before, f32[16,3,8,128]{3,2,1,0:T(8,128)S(1)} %collective-permute-done.4.left, f32[16,3,8,128]{3,2,1,0:T(8,128)S(1)} %get-tuple-element.55.refs_1_.own.l0, ...), custom_call_target="tpu_custom_call" | custom-call | tf_op jit(solution)/shard_map/middle/pallas_call | solution.py:243
  47.8 0.0 collective-permute-done.6.down
  47.8 1.6 %collective-permute-done.7.up = f32[3,2,3,8,128]{4,3,2,1,0:T(8,128)S(1)} collective-permute-done((f32[3,2,3,8,128]{4,3,2,1,0:T(8,128)S(1)}, f32[3,2,3,8,128]{4,3,2,1,0:T(8,128)S(1)}, u32[]{:S(2)}, u32[]{:S(2)}) %collective-permute-start.7) | collective-permute-done | bytes 73760 | tf_op jit(solution)/shard_map/ppermute | solution.py:523
  49.4 2.5 %outer.5 = (f32[18,3,3,8,128]{4,3,2,1,0:T(8,128)S(1)}, f32[16,3,8,128]{3,2,1,0:T(8,128)S(1)}) custom-call(f32[243,8,128]{2,1,0:T(8,128)S(1)} %get-tuple-element.41.coef, f32[2,8,128]{2,1,0:T(8,128)S(1)} %get-tuple-element.42.interval.before, f32[16,3,8,128]{3,2,1,0:T(8,128)S(1)} %collective-permute-done.4.left, ...), custom_call_target="tpu_custom_call", output_to_operand_aliasing={{0}: (10, {})} | custom-call | tf_op jit(solution)/shard_map/outer/pallas_call | solution.py:319
  51.9 1.3 collective-permute-start.9
  53.2 5.1 %collective-permute-start.8 = (f32[16,3,8,128]{3,2,1,0:T(8,128)S(1)}, f32[16,3,8,128]{3,2,1,0:T(8,128)S(1)}, u32[]{:S(2)}, u32[]{:S(2)}) collective-permute-start(f32[16,3,8,128]{3,2,1,0:T(8,128)S(1)} %get-tuple-element.60.refs_1_.own.l1), channel_id=1, source_target_pairs={{0,8},{8,16},{16,24},{24,32},{32,40},{40,48},{48,56},{56,64},{64,7... | collective-permute-start | bytes 589832 | tf_op jit(solution)/shard_map/ppermute | solution.py:524
  58.3 1.4 inner.6.part
  59.7 1.5 %sketch.7.refs_4_ = f32[8,128]{1,0:T(8,128)S(1)} custom-call(s32[128]{0:T(128)S(1)} %bitcast.100, f32[64,8,128]{2,1,0:T(8,128)S(1)} %get-tuple-element.40.signs, f32[18,3,3,8,128]{4,3,2,1,0:T(8,128)S(1)} %get-tuple-element.61.refs_0_.before.m1, f32[16,3,8,128]{3,2,1,0:T(8,128)S(1)} %get-tuple-element.60.refs_1_.own.l1), custom_call_target="tpu_custom_call" | custom-call | tf_op jit(solution)/shard_map/sketch/pallas_call | solution.py:376
  61.2 0.0 collective-permute-done.9.right
  61.3 4.3 %collective-permute-start.10 = (f32[3,2,3,8,128]{4,3,2,1,0:T(8,128)S(1)}, f32[3,2,3,8,128]{4,3,2,1,0:T(8,128)S(1)}, u32[]{:S(2)}, u32[]{:S(2)}) collective-permute-start(f32[3,2,3,8,128]{4,3,2,1,0:T(8,128)S(1)} %pad_maximum_fusion.6), channel_id=1, source_target_pairs={{0,1},{1,2},{2,3},{3,4},{4,5},{5,6},{6,7},{8,9},{9,10},{10,11},{11... | collective-permute-start | bytes 221192 | tf_op jit(solution)/shard_map/ppermute | solution.py:524
  65.7 1.9 %collective-permute-start.11 = (f32[3,2,3,8,128]{4,3,2,1,0:T(8,128)S(1)}, f32[3,2,3,8,128]{4,3,2,1,0:T(8,128)S(1)}, u32[]{:S(2)}, u32[]{:S(2)}) collective-permute-start(f32[3,2,3,8,128]{4,3,2,1,0:T(8,128)S(1)} %pad_maximum_fusion.7), channel_id=1, source_target_pairs={{1,0},{2,1},{3,2},{4,3},{5,4},{6,5},{7,6},{9,8},{10,9},{11,10},{12... | collective-permute-start | bytes 221192 | tf_op jit(solution)/shard_map/ppermute | solution.py:523
  67.6 2.1 %middle.6.started = f32[18,3,3,8,128]{4,3,2,1,0:T(8,128)S(1)} custom-call(f32[243,8,128]{2,1,0:T(8,128)S(1)} %get-tuple-element.41.coef, f32[2,8,128]{2,1,0:T(8,128)S(1)} %get-tuple-element.42.interval.before, f32[16,3,8,128]{3,2,1,0:T(8,128)S(1)} %collective-permute-done.8.left, f32[16,3,8,128]{3,2,1,0:T(8,128)S(1)} %get-tuple-element.60.refs_1_.own.l1, ...), custom_call_target="tpu_custom_call" | custom-call | tf_op jit(solution)/shard_map/middle/pallas_call | solution.py:243
  69.7 0.0 collective-permute-done.10.down
  69.7 1.6 %collective-permute-done.11.up = f32[3,2,3,8,128]{4,3,2,1,0:T(8,128)S(1)} collective-permute-done((f32[3,2,3,8,128]{4,3,2,1,0:T(8,128)S(1)}, f32[3,2,3,8,128]{4,3,2,1,0:T(8,128)S(1)}, u32[]{:S(2)}, u32[]{:S(2)}) %collective-permute-start.11) | collective-permute-done | bytes 73760 | tf_op jit(solution)/shard_map/ppermute | solution.py:523
  71.3 2.4 %outer.6 = (f32[18,3,3,8,128]{4,3,2,1,0:T(8,128)S(1)}, f32[16,3,8,128]{3,2,1,0:T(8,128)S(1)}) custom-call(f32[243,8,128]{2,1,0:T(8,128)S(1)} %get-tuple-element.41.coef, f32[2,8,128]{2,1,0:T(8,128)S(1)} %get-tuple-element.42.interval.before, f32[16,3,8,128]{3,2,1,0:T(8,128)S(1)} %collective-permute-done.8.left, ...), custom_call_target="tpu_custom_call", output_to_operand_aliasing={{0}: (10, {})} | custom-call | tf_op jit(solution)/shard_map/outer/pallas_call | solution.py:319
  73.7 1.3 collective-permute-start.13
  75.0 5.2 %collective-permute-start.12 = (f32[16,3,8,128]{3,2,1,0:T(8,128)S(1)}, f32[16,3,8,128]{3,2,1,0:T(8,128)S(1)}, u32[]{:S(2)}, u32[]{:S(2)}) collective-permute-start(f32[16,3,8,128]{3,2,1,0:T(8,128)S(1)} %get-tuple-element.65.refs_1_.own.l2), channel_id=1, source_target_pairs={{0,8},{8,16},{16,24},{24,32},{32,40},{40,48},{48,56},{56,64},{64,7... | collective-permute-start | bytes 589832 | tf_op jit(solution)/shard_map/ppermute | solution.py:524
  80.2 1.4 inner.7.part
  81.6 1.5 %sketch.8.refs_5_ = f32[8,128]{1,0:T(8,128)S(1)} custom-call(s32[128]{0:T(128)S(1)} %bitcast.101, f32[64,8,128]{2,1,0:T(8,128)S(1)} %get-tuple-element.40.signs, f32[18,3,3,8,128]{4,3,2,1,0:T(8,128)S(1)} %get-tuple-element.66.refs_0_.before.m2, f32[16,3,8,128]{3,2,1,0:T(8,128)S(1)} %get-tuple-element.65.refs_1_.own.l2), custom_call_target="tpu_custom_call" | custom-call | tf_op jit(solution)/shard_map/sketch/pallas_call | solution.py:376
  83.2 3.8 %collective-permute-start.14 = (f32[3,2,3,8,128]{4,3,2,1,0:T(8,128)S(1)}, f32[3,2,3,8,128]{4,3,2,1,0:T(8,128)S(1)}, u32[]{:S(2)}, u32[]{:S(2)}) collective-permute-start(f32[3,2,3,8,128]{4,3,2,1,0:T(8,128)S(1)} %pad_maximum_fusion.8), channel_id=1, source_target_pairs={{0,1},{1,2},{2,3},{3,4},{4,5},{5,6},{6,7},{8,9},{9,10},{10,11},{11... | collective-permute-start | bytes 221192 | tf_op jit(solution)/shard_map/ppermute | solution.py:524
  87.1 1.9 %collective-permute-start.15 = (f32[3,2,3,8,128]{4,3,2,1,0:T(8,128)S(1)}, f32[3,2,3,8,128]{4,3,2,1,0:T(8,128)S(1)}, u32[]{:S(2)}, u32[]{:S(2)}) collective-permute-start(f32[3,2,3,8,128]{4,3,2,1,0:T(8,128)S(1)} %pad_maximum_fusion.9), channel_id=1, source_target_pairs={{1,0},{2,1},{3,2},{4,3},{5,4},{6,5},{7,6},{9,8},{10,9},{11,10},{12... | collective-permute-start | bytes 221192 | tf_op jit(solution)/shard_map/ppermute | solution.py:523
  89.0 2.1 %middle.7.started = f32[18,3,3,8,128]{4,3,2,1,0:T(8,128)S(1)} custom-call(f32[243,8,128]{2,1,0:T(8,128)S(1)} %get-tuple-element.41.coef, f32[2,8,128]{2,1,0:T(8,128)S(1)} %get-tuple-element.42.interval.before, f32[16,3,8,128]{3,2,1,0:T(8,128)S(1)} %collective-permute-done.12.left, f32[16,3,8,128]{3,2,1,0:T(8,128)S(1)} %get-tuple-element.65.refs_1_.own.l2, ...), custom_call_target="tpu_custom_call" | custom-call | tf_op jit(solution)/shard_map/middle/pallas_call | solution.py:243
  91.2 1.6 %collective-permute-done.15.up = f32[3,2,3,8,128]{4,3,2,1,0:T(8,128)S(1)} collective-permute-done((f32[3,2,3,8,128]{4,3,2,1,0:T(8,128)S(1)}, f32[3,2,3,8,128]{4,3,2,1,0:T(8,128)S(1)}, u32[]{:S(2)}, u32[]{:S(2)}) %collective-permute-start.15) | collective-permute-done | bytes 73760 | tf_op jit(solution)/shard_map/ppermute | solution.py:523
  92.8 2.5 %outer.7 = (f32[18,3,3,8,128]{4,3,2,1,0:T(8,128)S(1)}, f32[16,3,8,128]{3,2,1,0:T(8,128)S(1)}) custom-call(f32[243,8,128]{2,1,0:T(8,128)S(1)} %get-tuple-element.41.coef, f32[2,8,128]{2,1,0:T(8,128)S(1)} %get-tuple-element.42.interval.before, f32[16,3,8,128]{3,2,1,0:T(8,128)S(1)} %collective-permute-done.12.left, ...), custom_call_target="tpu_custom_call", output_to_operand_aliasing={{0}: (10, {})} | custom-call | tf_op jit(solution)/shard_map/outer/pallas_call | solution.py:319
  95.3 1.5 %sketch.9 = f32[36,128]{1,0:T(8,128)S(1)} custom-call(s32[128]{0:T(128)S(1)} %bitcast.102, f32[64,8,128]{2,1,0:T(8,128)S(1)} %get-tuple-element.40.signs, f32[18,3,3,8,128]{4,3,2,1,0:T(8,128)S(1)} %get-tuple-element.70.refs_0_.m3, f32[16,3,8,128]{3,2,1,0:T(8,128)S(1)} %get-tuple-element.71.refs_1_.l3, f32[4,128]{1,0:T(4,128)S(1)} %sketch.5.refs_2_, ...), custom_call_target="tpu_custom_call" | custom-call | tf_op jit(solution)/shard_map/sketch/pallas_call | solution.py:376
  96.8 0.7 copy-done
  97.5 3.4 %psum.7 = f32[36,128]{1,0:T(8,128)S(1)} all-reduce(f32[36,128]{1,0:T(8,128)S(1)} %sketch.9), channel_id=1, replica_groups=mesh['gx_0'=4,'gx_1'=8,'gy_0'=4,'gy_1'=2] {'gy_1'}, use_global_device_ids=true, to_apply=%region_0.0 | all-reduce | flops 4608 | bytes 36864 | tf_op jit(solution)/shard_map/psum | solution.py:609
  100.9 24.9 %all_to_all.10.parts = f32[16,36,128]{2,1,0:T(8,128)S(1)} all-to-all(f32[16,36,128]{2,1,0:T(8,128)S(1)} %broadcast_in_dim.34), channel_id=1, replica_groups=mesh['gx_0'=4,'gx_1'=8,'gy_0'=4,'gy_1'=2] {'gx_0','gy_0'}, dimensions={0} | all-to-all | bytes 589824 | tf_op jit(solution)/shard_map/all_to_all | solution.py:611
  125.8 0.0 copy-start.1
  125.8 10.9 %all_to_all.11.table = f32[8,36,128]{2,1,0:T(8,128)S(1)} all-to-all(f32[8,36,128]{2,1,0:T(8,128)S(1)} %fold.1), channel_id=1, replica_groups=mesh['gx_0'=4,'gx_1'=8,'gy_0'=4,'gy_1'=2] {'gx_1'}, dimensions={0} | all-to-all | bytes 294912 | tf_op jit(solution)/shard_map/all_to_all | solution.py:612
  136.7 6.2 %finish.1 = (f32[2,16,3,4,128]{4,3,2,1,0:T(4,128)}, f32[2,16,3,4,128]{4,3,2,1,0:T(4,128)}) custom-call(f32[8,36,128]{2,1,0:T(8,128)S(1)} %all_to_all.11.table, f32[2,8,128]{2,1,0:T(8,128)S(1)} %get-tuple-element.42.interval.before, f32[16,3,8,128]{3,2,1,0:T(8,128)S(1)} %get-tuple-element.45.refs_0_.own.first, ...), custom_call_target="tpu_custom_call" | custom-call | tf_op jit(solution)/shard_map/finish/pallas_call | solution.py:510
  (53 shorter events, 0.4 us)
Async XLA Ops:
  0.6 0.7 copy-start.7
  1.3 0.9 copy-start.2
  2.2 0.7 copy-start.5
  2.9 0.7 copy-start.6
  3.7 6.8 %copy-start.9 = (f32[27,3,3]{0,2,1:T(4,128)S(1)}, f32[27,3,3]{0,2,1:T(4,128)}, u32[]{:S(2)}) copy-start(f32[27,3,3]{0,2,1:T(4,128)} %param.8) | copy-start | bytes 2920
  4.7 12.7 %collective-permute-start = (f32[400,128]{1,0:T(8,128)S(1)}, f32[400,128]{1,0:T(8,128)S(1)}, u32[]{:S(2)}, u32[]{:S(2)}) collective-permute-start(f32[400,128]{1,0:T(8,128)S(1)} %get-tuple-element.43), channel_id=1, source_target_pairs={{0,8},{8,16},{16,24},{24,32},{32,40},{40,48},{48,56},{56,64},{64,7... | collective-permute-start | bytes 614408 | tf_op jit(solution)/shard_map/ppermute | solution.py:524
  9.0 1.8 %copy-start.3 = (s32[2,16,3,128]{3,1,2,0:T(8,128)S(1)}, s32[2,16,3,128]{3,1,2,0:T(8,128)}, u32[]{:S(2)}) copy-start(s32[2,16,3,128]{3,1,2,0:T(8,128)} %param.12) | copy-start | bytes 147460
  9.0 8.3 %collective-permute-start.1 = (f32[400,128]{1,0:T(8,128)S(1)}, f32[400,128]{1,0:T(8,128)S(1)}, u32[]{:S(2)}, u32[]{:S(2)}) collective-permute-start(f32[400,128]{1,0:T(8,128)S(1)} %get-tuple-element.44), channel_id=1, source_target_pairs={{8,0},{16,8},{24,16},{32,24},{40,32},{48,40},{56,48},{64,56},{72,6... | collective-permute-start | bytes 614408 | tf_op jit(solution)/shard_map/ppermute | solution.py:523
  10.8 0.7 copy-start.4
  17.5 8.6 %collective-permute-start.3 = (f32[152,128]{1,0:T(8,128)S(1)}, f32[152,128]{1,0:T(8,128)S(1)}, u32[]{:S(2)}, u32[]{:S(2)}) collective-permute-start(f32[152,128]{1,0:T(8,128)S(1)} %pad_maximum_fusion.1), channel_id=1, source_target_pairs={{1,0},{2,1},{3,2},{4,3},{5,4},{6,5},{7,6},{9,8},{10,9},{11,10},{12... | collective-permute-start | bytes 233480 | tf_op jit(solution)/shard_map/ppermute | solution.py:523
  20.8 5.3 %collective-permute-start.2 = (f32[152,128]{1,0:T(8,128)S(1)}, f32[152,128]{1,0:T(8,128)S(1)}, u32[]{:S(2)}, u32[]{:S(2)}) collective-permute-start(f32[152,128]{1,0:T(8,128)S(1)} %pad_maximum_fusion), channel_id=1, source_target_pairs={{0,1},{1,2},{2,3},{3,4},{4,5},{5,6},{6,7},{8,9},{9,10},{10,11},{11... | collective-permute-start | bytes 233480 | tf_op jit(solution)/shard_map/ppermute | solution.py:524
  26.0 0.6 copy-start.8
  26.7 0.7 slice-start
  29.8 8.8 %collective-permute-start.5 = (f32[16,3,8,128]{3,2,1,0:T(8,128)S(1)}, f32[16,3,8,128]{3,2,1,0:T(8,128)S(1)}, u32[]{:S(2)}, u32[]{:S(2)}) collective-permute-start(f32[16,3,8,128]{3,2,1,0:T(8,128)S(1)} %get-tuple-element.55.refs_1_.own.l0), channel_id=1, source_target_pairs={{8,0},{16,8},{24,16},{32,24},{40,32},{48,40},{56,48},{64,56},{72,6... | collective-permute-start | bytes 589832 | tf_op jit(solution)/shard_map/ppermute | solution.py:523
  31.1 9.1 %collective-permute-start.4 = (f32[16,3,8,128]{3,2,1,0:T(8,128)S(1)}, f32[16,3,8,128]{3,2,1,0:T(8,128)S(1)}, u32[]{:S(2)}, u32[]{:S(2)}) collective-permute-start(f32[16,3,8,128]{3,2,1,0:T(8,128)S(1)} %get-tuple-element.55.refs_1_.own.l0), channel_id=1, source_target_pairs={{0,8},{8,16},{16,24},{24,32},{32,40},{40,48},{48,56},{56,64},{64,7... | collective-permute-start | bytes 589832 | tf_op jit(solution)/shard_map/ppermute | solution.py:524
  40.2 7.6 %collective-permute-start.6 = (f32[3,2,3,8,128]{4,3,2,1,0:T(8,128)S(1)}, f32[3,2,3,8,128]{4,3,2,1,0:T(8,128)S(1)}, u32[]{:S(2)}, u32[]{:S(2)}) collective-permute-start(f32[3,2,3,8,128]{4,3,2,1,0:T(8,128)S(1)} %pad_maximum_fusion.4), channel_id=1, source_target_pairs={{0,1},{1,2},{2,3},{3,4},{4,5},{5,6},{6,7},{8,9},{9,10},{10,11},{11... | collective-permute-start | bytes 221192 | tf_op jit(solution)/shard_map/ppermute | solution.py:524
  43.8 5.7 %collective-permute-start.7 = (f32[3,2,3,8,128]{4,3,2,1,0:T(8,128)S(1)}, f32[3,2,3,8,128]{4,3,2,1,0:T(8,128)S(1)}, u32[]{:S(2)}, u32[]{:S(2)}) collective-permute-start(f32[3,2,3,8,128]{4,3,2,1,0:T(8,128)S(1)} %pad_maximum_fusion.5), channel_id=1, source_target_pairs={{1,0},{2,1},{3,2},{4,3},{5,4},{6,5},{7,6},{9,8},{10,9},{11,10},{12... | collective-permute-start | bytes 221192 | tf_op jit(solution)/shard_map/ppermute | solution.py:523
  51.9 9.3 %collective-permute-start.9 = (f32[16,3,8,128]{3,2,1,0:T(8,128)S(1)}, f32[16,3,8,128]{3,2,1,0:T(8,128)S(1)}, u32[]{:S(2)}, u32[]{:S(2)}) collective-permute-start(f32[16,3,8,128]{3,2,1,0:T(8,128)S(1)} %get-tuple-element.60.refs_1_.own.l1), channel_id=1, source_target_pairs={{8,0},{16,8},{24,16},{32,24},{40,32},{48,40},{56,48},{64,56},{72,6... | collective-permute-start | bytes 589832 | tf_op jit(solution)/shard_map/ppermute | solution.py:523
  53.2 8.1 %collective-permute-start.8 = (f32[16,3,8,128]{3,2,1,0:T(8,128)S(1)}, f32[16,3,8,128]{3,2,1,0:T(8,128)S(1)}, u32[]{:S(2)}, u32[]{:S(2)}) collective-permute-start(f32[16,3,8,128]{3,2,1,0:T(8,128)S(1)} %get-tuple-element.60.refs_1_.own.l1), channel_id=1, source_target_pairs={{0,8},{8,16},{16,24},{24,32},{32,40},{40,48},{48,56},{56,64},{64,7... | collective-permute-start | bytes 589832 | tf_op jit(solution)/shard_map/ppermute | solution.py:524
  61.3 8.4 %collective-permute-start.10 = (f32[3,2,3,8,128]{4,3,2,1,0:T(8,128)S(1)}, f32[3,2,3,8,128]{4,3,2,1,0:T(8,128)S(1)}, u32[]{:S(2)}, u32[]{:S(2)}) collective-permute-start(f32[3,2,3,8,128]{4,3,2,1,0:T(8,128)S(1)} %pad_maximum_fusion.6), channel_id=1, source_target_pairs={{0,1},{1,2},{2,3},{3,4},{4,5},{5,6},{6,7},{8,9},{9,10},{10,11},{11... | collective-permute-start | bytes 221192 | tf_op jit(solution)/shard_map/ppermute | solution.py:524
  65.7 5.7 %collective-permute-start.11 = (f32[3,2,3,8,128]{4,3,2,1,0:T(8,128)S(1)}, f32[3,2,3,8,128]{4,3,2,1,0:T(8,128)S(1)}, u32[]{:S(2)}, u32[]{:S(2)}) collective-permute-start(f32[3,2,3,8,128]{4,3,2,1,0:T(8,128)S(1)} %pad_maximum_fusion.7), channel_id=1, source_target_pairs={{1,0},{2,1},{3,2},{4,3},{5,4},{6,5},{7,6},{9,8},{10,9},{11,10},{12... | collective-permute-start | bytes 221192 | tf_op jit(solution)/shard_map/ppermute | solution.py:523
  73.7 9.5 %collective-permute-start.13 = (f32[16,3,8,128]{3,2,1,0:T(8,128)S(1)}, f32[16,3,8,128]{3,2,1,0:T(8,128)S(1)}, u32[]{:S(2)}, u32[]{:S(2)}) collective-permute-start(f32[16,3,8,128]{3,2,1,0:T(8,128)S(1)} %get-tuple-element.65.refs_1_.own.l2), channel_id=1, source_target_pairs={{8,0},{16,8},{24,16},{32,24},{40,32},{48,40},{56,48},{64,56},{72,6... | collective-permute-start | bytes 589832 | tf_op jit(solution)/shard_map/ppermute | solution.py:523
  75.0 8.2 %collective-permute-start.12 = (f32[16,3,8,128]{3,2,1,0:T(8,128)S(1)}, f32[16,3,8,128]{3,2,1,0:T(8,128)S(1)}, u32[]{:S(2)}, u32[]{:S(2)}) collective-permute-start(f32[16,3,8,128]{3,2,1,0:T(8,128)S(1)} %get-tuple-element.65.refs_1_.own.l2), channel_id=1, source_target_pairs={{0,8},{8,16},{16,24},{24,32},{32,40},{40,48},{48,56},{56,64},{64,7... | collective-permute-start | bytes 589832 | tf_op jit(solution)/shard_map/ppermute | solution.py:524
  83.2 7.9 %collective-permute-start.14 = (f32[3,2,3,8,128]{4,3,2,1,0:T(8,128)S(1)}, f32[3,2,3,8,128]{4,3,2,1,0:T(8,128)S(1)}, u32[]{:S(2)}, u32[]{:S(2)}) collective-permute-start(f32[3,2,3,8,128]{4,3,2,1,0:T(8,128)S(1)} %pad_maximum_fusion.8), channel_id=1, source_target_pairs={{0,1},{1,2},{2,3},{3,4},{4,5},{5,6},{6,7},{8,9},{9,10},{10,11},{11... | collective-permute-start | bytes 221192 | tf_op jit(solution)/shard_map/ppermute | solution.py:524
  87.1 5.7 %collective-permute-start.15 = (f32[3,2,3,8,128]{4,3,2,1,0:T(8,128)S(1)}, f32[3,2,3,8,128]{4,3,2,1,0:T(8,128)S(1)}, u32[]{:S(2)}, u32[]{:S(2)}) collective-permute-start(f32[3,2,3,8,128]{4,3,2,1,0:T(8,128)S(1)} %pad_maximum_fusion.9), channel_id=1, source_target_pairs={{1,0},{2,1},{3,2},{4,3},{5,4},{6,5},{7,6},{9,8},{10,9},{11,10},{12... | collective-permute-start | bytes 221192 | tf_op jit(solution)/shard_map/ppermute | solution.py:523
  96.8 0.7 copy-start
  125.8 10.9 %copy-start.1 = (f32[16,3,8,128]{3,2,1,0:T(8,128)S(1)}, f32[16,3,8,128]{3,2,1,0:T(8,128)}, u32[]{:S(2)}) copy-start(f32[16,3,8,128]{3,2,1,0:T(8,128)} %copy-done) | copy-start | bytes 589828

commit v3 on v2

--- a/solution.py
+++ b/solution.py
@@ -28,7 +28,7 @@
     return jax.ShapeDtypeStruct(shape, F32)
 
 
-def prepare_kernel(class_scale, far_side, far_material, far_boundary, own, low, high, masked, *scratch):
+def prepare_kernel(class_scale, parity, far_side, far_material, far_boundary, own, first, second, masked, *scratch):
     right_side, material, boundary, sems = scratch
     copies = [
         pltpu.make_async_copy(far_material, material, sems.at[0]),
@@ -39,16 +39,20 @@
         copy.start()
     copies[0].wait()
     copies[1].wait()
-    for x in range(2):
-        for half in range(2):
-            rows = pl.ds(half * 8, 8)
+    even = parity[0] != 0.0
+    for half in range(2):
+        rows = pl.ds(half * 8, 8)
+        fields = []
+        for x in range(2):
             field = jnp.zeros((8, 128), F32)
             kinds = material[x, rows]
             for number in range(8):
                 field = field + jnp.where(kinds == number, class_scale[number], 0.0)
             field = jnp.where(boundary[x, rows] == 1, 0.0, field)
             masked[x, rows] = field
-            (low, high)[x][pl.ds(384 + half * 8, 8)] = field
+            fields.append(field)
+        first[pl.ds(384 + half * 8, 8)] = jnp.where(even, fields[1], fields[0])
+        second[pl.ds(384 + half * 8, 8)] = jnp.where(even, fields[0], fields[1])
 
     copies[2].wait()
 
@@ -56,18 +60,18 @@
         for c in range(3):
             tile = jnp.concatenate([right_side[0, y, c], right_side[1, y, c]], axis=0)
             own[y, c] = tile
-            low[pl.ds((y * 3 + c) * 8, 8)] = tile
-            high[pl.ds((y * 3 + c) * 8, 8)] = tile
+            first[pl.ds((y * 3 + c) * 8, 8)] = tile
+            second[pl.ds((y * 3 + c) * 8, 8)] = tile
         return carry
 
     lax.fori_loop(0, 16, one_row, 0)
 
 
-def prepare(class_scale, right_side, material, boundary):
+def prepare(class_scale, parity, *operands):
     return pl.pallas_call(
         prepare_kernel,
         out_shape=(shaped(16, 3, 8, 128), shaped(400, 128), shaped(400, 128), shaped(2, 16, 128)),
-        in_specs=[SMEM, FAR, FAR, FAR],
+        in_specs=[SMEM, VMEM, FAR, FAR, FAR],
         out_specs=(VMEM,) * 4,
         scratch_shapes=[
             pltpu.VMEM((2, 16, 3, 4, 128), F32),
@@ -77,16 +81,18 @@
         ],
         compiler_params=PARAMS,
         name="prepare",
-    )(class_scale, right_side, material, boundary)
-
-
-def setup_kernel(stencil, class_scale, rows, sign_bits, coef, interval, signs):
+    )(class_scale, parity, *[pltpu.with_memory_space_constraint(x, pltpu.HBM) for x in operands])
+
+
+def setup_kernel(stencil, class_scale, coef, interval):
     def fill(n, total):
-        tile = jnp.full((8, 128), stencil[n])
-        coef[n] = tile
-        return total + tile * tile
-
-    total = lax.fori_loop(0, 243, fill, jnp.zeros((8, 128), F32))
+        for k in range(9):
+            tile = jnp.full((8, 128), stencil[n * 9 + k])
+            coef[n * 9 + k] = tile
+            total = total + tile * tile
+        return total
+
+    total = lax.fori_loop(0, 27, fill, jnp.zeros((8, 128), F32))
     centre = [jnp.full((8, 128), stencil[13 * 9 + n]) for n in (0, 4, 8)]
     middle = (centre[0] + centre[1] + centre[2]) / 3.0
     for tile in centre:
@@ -102,6 +108,19 @@
     interval[0] = shift
     interval[1] = jnp.maximum(0.5 * (top - bottom), 0.05 * shift)
 
+
+def setup(stencil, class_scale):
+    return pl.pallas_call(
+        setup_kernel,
+        out_shape=(shaped(243, 8, 128), shaped(2, 8, 128)),
+        in_specs=[SMEM, SMEM],
+        out_specs=(VMEM,) * 2,
+        compiler_params=PARAMS,
+        name="setup",
+    )(stencil, class_scale)
+
+
+def signs_kernel(rows, sign_bits, signs):
     lanes = lax.broadcasted_iota(jnp.int32, (1, 128), 1)
     size = 1.0 / math.sqrt(128.0)
 
@@ -120,18 +139,18 @@
             signs[n, pl.ds(4 * part, 4), :] = jnp.broadcast_to(row, (4, 128))
         return carry
 
-    lax.fori_loop(0, 64, sample, 0, unroll=4)
-
-
-def setup(stencil, class_scale, rows, sign_bits):
-    return pl.pallas_call(
-        setup_kernel,
-        out_shape=(shaped(243, 8, 128), shaped(2, 8, 128), shaped(64, 8, 128)),
-        in_specs=[SMEM, SMEM, SMEM, VMEM],
-        out_specs=(VMEM,) * 3,
-        compiler_params=PARAMS,
-        name="setup",
-    )(stencil, class_scale, rows, sign_bits)
+    lax.fori_loop(0, 64, sample, 0, unroll=8)
+
+
+def sample_signs(rows, sign_bits):
+    return pl.pallas_call(
+        signs_kernel,
+        out_shape=shaped(64, 8, 128),
+        in_specs=[SMEM, VMEM],
+        out_specs=VMEM,
+        compiler_params=PARAMS,
+        name="signs",
+    )(rows, sign_bits)
 
 
 def stencil_rows(coef, component, rows, terms):
@@ -179,62 +198,112 @@
 SEVEN = 7
 
 
-def inner_kernel(coef, own, part):
+def inner_kernel(coef, own, part, turned):
+    def turn_rows(y, carry):
+        for c in range(3):
+            turned[y, c] = pltpu.roll(own[y, c], 4, 0)
+        return carry
+
+    lax.fori_loop(0, 16, turn_rows, 0)
+
     def body(i, carry):
-        component, first, side = i % 3, i // 3 % 2 * SEVEN, i // 6
-        terms = [(2 - 2 * side, lambda r, c: own[first + r, c])]
-        for r, total in enumerate(stencil_rows(coef, component, SEVEN, terms)):
-            part[first + r, side, component] = total
+        component, first = i % 3, i // 3 * SEVEN
+        for n, (dx, source) in enumerate(((2, own), (1, turned), (0, own))):
+            terms = [(dx, lambda r, c, source=source: source[first + r, c])]
+            for r, total in enumerate(stencil_rows(coef, component, SEVEN, terms)):
+                part[first + r, n, component] = total
         return carry
 
-    lax.fori_loop(0, 12, body, 0)
+    lax.fori_loop(0, 6, body, 0)
 
 
 def inner(coef, own):
     return pl.pallas_call(
         inner_kernel,
-        out_shape=shaped(14, 2, 3, 8, 128),
+        out_shape=shaped(14, 3, 3, 8, 128),
         in_specs=[VMEM, VMEM],
         out_specs=VMEM,
+        scratch_shapes=[pltpu.VMEM((16, 3, 8, 128), F32)],
         compiler_params=PARAMS,
         name="inner",
     )(coef, own)
 
 
+def second_step(mid, own, scale_own, value_of, coef, component, first, rows, last):
+    terms = [(dx, lambda r, c, dx=dx: mid[first + r, dx, c]) for dx in range(3)]
+    for r, total in enumerate(stencil_rows(coef, component, rows, terms)):
+        row = first + r
+        value = value_of(scale_own[row], total, mid[row + 1, 1, component])
+        last[row, component] = value - own[row, component]
+
+
+def join(mid, row):
+    half = tile_iota(0) < 4
+    for c in range(3):
+        mid[row, 1, c] = jnp.where(
+            half, pltpu.roll(mid[row, 0, c], 4, 0), pltpu.roll(mid[row, 2, c], 4, 0)
+        )
+
+
 def make_middle_kernel(first_round):
-    def kernel(coef, interval, left, own, right, part, before, scale, mid, work):
+    def kernel(
+        coef, interval, parity, swap_a, own, swap_b, part, before, scale, scale_own, mid, last,
+        left, right, beside,
+    ):
+        half = tile_iota(0) < 4
+        even = parity[0] != 0.0
+
         def fill(y, carry):
             for c in range(3):
-
-                def put(n, tile):
-                    work[y, n, c] = tile
-
-                five_pairs(put, left[y, c], own[y, c], right[y, c])
+                a, b = swap_a[y, c], swap_b[y, c]
+                lower, upper = jnp.where(even, b, a), jnp.where(even, a, b)
+                left[y, c] = lower
+                right[y, c] = upper
+                beside[y, c] = pltpu.roll(jnp.where(half, upper, lower), 4, 0)
             return carry
 
         lax.fori_loop(0, 16, fill, 0)
         value_of = recurrence(interval)
 
         def body(i, carry):
-            component, first, side = i % 3, i // 3 % 2 * SEVEN, i // 6
-            terms = [
-                (side + n, lambda r, c, n=n: work[first + r, 3 * side + n, c]) for n in range(2)
-            ]
-            for r, total in enumerate(stencil_rows(coef, component, SEVEN, terms)):
+            component, first = i % 3, i // 3 * SEVEN
+            sums = []
+            for dx, source in ((0, left), (1, beside), (2, right)):
+                terms = [(dx, lambda r, c, source=source: source[first + r, c])]
+                sums.append(stencil_rows(coef, component, SEVEN, terms))
+            for r in range(SEVEN):
                 row = first + r
-                value = value_of(
-                    scale[row + 1, side],
-                    total + part[row, side, component],
-                    work[row + 1, side * 2 + 1, component],
-                )
-                if first_round:
-                    value = value * 0.5
-                else:
-                    value = value - before[row + 2, side * 2, component]
-                mid[row + 2, side * 2, component] = value
+                near, far = part[row, 1, component], sums[1][r]
+                turned = pltpu.roll(own[row + 1, component], 4, 0)
+                centre = beside[row + 1, component]
+                for side in range(2):
+                    pick = half if side == 0 else jnp.logical_not(half)
+                    total = sums[2 * side][r] + part[row, 2 * side, component]
+                    value = value_of(
+                        scale[row + 1, side],
+                        total + jnp.where(pick, far, near),
+                        jnp.where(pick, centre, turned),
+                    )
+                    if first_round:
+                        value = value * 0.5
+                    else:
+                        value = value - before[row + 2, side * 2, component]
+                    mid[row + 2, side * 2, component] = value
             return carry
 
-        lax.fori_loop(0, 12, body, 0)
+        lax.fori_loop(0, 6, body, 0)
+
+        def join_rows(row, carry):
+            join(mid, row + 2)
+            return carry
+
+        lax.fori_loop(0, 14, join_rows, 0)
+
+        def second(i, carry):
+            second_step(mid, own, scale_own, value_of, coef, i % 3, 2 + i // 3 * 6, 6, last)
+            return carry
+
+        lax.fori_loop(0, 6, second, 0)
 
     return kernel
 
@@ -242,10 +311,10 @@
 def middle(first_round, *operands):
     return pl.pallas_call(
         make_middle_kernel(first_round),
-        out_shape=shaped(18, 3, 3, 8, 128),
-        in_specs=[VMEM] * 8,
-        out_specs=VMEM,
-        scratch_shapes=[pltpu.VMEM((16, 5, 3, 8, 128), F32)],
+        out_shape=(shaped(18, 3, 3, 8, 128), shaped(16, 3, 8, 128)),
+        in_specs=[VMEM] * 10,
+        out_specs=(VMEM, VMEM),
+        scratch_shapes=[pltpu.VMEM((16, 3, 8, 128), F32)] * 3,
         compiler_params=PARAMS,
         name="middle",
     )(*operands)
@@ -253,11 +322,21 @@
 
 def make_outer_kernel(first_round):
     def kernel(
-        coef, interval, left, own, right, down, up, before, scale, scale_own, started, mid, last, work
+        coef, interval, parity, swap_a, own, swap_b, swap_c, swap_d, before, scale, scale_own,
+        scale_far, mid_before, last_before, mid, last, *rest,
     ):
-        del started
-        half = tile_iota(0) < 4
+        del mid_before, last_before
+        work = rest[-1]
         value_of = recurrence(interval)
+        even_x, even_y = parity[0] != 0.0, parity[1] != 0.0
+        edge_scale = rest[-2]
+
+        def message(n, row, c):
+            if not first_round:
+                return swap_c[n, row, c], swap_d[n, row, c]
+            spot = pl.ds(((n * 2 + row) * 3 + c) * 8, 8)
+            return swap_c[spot], swap_d[spot]
+
         for edge in range(2):
             for row in range(4):
                 for c in range(3):
@@ -265,12 +344,32 @@
                     def put(n, tile):
                         work[edge, row, n, c] = tile
 
-                    far = (down, up)[edge]
-                    near = row - 2 + 14 * edge if edge == 0 else row + 14
                     if (row < 2) == (edge == 0):
-                        five_pairs(put, *[far[n, row % 2, c] for n in range(3)])
+                        tiles = []
+                        for n in range(3):
+                            a, b = message(n, row % 2, c)
+                            tiles.append(jnp.where(even_y, a, b) if edge else jnp.where(even_y, b, a))
+                        five_pairs(put, *tiles)
                     else:
-                        five_pairs(put, left[near, c], own[near, c], right[near, c])
+                        near = row - 2 if edge == 0 else row + 14
+                        a, b = swap_a[near, c], swap_b[near, c]
+                        five_pairs(
+                            put, jnp.where(even_x, b, a), own[near, c], jnp.where(even_x, a, b)
+                        )
+            for side in range(2):
+                if first_round:
+                    planes = []
+                    for x in range(2):
+                        spot = pl.ds(144 + 2 * side + x, 1)
+                        a, b = swap_c[spot], swap_d[spot]
+                        row = jnp.where(even_y[0:1], a, b) if edge else jnp.where(even_y[0:1], b, a)
+                        planes.append(jnp.broadcast_to(row, (8, 128)))
+                    far_tile = jnp.where(tile_iota(0) < 4, planes[0], planes[1])
+                    rest[0][edge, side] = far_tile
+                else:
+                    far_tile = scale_far[edge, side]
+                edge_scale[edge, edge, side] = far_tile
+                edge_scale[edge, 1 - edge, side] = scale[15 * edge, side]
 
         def edges(i, carry):
             component, edge = i % 3, i // 3
@@ -281,7 +380,7 @@
                 for r, total in enumerate(stencil_rows(coef, component, 2, terms)):
                     row = edge * 16 + r
                     value = value_of(
-                        scale[row, side], total, work[edge, r + 1, side * 2 + 1, component]
+                        edge_scale[edge, r, side], total, work[edge, r + 1, side * 2 + 1, component]
                     )
                     if first_round:
                         value = value * 0.5
@@ -291,38 +390,30 @@
             return carry
 
         lax.fori_loop(0, 6, edges, 0)
-
-        def join(row, carry):
-            for c in range(3):
-                mid[row, 1, c] = jnp.where(
-                    half, pltpu.roll(mid[row, 0, c], 4, 0), pltpu.roll(mid[row, 2, c], 4, 0)
-                )
+        for row in (0, 1, 16, 17):
+            join(mid, row)
+
+        def second(i, carry):
+            second_step(mid, own, scale_own, value_of, coef, i % 3, i // 3 * 14, 2, last)
             return carry
 
-        lax.fori_loop(0, 18, join, 0)
-
-        def second(i, carry):
-            component, first = i % 3, i // 3 * 8
-            terms = [(dx, lambda r, c, dx=dx: mid[first + r, dx, c]) for dx in range(3)]
-            for r, total in enumerate(stencil_rows(coef, component, 8, terms)):
-                row = first + r
-                value = value_of(scale_own[row], total, mid[row + 1, 1, component])
-                last[row, component] = value - own[row, component]
-            return carry
-
         lax.fori_loop(0, 6, second, 0)
 
     return kernel
 
 
 def outer(first_round, *operands):
+    far = (shaped(2, 2, 8, 128),) if first_round else ()
     return pl.pallas_call(
         make_outer_kernel(first_round),
-        out_shape=(shaped(18, 3, 3, 8, 128), shaped(16, 3, 8, 128)),
-        in_specs=[VMEM] * 11,
-        out_specs=(VMEM, VMEM),
-        scratch_shapes=[pltpu.VMEM((2, 4, 5, 3, 8, 128), F32)],
-        input_output_aliases={10: 0},
+        out_shape=(shaped(18, 3, 3, 8, 128), shaped(16, 3, 8, 128), *far),
+        in_specs=[VMEM] * 14,
+        out_specs=(VMEM,) * (2 + len(far)),
+        scratch_shapes=[
+            pltpu.VMEM((2, 2, 2, 8, 128), F32),
+            pltpu.VMEM((2, 4, 5, 3, 8, 128), F32),
+        ],
+        input_output_aliases={12: 0, 13: 1},
         compiler_params=PARAMS,
         name="outer",
     )(*operands)
@@ -350,20 +441,15 @@
 
         lax.fori_loop(0, 16, spread, 0)
 
-        def pick(group, sums):
-            sums = list(sums)
-            for k in range(8):
-                j = group * 8 + k
-                first = lax.shift_right_logical(rows[j], 7)
-                second = lax.shift_right_logical(rows[64 + j], 7)
-                second = jnp.where(second < 48, second + 48, second - 48)
-                sign = signs[j]
-                for n in range(count):
-                    tile = jnp.where(half, both[n, first], both[n, second]) * sign
-                    sums[n] = jnp.where(lane == j, jnp.sum(tile, axis=1, keepdims=True), sums[n])
-            return tuple(sums)
-
-        sums = lax.fori_loop(0, 8, pick, tuple(jnp.zeros((8, 128), F32) for _ in kinds))
+        sums = [jnp.zeros((8, 128), F32)] * count
+        for j in range(64):
+            first = lax.shift_right_logical(rows[j], 7)
+            second = lax.shift_right_logical(rows[64 + j], 7)
+            second = jnp.where(second < 48, second + 48, second - 48)
+            sign = signs[j]
+            for n in range(count):
+                tile = jnp.where(half, both[n, first], both[n, second]) * sign
+                sums[n] = jnp.where(lane == j, jnp.sum(tile, axis=1, keepdims=True), sums[n])
         for n in range(count):
             folded = jnp.where(lane < 64, sums[n], pltpu.roll(pltpu.roll(sums[n], 64, 1), 4, 0))
             out[pl.ds(base + n * 4, 4), :] = folded[0:4]
@@ -518,11 +604,13 @@
     )(table, interval, *blocks)
 
 
-def neighbours(low, high, axis):
+def swap(first, second, axis):
     count = lax.axis_size(axis)
-    after = lax.ppermute(low, axis, [(i + 1, i) for i in range(count - 1)])
-    before = lax.ppermute(high, axis, [(i, i + 1) for i in range(count - 1)])
-    return before, after
+    out = []
+    for start, operand in ((0, first), (1, second)):
+        pairs = [(i + k, i + 1 - k) for i in range(start, count - 1, 2) for k in range(2)]
+        out.append(lax.ppermute(operand, axis, pairs))
+    return out
 
 
 def fold(copies, count):
@@ -545,66 +633,85 @@
 
 def cycle(right_side, stencil, class_scale, material, boundary, sign_bits, sample_rows):
     rows = sample_rows.reshape(-1)
-    own, low, high, masked = prepare(
-        class_scale, right_side.transpose(0, 1, 3, 2, 4), material, boundary
+    flags = [lax.axis_index(axis) % 2 == 0 for axis in (GX, GY)]
+    parity = jnp.stack([jnp.broadcast_to(flag.astype(F32), (8, 128)) for flag in flags])
+    own, first, second, masked = prepare(
+        class_scale, parity, right_side.transpose(0, 1, 3, 2, 4), material, boundary
     )
     blocks = [own]
     sketches = []
 
-    def spread(planes, count):
-        pairs = planes.reshape(2, 2, count, 128).transpose(2, 0, 1, 3)
-        return jnp.broadcast_to(pairs[:, :, :, None], (count, 2, 2, 4, 128)).reshape(
-            count, 2, 8, 128
-        )
-
     for turn in range(STEPS // 2):
         first_round = turn == 0
         if first_round:
-            low, high = neighbours(low, high, GX)
-            coef, interval, signs = setup(
-                stencil.reshape(-1), class_scale, rows, sign_bits.transpose(0, 2, 1, 3)
-            )
+            swap_a, swap_b = swap(first, second, GX)
+            coef, interval = setup(stencil.reshape(-1), class_scale)
         else:
-            left, right = neighbours(own, own, GX)
-        part = sketch((0,) if first_round else (1, 0), rows, signs, blocks[-2:])
+            swap_a, swap_b = swap(own, own, GX)
+        if turn == 1:
+            signs = sample_signs(rows, sign_bits.transpose(0, 2, 1, 3))
+        if not first_round:
+            kinds = (0, 1, 0) if turn == 1 else (1, 0)
+            part = sketch(kinds, rows, signs, blocks[-len(kinds) :])
         started = inner(coef, own)
         if first_round:
-            low, high, part, started, masked = lax.optimization_barrier(
-                (low, high, part, started, masked)
+            swap_a, swap_b, started, masked = lax.optimization_barrier(
+                (swap_a, swap_b, started, masked)
             )
-            left, right = low[:384].reshape(own.shape), high[:384].reshape(own.shape)
-            planes = jnp.concatenate([low[None, 384:], masked, high[None, 384:]])
+            planes = [swap_a[None, 384:], swap_b[None, 384:]]
+            planes = jnp.concatenate(
+                [
+                    jnp.where(flags[0], planes[1], planes[0]),
+                    masked,
+                    jnp.where(flags[0], planes[0], planes[1]),
+                ]
+            )
+            swap_a, swap_b = swap_a[:384].reshape(own.shape), swap_b[:384].reshape(own.shape)
         else:
-            left, right, part, started = lax.optimization_barrier((left, right, part, started))
-        sketches.append(part)
-        bottom = jnp.stack([left[:2], own[:2], right[:2]])
-        top = jnp.stack([left[14:], own[14:], right[14:]])
+            swap_a, swap_b, part, started = lax.optimization_barrier(
+                (swap_a, swap_b, part, started)
+            )
+            sketches.append(part)
+
+        def ends(first):
+            a, b = swap_a[first : first + 2], swap_b[first : first + 2]
+            return jnp.stack(
+                [
+                    jnp.where(flags[0], b, a),
+                    own[first : first + 2],
+                    jnp.where(flags[0], a, b),
+                ]
+            )
+
+        bottom, top = ends(0), ends(14)
         if first_round:
-            flat_y = (3 * 2 * 3 * 8, 128)
-            down, up = neighbours(
-                jnp.concatenate([bottom.reshape(flat_y), planes[:, 0], planes[:, 0]]),
-                jnp.concatenate([top.reshape(flat_y), planes[:, 15], planes[:, 15]]),
-                GY,
-            )
-            scale_mid = spread(planes, 16)
+            flat = (3 * 2 * 3 * 8, 128)
+            bottom = jnp.concatenate([bottom.reshape(flat), planes[:, 0], planes[:, 0]])
+            top = jnp.concatenate([top.reshape(flat), planes[:, 15], planes[:, 15]])
+        swap_c, swap_d = swap(
+            jnp.where(flags[1], top, bottom), jnp.where(flags[1], bottom, top), GY
+        )
+        if first_round:
+            pairs = planes.reshape(2, 2, 16, 128).transpose(2, 0, 1, 3)
+            scale = jnp.broadcast_to(pairs[:, :, :, None], (16, 2, 2, 4, 128))
+            scale = scale.reshape(16, 2, 8, 128)
             scale_own = jnp.broadcast_to(
                 masked.transpose(1, 0, 2)[:, :, None], (16, 2, 4, 128)
             ).reshape(16, 8, 128)
-            before = interval
+            before = scale_far = interval
         else:
-            down, up = neighbours(bottom, top, GY)
             before = blocks[-2]
-        started = middle(first_round, coef, interval, left, own, right, started, before, scale_mid)
+        shared = (coef, interval, parity, swap_a, own, swap_b)
+        started = middle(first_round, *shared, started, before, scale, scale_own)
+        done = outer(
+            first_round,
+            *shared,
+            *(swap_c, swap_d, before, scale, scale_own, scale_far, *started),
+        )
         if first_round:
-            down, up, started, scale_own = lax.optimization_barrier((down, up, started, scale_own))
-            planes = jnp.concatenate([down[144:148, None], planes, up[144:148, None]], axis=1)
-            down, up = down[:144].reshape(bottom.shape), up[:144].reshape(top.shape)
-            scale = spread(planes, 18)
-        mid, own = outer(
-            first_round,
-            *(coef, interval, left, own, right, down, up, before, scale, scale_own, started),
-        )
-        blocks += [mid, own]
+            scale_far = done[2]
+        own = done[1]
+        blocks += done[:2]
 
     table = lax.psum(sketch((1, 0), rows, signs, blocks[-2:], sketches), "gy_1")
     copies = jnp.broadcast_to(table, (16,) + table.shape)

time: 144 us -> 122 us (0.85)
  starting transfers between devices: 48.2 us -> 40.5 us
  Pallas kernels: 41.6 us -> 35.8 us
  blocking collectives: 39.1 us -> 34.2 us
  local copies, waits for them, and re-layouts: 6.14 us -> 2.4 us
    ppermute x16, starting transfers between devices: 48.2 us -> 40.5 us  [swap(): out.append(lax.ppermute(operand, axis, pairs))]
    all_to_all x1, blocking collectives: 24.9 us -> 18.9 us  [cycle(): copies = lax.all_to_all(copies, ('gx_0', 'gy_0'), 0, 0, tiled=True)]
    pallas_call x5 -> x4, Pallas kernels: 7.66 us -> 4.04 us  [sketch(): pl.pallas_call(make_sketch_kernel(kinds, len(earlier)), out_shape=shaped(...]
    unnamed x21 -> x13, local copies, waits for them, and re-layouts: 5.04 us -> 2.03 us
    pallas_call x4, Pallas kernels: 9.67 us -> 7.11 us  [outer(): pl.pallas_call(make_outer_kernel(first_round), out_shape=(shaped(18, 3, 3...]
    pallas_call x1, Pallas kernels: 2.96 us -> 1 us  [setup(): pl.pallas_call(setup_kernel, out_shape=(shaped(243, 8, 128), shaped(2, 8,...]
    pallas_call x8 -> x9, Pallas kernels: 14.1 us -> 15.8 us  [the longest x4 9.96 us: middle(): pl.pallas_call(make_middle_kernel(first_round), out_shape=(shaped(18, 3,...]
where the time goes in v3:
time: 122 us
  starting transfers between devices  40.5 us (33%)
  Pallas kernels  35.8 us (29%)
  blocking collectives  34.2 us (28%)
  waiting for transfers between devices  7.61 us (6%)
  local copies, waits for them, and re-layouts  2.4 us (2%)
    ppermute x16, starting transfers between devices, swap(): out.append(lax.ppermute(operand, axis, pairs))  40.5 us
    all_to_all x1, blocking collectives, cycle(): copies = lax.all_to_all(copies, ('gx_0', 'gy_0'), 0, 0, tiled=True)  18.9 us
    all_to_all x1, blocking collectives, cycle(): copies = lax.all_to_all(fold(copies, 8), ('gx_1',), 0, 0, tiled=True)  11.6 us
    pallas_call x4, Pallas kernels, middle(): pl.pallas_call(make_middle_kernel(first_round), out_shape=(shaped(18, 3,...  9.96 us
    ppermute x16, waiting for transfers between devices, swap(): out.append(lax.ppermute(operand, axis, pairs))  7.61 us
    pallas_call x4, Pallas kernels, outer(): pl.pallas_call(make_outer_kernel(first_round), out_shape=(shaped(18, 3, 3...  7.11 us
    pallas_call x1, Pallas kernels, finish(): pl.pallas_call(finish_kernel, out_shape=(shaped(2, 16, 3, 4, 128), shaped...  6.19 us
    pallas_call x4, Pallas kernels, inner(): pl.pallas_call(inner_kernel, out_shape=shaped(14, 3, 3, 8, 128), in_specs...  4.64 us
  transfers between devices with their start and end apart: 16, of which 4 were waited for; matrix products, arithmetic and copies ran while one was open for 0% of the time, Pallas kernels for 16%

profile of v3, /device:TPU:1, one launch (start us, length us, event | category | flops | bytes accessed | tf_op | source)
XLA Modules:
  0.0 121.7 jit_solution(11502134769649289125)
XLA Ops:
  0.7 0.0 copy-start.4
  0.7 0.1 stack.97.parity
  0.7 0.6 copy-done.4
  1.3 1.6 %prepare.1 = (f32[16,3,8,128]{3,2,1,0:T(8,128)S(1)}, f32[400,128]{1,0:T(8,128)S(1)}, f32[400,128]{1,0:T(8,128)S(1)}, f32[2,16,128]{2,1,0:T(8,128)S(1)}) custom-call(f32[8]{0:T(128)S(1)} %copy-done.4, f32[2,8,128]{2,1,0:T(8,128)S(1)} %stack.97.parity, f32[2,16,3,4,128]{4,3,2,1,0:T(4,128)} %bitcast.97, s32[2,16,128]{2,1,0:T(8,128)} %far_material.1, ...), custom_call_target="tpu_custom_call" | custom-call | tf_op jit(solution)/shard_map/prepare/pallas_call | solution.py:71
  3.0 2.5 %collective-permute-start = (f32[400,128]{1,0:T(8,128)S(1)}, f32[400,128]{1,0:T(8,128)S(1)}, u32[]{:S(2)}, u32[]{:S(2)}) collective-permute-start(f32[400,128]{1,0:T(8,128)S(1)} %get-tuple-element.45), channel_id=1, source_target_pairs={{0,8},{8,0},{16,24},{24,16},{32,40},{40,32},{48,56},{56,48},{64,72... | collective-permute-start | bytes 614408 | tf_op jit(solution)/shard_map/ppermute | solution.py:612
  5.5 0.7 collective-permute-start.1
  6.2 0.1 copy.20
  6.3 0.2 reshape.118.stencil
  6.5 1.0 setup.1
  7.5 1.2 inner.4.part
  8.7 0.6 collective-permute-done
  9.3 0.0 collective-permute-done.1
  9.4 0.0 copy-start.2
  9.4 5.3 %collective-permute-start.3 = (f32[152,128]{1,0:T(8,128)S(1)}, f32[152,128]{1,0:T(8,128)S(1)}, u32[]{:S(2)}, u32[]{:S(2)}) collective-permute-start(f32[152,128]{1,0:T(8,128)S(1)} %get-tuple-element.110), channel_id=1, source_target_pairs={{1,2},{2,1},{3,4},{4,3},{5,6},{6,5},{9,10},{10,9},{11,12},{12,11},... | collective-permute-start | bytes 233480 | tf_op jit(solution)/shard_map/ppermute | solution.py:612
  14.7 0.1 collective-permute-start.2
  14.8 0.0 copy-start.3
  14.8 0.6 copy-done.3
  15.5 1.2 signs.1
  16.8 2.5 %middle.4 = (f32[18,3,3,8,128]{4,3,2,1,0:T(8,128)S(1)}, f32[16,3,8,128]{3,2,1,0:T(8,128)S(1)}) custom-call(f32[243,8,128]{2,1,0:T(8,128)S(1)} %get-tuple-element.43.coef, f32[2,8,128]{2,1,0:T(8,128)S(1)} %get-tuple-element.44.interval.before.scale_far, f32[2,8,128]{2,1,0:T(8,128)S(1)} %stack.97.parity, f32[16,3,8,128]{3,2,1,0:T(8,128)S(1)} %bitcast.86, ...), custom_call_target="tpu_custom_call" | custom-call | tf_op jit(solution)/shard_map/middle/pallas_call | solution.py:312
  19.3 0.0 collective-permute-done.3.swap_d
  19.3 0.0 collective-permute-done.2.swap_c
  19.3 1.8 %outer.4 = (f32[18,3,3,8,128]{4,3,2,1,0:T(8,128)S(1)}, f32[16,3,8,128]{3,2,1,0:T(8,128)S(1)}, f32[2,2,8,128]{3,2,1,0:T(8,128)S(1)}) custom-call(f32[243,8,128]{2,1,0:T(8,128)S(1)} %get-tuple-element.43.coef, f32[2,8,128]{2,1,0:T(8,128)S(1)} %get-tuple-element.44.interval.before.scale_far, ...), custom_call_target="tpu_custom_call", output_to_operand_aliasing={{0}: (12, {}), {1}: (13, {})} | custom-call | tf_op jit(solution)/shard_map/outer/pallas_call | solution.py:407
  21.1 0.7 collective-permute-start.5
  21.7 7.9 %collective-permute-start.4 = (f32[16,3,8,128]{3,2,1,0:T(8,128)S(1)}, f32[16,3,8,128]{3,2,1,0:T(8,128)S(1)}, u32[]{:S(2)}, u32[]{:S(2)}) collective-permute-start(f32[16,3,8,128]{3,2,1,0:T(8,128)S(1)} %get-tuple-element.55.refs_2_.own.l0), channel_id=1, source_target_pairs={{0,8},{8,0},{16,24},{24,16},{32,40},{40,32},{48,56},{56,48},{64,72... | collective-permute-start | bytes 589832 | tf_op jit(solution)/shard_map/ppermute | solution.py:612
  29.7 1.2 inner.5.part
  30.8 1.1 sketch.4.refs_2_
  31.9 0.0 collective-permute-done.5.swap_b
  31.9 2.3 %collective-permute-done.4.swap_a = f32[16,3,8,128]{3,2,1,0:T(8,128)S(1)} collective-permute-done((f32[16,3,8,128]{3,2,1,0:T(8,128)S(1)}, f32[16,3,8,128]{3,2,1,0:T(8,128)S(1)}, u32[]{:S(2)}, u32[]{:S(2)}) %collective-permute-start.4) | collective-permute-done | bytes 196640 | tf_op jit(solution)/shard_map/ppermute | solution.py:612
  34.2 4.4 %collective-permute-start.7 = (f32[3,2,3,8,128]{4,3,2,1,0:T(8,128)S(1)}, f32[3,2,3,8,128]{4,3,2,1,0:T(8,128)S(1)}, u32[]{:S(2)}, u32[]{:S(2)}) collective-permute-start(f32[3,2,3,8,128]{4,3,2,1,0:T(8,128)S(1)} %get-tuple-element.116), channel_id=1, source_target_pairs={{1,2},{2,1},{3,4},{4,3},{5,6},{6,5},{9,10},{10,9},{11,12},{12,11},... | collective-permute-start | bytes 221192 | tf_op jit(solution)/shard_map/ppermute | solution.py:612
  38.6 0.1 collective-permute-start.6
  38.7 2.5 %middle.5 = (f32[18,3,3,8,128]{4,3,2,1,0:T(8,128)S(1)}, f32[16,3,8,128]{3,2,1,0:T(8,128)S(1)}) custom-call(f32[243,8,128]{2,1,0:T(8,128)S(1)} %get-tuple-element.43.coef, f32[2,8,128]{2,1,0:T(8,128)S(1)} %get-tuple-element.44.interval.before.scale_far, f32[2,8,128]{2,1,0:T(8,128)S(1)} %stack.97.parity, f32[16,3,8,128]{3,2,1,0:T(8,128)S(1)} %collective-permute-done.4.swap_a, ...), custom_call_target="tpu_custom_call" | custom-call | tf_op jit(solution)/shard_map/middle/pallas_call | solution.py:312
  41.2 0.0 collective-permute-done.7.swap_d
  41.2 0.0 collective-permute-done.6.swap_c
  41.2 1.8 %outer.5 = (f32[18,3,3,8,128]{4,3,2,1,0:T(8,128)S(1)}, f32[16,3,8,128]{3,2,1,0:T(8,128)S(1)}) custom-call(f32[243,8,128]{2,1,0:T(8,128)S(1)} %get-tuple-element.43.coef, f32[2,8,128]{2,1,0:T(8,128)S(1)} %get-tuple-element.44.interval.before.scale_far, f32[2,8,128]{2,1,0:T(8,128)S(1)} %stack.97.parity, ...), custom_call_target="tpu_custom_call", output_to_operand_aliasing={{0}: (12, {}), {1}: (13, {})} | custom-call | tf_op jit(solution)/shard_map/outer/pallas_call | solution.py:407
  43.0 0.7 collective-permute-start.9
  43.6 6.1 %collective-permute-start.8 = (f32[16,3,8,128]{3,2,1,0:T(8,128)S(1)}, f32[16,3,8,128]{3,2,1,0:T(8,128)S(1)}, u32[]{:S(2)}, u32[]{:S(2)}) collective-permute-start(f32[16,3,8,128]{3,2,1,0:T(8,128)S(1)} %get-tuple-element.63.refs_1_.own.l1), channel_id=1, source_target_pairs={{0,8},{8,0},{16,24},{24,16},{32,40},{40,32},{48,56},{56,48},{64,72... | collective-permute-start | bytes 589832 | tf_op jit(solution)/shard_map/ppermute | solution.py:612
  49.7 1.2 inner.6.part
  50.9 1.0 sketch.5.refs_3_
  51.9 0.0 collective-permute-done.9.swap_b
  51.9 2.3 %collective-permute-done.8.swap_a = f32[16,3,8,128]{3,2,1,0:T(8,128)S(1)} collective-permute-done((f32[16,3,8,128]{3,2,1,0:T(8,128)S(1)}, f32[16,3,8,128]{3,2,1,0:T(8,128)S(1)}, u32[]{:S(2)}, u32[]{:S(2)}) %collective-permute-start.8) | collective-permute-done | bytes 196640 | tf_op jit(solution)/shard_map/ppermute | solution.py:612
  54.3 4.1 %collective-permute-start.11 = (f32[3,2,3,8,128]{4,3,2,1,0:T(8,128)S(1)}, f32[3,2,3,8,128]{4,3,2,1,0:T(8,128)S(1)}, u32[]{:S(2)}, u32[]{:S(2)}) collective-permute-start(f32[3,2,3,8,128]{4,3,2,1,0:T(8,128)S(1)} %get-tuple-element.114), channel_id=1, source_target_pairs={{1,2},{2,1},{3,4},{4,3},{5,6},{6,5},{9,10},{10,9},{11,12},{12,11},... | collective-permute-start | bytes 221192 | tf_op jit(solution)/shard_map/ppermute | solution.py:612
  58.4 0.1 collective-permute-start.10
  58.5 2.5 %middle.6 = (f32[18,3,3,8,128]{4,3,2,1,0:T(8,128)S(1)}, f32[16,3,8,128]{3,2,1,0:T(8,128)S(1)}) custom-call(f32[243,8,128]{2,1,0:T(8,128)S(1)} %get-tuple-element.43.coef, f32[2,8,128]{2,1,0:T(8,128)S(1)} %get-tuple-element.44.interval.before.scale_far, f32[2,8,128]{2,1,0:T(8,128)S(1)} %stack.97.parity, f32[16,3,8,128]{3,2,1,0:T(8,128)S(1)} %collective-permute-done.8.swap_a, ...), custom_call_target="tpu_custom_call" | custom-call | tf_op jit(solution)/shard_map/middle/pallas_call | solution.py:312
  61.0 0.0 collective-permute-done.11.swap_d
  61.0 0.0 collective-permute-done.10.swap_c
  61.0 1.8 %outer.6 = (f32[18,3,3,8,128]{4,3,2,1,0:T(8,128)S(1)}, f32[16,3,8,128]{3,2,1,0:T(8,128)S(1)}) custom-call(f32[243,8,128]{2,1,0:T(8,128)S(1)} %get-tuple-element.43.coef, f32[2,8,128]{2,1,0:T(8,128)S(1)} %get-tuple-element.44.interval.before.scale_far, f32[2,8,128]{2,1,0:T(8,128)S(1)} %stack.97.parity, ...), custom_call_target="tpu_custom_call", output_to_operand_aliasing={{0}: (12, {}), {1}: (13, {})} | custom-call | tf_op jit(solution)/shard_map/outer/pallas_call | solution.py:407
  62.7 0.7 collective-permute-start.13
  63.4 3.9 %collective-permute-start.12 = (f32[16,3,8,128]{3,2,1,0:T(8,128)S(1)}, f32[16,3,8,128]{3,2,1,0:T(8,128)S(1)}, u32[]{:S(2)}, u32[]{:S(2)}) collective-permute-start(f32[16,3,8,128]{3,2,1,0:T(8,128)S(1)} %get-tuple-element.70.refs_1_.own.l2), channel_id=1, source_target_pairs={{0,8},{8,0},{16,24},{24,16},{32,40},{40,32},{48,56},{56,48},{64,72... | collective-permute-start | bytes 589832 | tf_op jit(solution)/shard_map/ppermute | solution.py:612
  67.3 1.2 inner.7.part
  68.5 1.0 sketch.6.refs_4_
  69.5 0.0 collective-permute-done.13.swap_b
  69.5 2.3 %collective-permute-done.12.swap_a = f32[16,3,8,128]{3,2,1,0:T(8,128)S(1)} collective-permute-done((f32[16,3,8,128]{3,2,1,0:T(8,128)S(1)}, f32[16,3,8,128]{3,2,1,0:T(8,128)S(1)}, u32[]{:S(2)}, u32[]{:S(2)}) %collective-permute-start.12) | collective-permute-done | bytes 196640 | tf_op jit(solution)/shard_map/ppermute | solution.py:612
  71.9 3.3 %collective-permute-start.15 = (f32[3,2,3,8,128]{4,3,2,1,0:T(8,128)S(1)}, f32[3,2,3,8,128]{4,3,2,1,0:T(8,128)S(1)}, u32[]{:S(2)}, u32[]{:S(2)}) collective-permute-start(f32[3,2,3,8,128]{4,3,2,1,0:T(8,128)S(1)} %get-tuple-element.112), channel_id=1, source_target_pairs={{1,2},{2,1},{3,4},{4,3},{5,6},{6,5},{9,10},{10,9},{11,12},{12,11},... | collective-permute-start | bytes 221192 | tf_op jit(solution)/shard_map/ppermute | solution.py:612
  75.2 0.1 collective-permute-start.14
  75.3 2.5 %middle.7 = (f32[18,3,3,8,128]{4,3,2,1,0:T(8,128)S(1)}, f32[16,3,8,128]{3,2,1,0:T(8,128)S(1)}) custom-call(f32[243,8,128]{2,1,0:T(8,128)S(1)} %get-tuple-element.43.coef, f32[2,8,128]{2,1,0:T(8,128)S(1)} %get-tuple-element.44.interval.before.scale_far, f32[2,8,128]{2,1,0:T(8,128)S(1)} %stack.97.parity, f32[16,3,8,128]{3,2,1,0:T(8,128)S(1)} %collective-permute-done.12.swap_a, ...), custom_call_target="tpu_custom_call" | custom-call | tf_op jit(solution)/shard_map/middle/pallas_call | solution.py:312
  77.8 0.0 collective-permute-done.15.swap_d
  77.8 1.8 %outer.7 = (f32[18,3,3,8,128]{4,3,2,1,0:T(8,128)S(1)}, f32[16,3,8,128]{3,2,1,0:T(8,128)S(1)}) custom-call(f32[243,8,128]{2,1,0:T(8,128)S(1)} %get-tuple-element.43.coef, f32[2,8,128]{2,1,0:T(8,128)S(1)} %get-tuple-element.44.interval.before.scale_far, f32[2,8,128]{2,1,0:T(8,128)S(1)} %stack.97.parity, ...), custom_call_target="tpu_custom_call", output_to_operand_aliasing={{0}: (12, {}), {1}: (13, {})} | custom-call | tf_op jit(solution)/shard_map/outer/pallas_call | solution.py:407
  79.6 1.0 sketch.7
  80.6 0.7 copy-done
  81.3 3.7 %psum.7 = f32[36,128]{1,0:T(8,128)S(1)} all-reduce(f32[36,128]{1,0:T(8,128)S(1)} %sketch.7), channel_id=1, replica_groups=mesh['gx_0'=4,'gx_1'=8,'gy_0'=4,'gy_1'=2] {'gy_1'}, use_global_device_ids=true, to_apply=%region_0.1 | all-reduce | flops 4608 | bytes 36864 | tf_op jit(solution)/shard_map/psum | solution.py:716
  85.0 18.9 %all_to_all.10.parts = f32[16,36,128]{2,1,0:T(8,128)S(1)} all-to-all(f32[16,36,128]{2,1,0:T(8,128)S(1)} %broadcast_in_dim.8), channel_id=1, replica_groups=mesh['gx_0'=4,'gx_1'=8,'gy_0'=4,'gy_1'=2] {'gx_0','gy_0'}, dimensions={0} | all-to-all | bytes 589824 | tf_op jit(solution)/shard_map/all_to_all | solution.py:718
  103.9 0.0 copy-start.1
  103.9 11.6 %all_to_all.11.table = f32[8,36,128]{2,1,0:T(8,128)S(1)} all-to-all(f32[8,36,128]{2,1,0:T(8,128)S(1)} %fold.1), channel_id=1, replica_groups=mesh['gx_0'=4,'gx_1'=8,'gy_0'=4,'gy_1'=2] {'gx_1'}, dimensions={0} | all-to-all | bytes 294912 | tf_op jit(solution)/shard_map/all_to_all | solution.py:719
  115.5 6.2 %finish.1 = (f32[2,16,3,4,128]{4,3,2,1,0:T(4,128)}, f32[2,16,3,4,128]{4,3,2,1,0:T(4,128)}) custom-call(f32[8,36,128]{2,1,0:T(8,128)S(1)} %all_to_all.11.table, f32[2,8,128]{2,1,0:T(8,128)S(1)} %get-tuple-element.44.interval.before.scale_far, f32[16,3,8,128]{3,2,1,0:T(8,128)S(1)} %get-tuple-element.47.own.refs_0_.first, ...), custom_call_target="tpu_custom_call" | custom-call | tf_op jit(solution)/shard_map/finish/pallas_call | solution.py:596
  (31 shorter events, 0.3 us)
Async XLA Ops:
  0.7 0.7 copy-start.4
  1.3 4.9 %copy-start.5 = (f32[27,3,3]{0,2,1:T(4,128)S(1)}, f32[27,3,3]{0,2,1:T(4,128)}, u32[]{:S(2)}) copy-start(f32[27,3,3]{0,2,1:T(4,128)} %param.8) | copy-start | bytes 2920
  3.0 6.3 %collective-permute-start = (f32[400,128]{1,0:T(8,128)S(1)}, f32[400,128]{1,0:T(8,128)S(1)}, u32[]{:S(2)}, u32[]{:S(2)}) collective-permute-start(f32[400,128]{1,0:T(8,128)S(1)} %get-tuple-element.45), channel_id=1, source_target_pairs={{0,8},{8,0},{16,24},{24,16},{32,40},{40,32},{48,56},{56,48},{64,72... | collective-permute-start | bytes 614408 | tf_op jit(solution)/shard_map/ppermute | solution.py:612
  5.5 3.8 %collective-permute-start.1 = (f32[400,128]{1,0:T(8,128)S(1)}, f32[400,128]{1,0:T(8,128)S(1)}, u32[]{:S(2)}, u32[]{:S(2)}) collective-permute-start(f32[400,128]{1,0:T(8,128)S(1)} %get-tuple-element.46), channel_id=1, source_target_pairs={{8,16},{16,8},{24,32},{32,24},{40,48},{48,40},{56,64},{64,56},{72,... | collective-permute-start | bytes 614408 | tf_op jit(solution)/shard_map/ppermute | solution.py:612
  9.4 5.4 %copy-start.2 = (s32[2,16,3,128]{3,1,2,0:T(8,128)S(1)}, s32[2,16,3,128]{3,1,2,0:T(8,128)}, u32[]{:S(2)}) copy-start(s32[2,16,3,128]{3,1,2,0:T(8,128)} %param.12) | copy-start | bytes 147460
  9.4 9.9 %collective-permute-start.3 = (f32[152,128]{1,0:T(8,128)S(1)}, f32[152,128]{1,0:T(8,128)S(1)}, u32[]{:S(2)}, u32[]{:S(2)}) collective-permute-start(f32[152,128]{1,0:T(8,128)S(1)} %get-tuple-element.110), channel_id=1, source_target_pairs={{1,2},{2,1},{3,4},{4,3},{5,6},{6,5},{9,10},{10,9},{11,12},{12,11},... | collective-permute-start | bytes 233480 | tf_op jit(solution)/shard_map/ppermute | solution.py:612
  14.7 4.6 %collective-permute-start.2 = (f32[152,128]{1,0:T(8,128)S(1)}, f32[152,128]{1,0:T(8,128)S(1)}, u32[]{:S(2)}, u32[]{:S(2)}) collective-permute-start(f32[152,128]{1,0:T(8,128)S(1)} %get-tuple-element.111), channel_id=1, source_target_pairs={{0,1},{1,0},{2,3},{3,2},{4,5},{5,4},{6,7},{7,6},{8,9},{9,8},{10,11... | collective-permute-start | bytes 233480 | tf_op jit(solution)/shard_map/ppermute | solution.py:612
  14.8 0.7 copy-start.3
  21.1 10.8 %collective-permute-start.5 = (f32[16,3,8,128]{3,2,1,0:T(8,128)S(1)}, f32[16,3,8,128]{3,2,1,0:T(8,128)S(1)}, u32[]{:S(2)}, u32[]{:S(2)}) collective-permute-start(f32[16,3,8,128]{3,2,1,0:T(8,128)S(1)} %get-tuple-element.55.refs_2_.own.l0), channel_id=1, source_target_pairs={{8,16},{16,8},{24,32},{32,24},{40,48},{48,40},{56,64},{64,56},{72,... | collective-permute-start | bytes 589832 | tf_op jit(solution)/shard_map/ppermute | solution.py:612
  21.7 12.4 %collective-permute-start.4 = (f32[16,3,8,128]{3,2,1,0:T(8,128)S(1)}, f32[16,3,8,128]{3,2,1,0:T(8,128)S(1)}, u32[]{:S(2)}, u32[]{:S(2)}) collective-permute-start(f32[16,3,8,128]{3,2,1,0:T(8,128)S(1)} %get-tuple-element.55.refs_2_.own.l0), channel_id=1, source_target_pairs={{0,8},{8,0},{16,24},{24,16},{32,40},{40,32},{48,56},{56,48},{64,72... | collective-permute-start | bytes 589832 | tf_op jit(solution)/shard_map/ppermute | solution.py:612
  34.2 7.0 %collective-permute-start.7 = (f32[3,2,3,8,128]{4,3,2,1,0:T(8,128)S(1)}, f32[3,2,3,8,128]{4,3,2,1,0:T(8,128)S(1)}, u32[]{:S(2)}, u32[]{:S(2)}) collective-permute-start(f32[3,2,3,8,128]{4,3,2,1,0:T(8,128)S(1)} %get-tuple-element.116), channel_id=1, source_target_pairs={{1,2},{2,1},{3,4},{4,3},{5,6},{6,5},{9,10},{10,9},{11,12},{12,11},... | collective-permute-start | bytes 221192 | tf_op jit(solution)/shard_map/ppermute | solution.py:612
  38.6 2.6 %collective-permute-start.6 = (f32[3,2,3,8,128]{4,3,2,1,0:T(8,128)S(1)}, f32[3,2,3,8,128]{4,3,2,1,0:T(8,128)S(1)}, u32[]{:S(2)}, u32[]{:S(2)}) collective-permute-start(f32[3,2,3,8,128]{4,3,2,1,0:T(8,128)S(1)} %get-tuple-element.117), channel_id=1, source_target_pairs={{0,1},{1,0},{2,3},{3,2},{4,5},{5,4},{6,7},{7,6},{8,9},{9,8},{10,11... | collective-permute-start | bytes 221192 | tf_op jit(solution)/shard_map/ppermute | solution.py:612
  43.0 8.9 %collective-permute-start.9 = (f32[16,3,8,128]{3,2,1,0:T(8,128)S(1)}, f32[16,3,8,128]{3,2,1,0:T(8,128)S(1)}, u32[]{:S(2)}, u32[]{:S(2)}) collective-permute-start(f32[16,3,8,128]{3,2,1,0:T(8,128)S(1)} %get-tuple-element.63.refs_1_.own.l1), channel_id=1, source_target_pairs={{8,16},{16,8},{24,32},{32,24},{40,48},{48,40},{56,64},{64,56},{72,... | collective-permute-start | bytes 589832 | tf_op jit(solution)/shard_map/ppermute | solution.py:612
  43.6 10.6 %collective-permute-start.8 = (f32[16,3,8,128]{3,2,1,0:T(8,128)S(1)}, f32[16,3,8,128]{3,2,1,0:T(8,128)S(1)}, u32[]{:S(2)}, u32[]{:S(2)}) collective-permute-start(f32[16,3,8,128]{3,2,1,0:T(8,128)S(1)} %get-tuple-element.63.refs_1_.own.l1), channel_id=1, source_target_pairs={{0,8},{8,0},{16,24},{24,16},{32,40},{40,32},{48,56},{56,48},{64,72... | collective-permute-start | bytes 589832 | tf_op jit(solution)/shard_map/ppermute | solution.py:612
  54.3 6.7 %collective-permute-start.11 = (f32[3,2,3,8,128]{4,3,2,1,0:T(8,128)S(1)}, f32[3,2,3,8,128]{4,3,2,1,0:T(8,128)S(1)}, u32[]{:S(2)}, u32[]{:S(2)}) collective-permute-start(f32[3,2,3,8,128]{4,3,2,1,0:T(8,128)S(1)} %get-tuple-element.114), channel_id=1, source_target_pairs={{1,2},{2,1},{3,4},{4,3},{5,6},{6,5},{9,10},{10,9},{11,12},{12,11},... | collective-permute-start | bytes 221192 | tf_op jit(solution)/shard_map/ppermute | solution.py:612
  58.4 2.6 %collective-permute-start.10 = (f32[3,2,3,8,128]{4,3,2,1,0:T(8,128)S(1)}, f32[3,2,3,8,128]{4,3,2,1,0:T(8,128)S(1)}, u32[]{:S(2)}, u32[]{:S(2)}) collective-permute-start(f32[3,2,3,8,128]{4,3,2,1,0:T(8,128)S(1)} %get-tuple-element.115), channel_id=1, source_target_pairs={{0,1},{1,0},{2,3},{3,2},{4,5},{5,4},{6,7},{7,6},{8,9},{9,8},{10,11... | collective-permute-start | bytes 221192 | tf_op jit(solution)/shard_map/ppermute | solution.py:612
  62.7 6.7 %collective-permute-start.13 = (f32[16,3,8,128]{3,2,1,0:T(8,128)S(1)}, f32[16,3,8,128]{3,2,1,0:T(8,128)S(1)}, u32[]{:S(2)}, u32[]{:S(2)}) collective-permute-start(f32[16,3,8,128]{3,2,1,0:T(8,128)S(1)} %get-tuple-element.70.refs_1_.own.l2), channel_id=1, source_target_pairs={{8,16},{16,8},{24,32},{32,24},{40,48},{48,40},{56,64},{64,56},{72,... | collective-permute-start | bytes 589832 | tf_op jit(solution)/shard_map/ppermute | solution.py:612
  63.4 8.4 %collective-permute-start.12 = (f32[16,3,8,128]{3,2,1,0:T(8,128)S(1)}, f32[16,3,8,128]{3,2,1,0:T(8,128)S(1)}, u32[]{:S(2)}, u32[]{:S(2)}) collective-permute-start(f32[16,3,8,128]{3,2,1,0:T(8,128)S(1)} %get-tuple-element.70.refs_1_.own.l2), channel_id=1, source_target_pairs={{0,8},{8,0},{16,24},{24,16},{32,40},{40,32},{48,56},{56,48},{64,72... | collective-permute-start | bytes 589832 | tf_op jit(solution)/shard_map/ppermute | solution.py:612
  71.9 6.0 %collective-permute-start.15 = (f32[3,2,3,8,128]{4,3,2,1,0:T(8,128)S(1)}, f32[3,2,3,8,128]{4,3,2,1,0:T(8,128)S(1)}, u32[]{:S(2)}, u32[]{:S(2)}) collective-permute-start(f32[3,2,3,8,128]{4,3,2,1,0:T(8,128)S(1)} %get-tuple-element.112), channel_id=1, source_target_pairs={{1,2},{2,1},{3,4},{4,3},{5,6},{6,5},{9,10},{10,9},{11,12},{12,11},... | collective-permute-start | bytes 221192 | tf_op jit(solution)/shard_map/ppermute | solution.py:612
  75.2 2.6 %collective-permute-start.14 = (f32[3,2,3,8,128]{4,3,2,1,0:T(8,128)S(1)}, f32[3,2,3,8,128]{4,3,2,1,0:T(8,128)S(1)}, u32[]{:S(2)}, u32[]{:S(2)}) collective-permute-start(f32[3,2,3,8,128]{4,3,2,1,0:T(8,128)S(1)} %get-tuple-element.113), channel_id=1, source_target_pairs={{0,1},{1,0},{2,3},{3,2},{4,5},{5,4},{6,7},{7,6},{8,9},{9,8},{10,11... | collective-permute-start | bytes 221192 | tf_op jit(solution)/shard_map/ppermute | solution.py:612
  80.6 0.7 copy-start
  103.9 11.6 %copy-start.1 = (f32[16,3,8,128]{3,2,1,0:T(8,128)S(1)}, f32[16,3,8,128]{3,2,1,0:T(8,128)}, u32[]{:S(2)}) copy-start(f32[16,3,8,128]{3,2,1,0:T(8,128)} %copy-done) | copy-start | bytes 589828

commit v4 on v3

--- a/solution.py
+++ b/solution.py
@@ -28,17 +28,18 @@
     return jax.ShapeDtypeStruct(shape, F32)
 
 
-def prepare_kernel(class_scale, parity, far_side, far_material, far_boundary, own, first, second, masked, *scratch):
-    right_side, material, boundary, sems = scratch
+def prepare_kernel(parity, far_class, far_side, far_material, far_boundary, own, first, second, masked, *scratch):
+    class_scale, right_side, material, boundary, sems = scratch
     copies = [
+        pltpu.make_async_copy(far_class, class_scale, sems.at[3]),
         pltpu.make_async_copy(far_material, material, sems.at[0]),
         pltpu.make_async_copy(far_boundary, boundary, sems.at[1]),
         pltpu.make_async_copy(far_side, right_side, sems.at[2]),
     ]
     for copy in copies:
         copy.start()
-    copies[0].wait()
-    copies[1].wait()
+    for copy in copies[:3]:
+        copy.wait()
     even = parity[0] != 0.0
     for half in range(2):
         rows = pl.ds(half * 8, 8)
@@ -54,7 +55,7 @@
         first[pl.ds(384 + half * 8, 8)] = jnp.where(even, fields[1], fields[0])
         second[pl.ds(384 + half * 8, 8)] = jnp.where(even, fields[0], fields[1])
 
-    copies[2].wait()
+    copies[3].wait()
 
     def one_row(y, carry):
         for c in range(3):
@@ -67,21 +68,22 @@
     lax.fori_loop(0, 16, one_row, 0)
 
 
-def prepare(class_scale, parity, *operands):
+def prepare(parity, *operands):
     return pl.pallas_call(
         prepare_kernel,
         out_shape=(shaped(16, 3, 8, 128), shaped(400, 128), shaped(400, 128), shaped(2, 16, 128)),
-        in_specs=[SMEM, VMEM, FAR, FAR, FAR],
+        in_specs=[VMEM, FAR, FAR, FAR, FAR],
         out_specs=(VMEM,) * 4,
         scratch_shapes=[
+            pltpu.SMEM((8,), F32),
             pltpu.VMEM((2, 16, 3, 4, 128), F32),
             pltpu.VMEM((2, 16, 128), jnp.int32),
             pltpu.VMEM((2, 16, 128), jnp.int32),
-            pltpu.SemaphoreType.DMA((3,)),
+            pltpu.SemaphoreType.DMA((4,)),
         ],
         compiler_params=PARAMS,
         name="prepare",
-    )(class_scale, parity, *[pltpu.with_memory_space_constraint(x, pltpu.HBM) for x in operands])
+    )(parity, *[pltpu.with_memory_space_constraint(x, pltpu.HBM) for x in operands])
 
 
 def setup_kernel(stencil, class_scale, coef, interval):
@@ -320,16 +322,21 @@
     )(*operands)
 
 
-def make_outer_kernel(first_round):
+def make_outer_kernel(first_round, extra):
+    final = extra > 0
+
     def kernel(
         coef, interval, parity, swap_a, own, swap_b, swap_c, swap_d, before, scale, scale_own,
-        scale_far, mid_before, last_before, mid, last, *rest,
+        scale_far, mid_before, last_before, *refs,
     ):
         del mid_before, last_before
-        work = rest[-1]
+        if final:
+            rows, signs, *parts = refs[:extra]
+            table, both = refs[extra + 2], refs[-1]
+        mid, last, *rest = refs[extra:]
+        edge_scale, work = rest[-3:-1] if final else rest[-2:]
         value_of = recurrence(interval)
         even_x, even_y = parity[0] != 0.0, parity[1] != 0.0
-        edge_scale = rest[-2]
 
         def message(n, row, c):
             if not first_round:
@@ -372,11 +379,9 @@
                 edge_scale[edge, 1 - edge, side] = scale[15 * edge, side]
 
         def edges(i, carry):
-            component, edge = i % 3, i // 3
-            for side in range(2):
-                terms = [
-                    (dx, lambda r, c, dx=dx: work[edge, r, side * 2 + dx, c]) for dx in range(3)
-                ]
+            edge, side = i // 2, i % 2
+            terms = [(dx, lambda r, c, dx=dx: work[edge, r, side * 2 + dx, c]) for dx in range(3)]
+            for component in range(3):
                 for r, total in enumerate(stencil_rows(coef, component, 2, terms)):
                     row = edge * 16 + r
                     value = value_of(
@@ -389,85 +394,92 @@
                     mid[row, side * 2, component] = value
             return carry
 
-        lax.fori_loop(0, 6, edges, 0)
+        lax.fori_loop(0, 4, edges, 0)
         for row in (0, 1, 16, 17):
             join(mid, row)
 
-        def second(i, carry):
-            second_step(mid, own, scale_own, value_of, coef, i % 3, i // 3 * 14, 2, last)
+        def second(edge, carry):
+            for component in range(3):
+                second_step(mid, own, scale_own, value_of, coef, component, edge * 14, 2, last)
             return carry
 
-        lax.fori_loop(0, 6, second, 0)
+        lax.fori_loop(0, 2, second, 0)
+        if final:
+            sketch_blocks(((mid, 1), (last, 0)), rows, signs, both, table, parts)
 
     return kernel
 
 
-def outer(first_round, *operands):
-    far = (shaped(2, 2, 8, 128),) if first_round else ()
-    return pl.pallas_call(
-        make_outer_kernel(first_round),
-        out_shape=(shaped(18, 3, 3, 8, 128), shaped(16, 3, 8, 128), *far),
-        in_specs=[VMEM] * 14,
-        out_specs=(VMEM,) * (2 + len(far)),
-        scratch_shapes=[
-            pltpu.VMEM((2, 2, 2, 8, 128), F32),
-            pltpu.VMEM((2, 4, 5, 3, 8, 128), F32),
-        ],
+def outer(first_round, *operands, tail=()):
+    extra = ()
+    scratch = [pltpu.VMEM((2, 2, 2, 8, 128), F32), pltpu.VMEM((2, 4, 5, 3, 8, 128), F32)]
+    if first_round:
+        extra = (shaped(2, 2, 8, 128),)
+    if tail:
+        extra = (shaped(36, 128),)
+        scratch.append(pltpu.VMEM((2, 96, 8, 128), F32))
+    return pl.pallas_call(
+        make_outer_kernel(first_round, len(tail)),
+        out_shape=(shaped(18, 3, 3, 8, 128), shaped(16, 3, 8, 128), *extra),
+        in_specs=[VMEM] * 14 + [SMEM] * bool(tail) + [VMEM] * (len(tail) - 1),
+        out_specs=(VMEM,) * (2 + len(extra)),
+        scratch_shapes=scratch,
         input_output_aliases={12: 0, 13: 1},
         compiler_params=PARAMS,
         name="outer",
-    )(*operands)
-
-
-def make_sketch_kernel(kinds, earlier):
+    )(*operands, *tail)
+
+
+def sketch_blocks(blocks, rows, signs, both, out, earlier=()):
+    base = 0
+    for part in earlier:
+        size = part.shape[0]
+        out[pl.ds(base, size), :] = part[...]
+        base += size
+    half = tile_iota(0) < 4
+    lane = tile_iota(1)
+
+    def spread(y, carry):
+        for n, (block, kind) in enumerate(blocks):
+            for c in range(3):
+                tile = block[y + 1, 1, c] if kind else block[y, c]
+                both[n, y * 3 + c] = tile
+                both[n, 48 + y * 3 + c] = pltpu.roll(tile, 4, 0)
+        return carry
+
+    lax.fori_loop(0, 16, spread, 0)
+    sums = [jnp.zeros((8, 128), F32)] * len(blocks)
+    for j in range(64):
+        first = lax.shift_right_logical(rows[j], 7)
+        second = lax.shift_right_logical(rows[64 + j], 7)
+        second = jnp.where(second < 48, second + 48, second - 48)
+        sign = signs[j]
+        for n in range(len(blocks)):
+            tile = jnp.where(half, both[n, first], both[n, second]) * sign
+            sums[n] = jnp.where(lane == j, jnp.sum(tile, axis=1, keepdims=True), sums[n])
+    for n, total in enumerate(sums):
+        folded = jnp.where(lane < 64, total, pltpu.roll(pltpu.roll(total, 64, 1), 4, 0))
+        out[pl.ds(base + n * 4, 4), :] = folded[0:4]
+
+
+def make_sketch_kernel(kinds):
     def kernel(rows, signs, *refs):
-        count = len(kinds)
-        blocks, out, both = refs[:count], refs[-2], refs[-1]
-        base = 0
-        for part in refs[count : count + earlier]:
-            size = part.shape[0]
-            out[pl.ds(base, size), :] = part[...]
-            base += size
-        half = tile_iota(0) < 4
-        lane = tile_iota(1)
-
-        def spread(y, carry):
-            for n, kind in enumerate(kinds):
-                for c in range(3):
-                    tile = blocks[n][y + 1, 1, c] if kind else blocks[n][y, c]
-                    both[n, y * 3 + c] = tile
-                    both[n, 48 + y * 3 + c] = pltpu.roll(tile, 4, 0)
-            return carry
-
-        lax.fori_loop(0, 16, spread, 0)
-
-        sums = [jnp.zeros((8, 128), F32)] * count
-        for j in range(64):
-            first = lax.shift_right_logical(rows[j], 7)
-            second = lax.shift_right_logical(rows[64 + j], 7)
-            second = jnp.where(second < 48, second + 48, second - 48)
-            sign = signs[j]
-            for n in range(count):
-                tile = jnp.where(half, both[n, first], both[n, second]) * sign
-                sums[n] = jnp.where(lane == j, jnp.sum(tile, axis=1, keepdims=True), sums[n])
-        for n in range(count):
-            folded = jnp.where(lane < 64, sums[n], pltpu.roll(pltpu.roll(sums[n], 64, 1), 4, 0))
-            out[pl.ds(base + n * 4, 4), :] = folded[0:4]
+        blocks = list(zip(refs[: len(kinds)], kinds))
+        sketch_blocks(blocks, rows, signs, refs[-1], refs[-2])
 
     return kernel
 
 
-def sketch(kinds, rows, signs, blocks, earlier=()):
-    size = 4 * len(kinds) + sum(part.shape[0] for part in earlier)
-    return pl.pallas_call(
-        make_sketch_kernel(kinds, len(earlier)),
-        out_shape=shaped(size, 128),
-        in_specs=[SMEM] + [VMEM] * (1 + len(kinds) + len(earlier)),
+def sketch(kinds, rows, signs, blocks):
+    return pl.pallas_call(
+        make_sketch_kernel(kinds),
+        out_shape=shaped(4 * len(kinds), 128),
+        in_specs=[SMEM] + [VMEM] * (1 + len(kinds)),
         out_specs=VMEM,
         scratch_shapes=[pltpu.VMEM((len(kinds), 96, 8, 128), F32)],
         compiler_params=PARAMS,
         name="sketch",
-    )(rows, signs, *blocks, *earlier)
+    )(rows, signs, *blocks)
 
 
 def dot(a, b):
@@ -613,22 +625,25 @@
     return out
 
 
-def fold(copies, count):
-    def kernel(parts, out):
-        total = parts[0]
-        for n in range(1, copies.shape[0]):
-            total = total + parts[n]
+def fold(count, *operands):
+    def kernel(*refs):
+        tables = []
+        for ref in refs[:-1]:
+            tables += [ref[...]] if len(ref.shape) == 2 else [ref[n] for n in range(ref.shape[0])]
+        total = tables[0]
+        for table in tables[1:]:
+            total = total + table
         for n in range(count):
-            out[n] = total
+            refs[-1][n] = total
 
     return pl.pallas_call(
         kernel,
-        out_shape=shaped(count, *copies.shape[1:]),
-        in_specs=[VMEM],
+        out_shape=shaped(count, 36, 128),
+        in_specs=[VMEM] * len(operands),
         out_specs=VMEM,
         compiler_params=PARAMS,
         name="fold",
-    )(copies)
+    )(*operands)
 
 
 def cycle(right_side, stencil, class_scale, material, boundary, sign_bits, sample_rows):
@@ -636,7 +651,7 @@
     flags = [lax.axis_index(axis) % 2 == 0 for axis in (GX, GY)]
     parity = jnp.stack([jnp.broadcast_to(flag.astype(F32), (8, 128)) for flag in flags])
     own, first, second, masked = prepare(
-        class_scale, parity, right_side.transpose(0, 1, 3, 2, 4), material, boundary
+        parity, class_scale, right_side.transpose(0, 1, 3, 2, 4), material, boundary
     )
     blocks = [own]
     sketches = []
@@ -707,16 +722,17 @@
             first_round,
             *shared,
             *(swap_c, swap_d, before, scale, scale_own, scale_far, *started),
+            tail=(rows, signs, *sketches) if turn == STEPS // 2 - 1 else (),
         )
         if first_round:
             scale_far = done[2]
         own = done[1]
         blocks += done[:2]
 
-    table = lax.psum(sketch((1, 0), rows, signs, blocks[-2:], sketches), "gy_1")
-    copies = jnp.broadcast_to(table, (16,) + table.shape)
-    copies = lax.all_to_all(copies, ("gx_0", "gy_0"), 0, 0, tiled=True)
-    copies = lax.all_to_all(fold(copies, 8), ("gx_1",), 0, 0, tiled=True)
+    table = done[2]
+    other = lax.ppermute(table, "gy_1", [(0, 1), (1, 0)])
+    copies = lax.all_to_all(fold(16, table, other), ("gx_0", "gy_0"), 0, 0, tiled=True)
+    copies = lax.all_to_all(fold(8, copies), ("gx_1",), 0, 0, tiled=True)
     iterate, remainder = finish(copies, interval, blocks)
     return iterate.transpose(0, 1, 3, 2, 4), remainder.transpose(0, 1, 3, 2, 4)
 

time: 122 us -> 116 us (0.951)
  blocking collectives: 34.2 us -> 30.1 us
  Pallas kernels: 35.8 us -> 33 us
    psum x1 -> x0, blocking collectives: 3.72 us -> none  [cycle(): table = lax.psum(sketch((1, 0), rows, signs, blocks[-2:], sketches), 'gy_1')]
    pallas_call x9, Pallas kernels: 11.2 us -> 8.94 us  [the longest x4 5.85 us: outer(): pl.pallas_call(make_outer_kernel(first_round, len(tail)), out_shape=(shap...]
  transfers between devices with their start and end apart: 16 -> 17, of which waited for: 4 -> 5; matrix products, arithmetic and copies ran while one was open for 0% -> 0% of each run, Pallas kernels for 16% -> 17%
where the time goes in v4:
time: 116 us; the launch traced here: 115 us
  starting transfers between devices  41.1 us (35%)
  Pallas kernels  33 us (28%)
  blocking collectives  30.1 us (26%)
  waiting for transfers between devices  7.96 us (7%)
  local copies, waits for them, and re-layouts  1.6 us (1%)
    ppermute x16, starting transfers between devices, swap(): out.append(lax.ppermute(operand, axis, pairs))  40.6 us
    all_to_all x1, blocking collectives, cycle(): lax.all_to_all(fold(16, table, other), ('gx_0', 'gy_0'), 0, 0, tiled=True)  18.7 us
    all_to_all x1, blocking collectives, cycle(): copies = lax.all_to_all(fold(8, copies), ('gx_1',), 0, 0, tiled=True)  11.4 us
    pallas_call x4, Pallas kernels, middle(): pl.pallas_call(make_middle_kernel(first_round), out_shape=(shaped(18, 3,...  9.97 us
    ppermute x16, waiting for transfers between devices, swap(): out.append(lax.ppermute(operand, axis, pairs))  7.12 us
    pallas_call x1, Pallas kernels, finish(): pl.pallas_call(finish_kernel, out_shape=(shaped(2, 16, 3, 4, 128), shaped...  6.19 us
    pallas_call x4, Pallas kernels, outer(): pl.pallas_call(make_outer_kernel(first_round, len(tail)), out_shape=(shap...  5.85 us
    pallas_call x4, Pallas kernels, inner(): pl.pallas_call(inner_kernel, out_shape=shaped(14, 3, 3, 8, 128), in_specs...  4.64 us
  transfers between devices with their start and end apart: 17, of which 5 were waited for; matrix products, arithmetic and copies ran while one was open for 0% of the time, Pallas kernels for 17%

profile of v4, /device:TPU:1, one launch (start us, length us, event | category | flops | bytes accessed | tf_op | source)
XLA Modules:
  0.0 114.9 jit_solution(8864202167362437204)
XLA Ops:
  0.7 0.1 stack.97.parity
  0.7 1.1 prepare.1
  1.9 2.5 %collective-permute-start = (f32[400,128]{1,0:T(8,128)S(1)}, f32[400,128]{1,0:T(8,128)S(1)}, u32[]{:S(2)}, u32[]{:S(2)}) collective-permute-start(f32[400,128]{1,0:T(8,128)S(1)} %get-tuple-element.46), channel_id=1, source_target_pairs={{0,8},{8,0},{16,24},{24,16},{32,40},{40,32},{48,56},{56,48},{64,72... | collective-permute-start | bytes 614408 | tf_op jit(solution)/shard_map/ppermute | solution.py:624
  4.4 0.7 collective-permute-start.1
  5.1 0.0 copy-done.3
  5.1 0.1 copy.20
  5.2 0.0 copy-start.2
  5.2 0.2 reshape.117.stencil
  5.4 0.5 copy-done.2
  5.9 1.0 setup.1
  6.9 1.2 %inner.4.part = f32[14,3,3,8,128]{4,3,2,1,0:T(8,128)S(1)} custom-call(f32[243,8,128]{2,1,0:T(8,128)S(1)} %get-tuple-element.44.coef, f32[16,3,8,128]{3,2,1,0:T(8,128)S(1)} %get-tuple-element.48.own.refs_0_.first), custom_call_target="tpu_custom_call" | custom-call | tf_op jit(solution)/shard_map/inner/pallas_call | solution.py:223
  8.0 0.1 collective-permute-done
  8.2 0.0 collective-permute-done.1
  8.3 0.0 copy-start
  8.3 5.3 %collective-permute-start.3 = (f32[152,128]{1,0:T(8,128)S(1)}, f32[152,128]{1,0:T(8,128)S(1)}, u32[]{:S(2)}, u32[]{:S(2)}) collective-permute-start(f32[152,128]{1,0:T(8,128)S(1)} %get-tuple-element.112), channel_id=1, source_target_pairs={{1,2},{2,1},{3,4},{4,3},{5,6},{6,5},{9,10},{10,9},{11,12},{12,11},... | collective-permute-start | bytes 233480 | tf_op jit(solution)/shard_map/ppermute | solution.py:624
  13.6 0.1 collective-permute-start.2
  13.7 0.0 copy-start.1
  13.7 0.6 copy-done.1
  14.4 1.2 %signs.1.refs_1_ = f32[64,8,128]{2,1,0:T(8,128)S(1)} custom-call(s32[128]{0:T(128)S(1)} %bitcast.90, s32[2,3,16,128]{3,2,1,0:T(8,128)S(1)} %bitcast.89), custom_call_target="tpu_custom_call" | custom-call | tf_op jit(solution)/shard_map/signs/pallas_call | solution.py:148
  15.7 2.5 %middle.4 = (f32[18,3,3,8,128]{4,3,2,1,0:T(8,128)S(1)}, f32[16,3,8,128]{3,2,1,0:T(8,128)S(1)}) custom-call(f32[243,8,128]{2,1,0:T(8,128)S(1)} %get-tuple-element.44.coef, f32[2,8,128]{2,1,0:T(8,128)S(1)} %get-tuple-element.45.interval.before.scale_far, f32[2,8,128]{2,1,0:T(8,128)S(1)} %stack.97.parity, f32[16,3,8,128]{3,2,1,0:T(8,128)S(1)} %bitcast.86, ...), custom_call_target="tpu_custom_call" | custom-call | tf_op jit(solution)/shard_map/middle/pallas_call | solution.py:314
  18.2 0.0 collective-permute-done.3.swap_d
  18.2 0.0 collective-permute-done.2.swap_c
  18.2 1.2 %outer.4 = (f32[18,3,3,8,128]{4,3,2,1,0:T(8,128)S(1)}, f32[16,3,8,128]{3,2,1,0:T(8,128)S(1)}, f32[2,2,8,128]{3,2,1,0:T(8,128)S(1)}) custom-call(f32[243,8,128]{2,1,0:T(8,128)S(1)} %get-tuple-element.44.coef, f32[2,8,128]{2,1,0:T(8,128)S(1)} %get-tuple-element.45.interval.before.scale_far, ...), custom_call_target="tpu_custom_call", output_to_operand_aliasing={{0}: (12, {}), {1}: (13, {})} | custom-call | tf_op jit(solution)/shard_map/outer/pallas_call | solution.py:421
  19.4 0.7 collective-permute-start.5
  20.1 7.9 %collective-permute-start.4 = (f32[16,3,8,128]{3,2,1,0:T(8,128)S(1)}, f32[16,3,8,128]{3,2,1,0:T(8,128)S(1)}, u32[]{:S(2)}, u32[]{:S(2)}) collective-permute-start(f32[16,3,8,128]{3,2,1,0:T(8,128)S(1)} %get-tuple-element.56.refs_2_.own.l0), channel_id=1, source_target_pairs={{0,8},{8,0},{16,24},{24,16},{32,40},{40,32},{48,56},{56,48},{64,72... | collective-permute-start | bytes 589832 | tf_op jit(solution)/shard_map/ppermute | solution.py:624
  28.0 1.2 %inner.5.part = f32[14,3,3,8,128]{4,3,2,1,0:T(8,128)S(1)} custom-call(f32[243,8,128]{2,1,0:T(8,128)S(1)} %get-tuple-element.44.coef, f32[16,3,8,128]{3,2,1,0:T(8,128)S(1)} %get-tuple-element.56.refs_2_.own.l0), custom_call_target="tpu_custom_call" | custom-call | tf_op jit(solution)/shard_map/inner/pallas_call | solution.py:223
  29.2 1.1 sketch.3.refs_2_
  30.2 0.0 collective-permute-done.5.swap_b
  30.2 2.3 %collective-permute-done.4.swap_a = f32[16,3,8,128]{3,2,1,0:T(8,128)S(1)} collective-permute-done((f32[16,3,8,128]{3,2,1,0:T(8,128)S(1)}, f32[16,3,8,128]{3,2,1,0:T(8,128)S(1)}, u32[]{:S(2)}, u32[]{:S(2)}) %collective-permute-start.4) | collective-permute-done | bytes 196640 | tf_op jit(solution)/shard_map/ppermute | solution.py:624
  32.6 4.4 %collective-permute-start.7 = (f32[3,2,3,8,128]{4,3,2,1,0:T(8,128)S(1)}, f32[3,2,3,8,128]{4,3,2,1,0:T(8,128)S(1)}, u32[]{:S(2)}, u32[]{:S(2)}) collective-permute-start(f32[3,2,3,8,128]{4,3,2,1,0:T(8,128)S(1)} %get-tuple-element.118), channel_id=1, source_target_pairs={{1,2},{2,1},{3,4},{4,3},{5,6},{6,5},{9,10},{10,9},{11,12},{12,11},... | collective-permute-start | bytes 221192 | tf_op jit(solution)/shard_map/ppermute | solution.py:624
  36.9 0.1 collective-permute-start.6
  37.0 2.5 %middle.5 = (f32[18,3,3,8,128]{4,3,2,1,0:T(8,128)S(1)}, f32[16,3,8,128]{3,2,1,0:T(8,128)S(1)}) custom-call(f32[243,8,128]{2,1,0:T(8,128)S(1)} %get-tuple-element.44.coef, f32[2,8,128]{2,1,0:T(8,128)S(1)} %get-tuple-element.45.interval.before.scale_far, f32[2,8,128]{2,1,0:T(8,128)S(1)} %stack.97.parity, f32[16,3,8,128]{3,2,1,0:T(8,128)S(1)} %collective-permute-done.4.swap_a, ...), custom_call_target="tpu_custom_call" | custom-call | tf_op jit(solution)/shard_map/middle/pallas_call | solution.py:314
  39.5 0.0 collective-permute-done.7.swap_d
  39.5 0.0 collective-permute-done.6.swap_c
  39.5 1.2 %outer.5 = (f32[18,3,3,8,128]{4,3,2,1,0:T(8,128)S(1)}, f32[16,3,8,128]{3,2,1,0:T(8,128)S(1)}) custom-call(f32[243,8,128]{2,1,0:T(8,128)S(1)} %get-tuple-element.44.coef, f32[2,8,128]{2,1,0:T(8,128)S(1)} %get-tuple-element.45.interval.before.scale_far, f32[2,8,128]{2,1,0:T(8,128)S(1)} %stack.97.parity, ...), custom_call_target="tpu_custom_call", output_to_operand_aliasing={{0}: (12, {}), {1}: (13, {})} | custom-call | tf_op jit(solution)/shard_map/outer/pallas_call | solution.py:421
  40.7 0.7 collective-permute-start.9
  41.4 6.1 %collective-permute-start.8 = (f32[16,3,8,128]{3,2,1,0:T(8,128)S(1)}, f32[16,3,8,128]{3,2,1,0:T(8,128)S(1)}, u32[]{:S(2)}, u32[]{:S(2)}) collective-permute-start(f32[16,3,8,128]{3,2,1,0:T(8,128)S(1)} %get-tuple-element.64.refs_1_.own.l1), channel_id=1, source_target_pairs={{0,8},{8,0},{16,24},{24,16},{32,40},{40,32},{48,56},{56,48},{64,72... | collective-permute-start | bytes 589832 | tf_op jit(solution)/shard_map/ppermute | solution.py:624
  47.5 1.2 %inner.6.part = f32[14,3,3,8,128]{4,3,2,1,0:T(8,128)S(1)} custom-call(f32[243,8,128]{2,1,0:T(8,128)S(1)} %get-tuple-element.44.coef, f32[16,3,8,128]{3,2,1,0:T(8,128)S(1)} %get-tuple-element.64.refs_1_.own.l1), custom_call_target="tpu_custom_call" | custom-call | tf_op jit(solution)/shard_map/inner/pallas_call | solution.py:223
  48.7 1.0 sketch.4.refs_3_
  49.7 0.0 collective-permute-done.9.swap_b
  49.7 2.3 %collective-permute-done.8.swap_a = f32[16,3,8,128]{3,2,1,0:T(8,128)S(1)} collective-permute-done((f32[16,3,8,128]{3,2,1,0:T(8,128)S(1)}, f32[16,3,8,128]{3,2,1,0:T(8,128)S(1)}, u32[]{:S(2)}, u32[]{:S(2)}) %collective-permute-start.8) | collective-permute-done | bytes 196640 | tf_op jit(solution)/shard_map/ppermute | solution.py:624
  52.1 4.1 %collective-permute-start.11 = (f32[3,2,3,8,128]{4,3,2,1,0:T(8,128)S(1)}, f32[3,2,3,8,128]{4,3,2,1,0:T(8,128)S(1)}, u32[]{:S(2)}, u32[]{:S(2)}) collective-permute-start(f32[3,2,3,8,128]{4,3,2,1,0:T(8,128)S(1)} %get-tuple-element.116), channel_id=1, source_target_pairs={{1,2},{2,1},{3,4},{4,3},{5,6},{6,5},{9,10},{10,9},{11,12},{12,11},... | collective-permute-start | bytes 221192 | tf_op jit(solution)/shard_map/ppermute | solution.py:624
  56.2 0.1 collective-permute-start.10
  56.3 2.5 %middle.6 = (f32[18,3,3,8,128]{4,3,2,1,0:T(8,128)S(1)}, f32[16,3,8,128]{3,2,1,0:T(8,128)S(1)}) custom-call(f32[243,8,128]{2,1,0:T(8,128)S(1)} %get-tuple-element.44.coef, f32[2,8,128]{2,1,0:T(8,128)S(1)} %get-tuple-element.45.interval.before.scale_far, f32[2,8,128]{2,1,0:T(8,128)S(1)} %stack.97.parity, f32[16,3,8,128]{3,2,1,0:T(8,128)S(1)} %collective-permute-done.8.swap_a, ...), custom_call_target="tpu_custom_call" | custom-call | tf_op jit(solution)/shard_map/middle/pallas_call | solution.py:314
  58.8 0.0 collective-permute-done.11.swap_d
  58.8 0.0 collective-permute-done.10.swap_c
  58.8 1.2 %outer.6 = (f32[18,3,3,8,128]{4,3,2,1,0:T(8,128)S(1)}, f32[16,3,8,128]{3,2,1,0:T(8,128)S(1)}) custom-call(f32[243,8,128]{2,1,0:T(8,128)S(1)} %get-tuple-element.44.coef, f32[2,8,128]{2,1,0:T(8,128)S(1)} %get-tuple-element.45.interval.before.scale_far, f32[2,8,128]{2,1,0:T(8,128)S(1)} %stack.97.parity, ...), custom_call_target="tpu_custom_call", output_to_operand_aliasing={{0}: (12, {}), {1}: (13, {})} | custom-call | tf_op jit(solution)/shard_map/outer/pallas_call | solution.py:421
  60.0 0.7 collective-permute-start.13
  60.7 3.9 %collective-permute-start.12 = (f32[16,3,8,128]{3,2,1,0:T(8,128)S(1)}, f32[16,3,8,128]{3,2,1,0:T(8,128)S(1)}, u32[]{:S(2)}, u32[]{:S(2)}) collective-permute-start(f32[16,3,8,128]{3,2,1,0:T(8,128)S(1)} %get-tuple-element.71.refs_1_.own.l2), channel_id=1, source_target_pairs={{0,8},{8,0},{16,24},{24,16},{32,40},{40,32},{48,56},{56,48},{64,72... | collective-permute-start | bytes 589832 | tf_op jit(solution)/shard_map/ppermute | solution.py:624
  64.6 1.2 %inner.7.part = f32[14,3,3,8,128]{4,3,2,1,0:T(8,128)S(1)} custom-call(f32[243,8,128]{2,1,0:T(8,128)S(1)} %get-tuple-element.44.coef, f32[16,3,8,128]{3,2,1,0:T(8,128)S(1)} %get-tuple-element.71.refs_1_.own.l2), custom_call_target="tpu_custom_call" | custom-call | tf_op jit(solution)/shard_map/inner/pallas_call | solution.py:223
  65.7 1.0 sketch.5.refs_4_
  66.7 0.0 collective-permute-done.13.swap_b
  66.7 2.3 %collective-permute-done.12.swap_a = f32[16,3,8,128]{3,2,1,0:T(8,128)S(1)} collective-permute-done((f32[16,3,8,128]{3,2,1,0:T(8,128)S(1)}, f32[16,3,8,128]{3,2,1,0:T(8,128)S(1)}, u32[]{:S(2)}, u32[]{:S(2)}) %collective-permute-start.12) | collective-permute-done | bytes 196640 | tf_op jit(solution)/shard_map/ppermute | solution.py:624
  69.1 3.3 %collective-permute-start.15 = (f32[3,2,3,8,128]{4,3,2,1,0:T(8,128)S(1)}, f32[3,2,3,8,128]{4,3,2,1,0:T(8,128)S(1)}, u32[]{:S(2)}, u32[]{:S(2)}) collective-permute-start(f32[3,2,3,8,128]{4,3,2,1,0:T(8,128)S(1)} %get-tuple-element.114), channel_id=1, source_target_pairs={{1,2},{2,1},{3,4},{4,3},{5,6},{6,5},{9,10},{10,9},{11,12},{12,11},... | collective-permute-start | bytes 221192 | tf_op jit(solution)/shard_map/ppermute | solution.py:624
  72.5 0.1 collective-permute-start.14
  72.6 2.5 %middle.7 = (f32[18,3,3,8,128]{4,3,2,1,0:T(8,128)S(1)}, f32[16,3,8,128]{3,2,1,0:T(8,128)S(1)}) custom-call(f32[243,8,128]{2,1,0:T(8,128)S(1)} %get-tuple-element.44.coef, f32[2,8,128]{2,1,0:T(8,128)S(1)} %get-tuple-element.45.interval.before.scale_far, f32[2,8,128]{2,1,0:T(8,128)S(1)} %stack.97.parity, f32[16,3,8,128]{3,2,1,0:T(8,128)S(1)} %collective-permute-done.12.swap_a, ...), custom_call_target="tpu_custom_call" | custom-call | tf_op jit(solution)/shard_map/middle/pallas_call | solution.py:314
  75.1 0.0 collective-permute-done.15.swap_d
  75.1 0.0 collective-permute-done.14.swap_c
  75.1 2.2 %outer.7 = (f32[18,3,3,8,128]{4,3,2,1,0:T(8,128)S(1)}, f32[16,3,8,128]{3,2,1,0:T(8,128)S(1)}, f32[36,128]{1,0:T(8,128)S(1)}) custom-call(f32[243,8,128]{2,1,0:T(8,128)S(1)} %get-tuple-element.44.coef, f32[2,8,128]{2,1,0:T(8,128)S(1)} %get-tuple-element.45.interval.before.scale_far, ...), custom_call_target="tpu_custom_call", output_to_operand_aliasing={{0}: (12, {}), {1}: (13, {})} | custom-call | tf_op jit(solution)/shard_map/outer/pallas_call | solution.py:421
  77.3 0.5 collective-permute-start.16
  77.8 0.8 collective-permute-done.16.refs_1_
  78.6 18.7 %all_to_all.10.refs_0_ = f32[16,36,128]{2,1,0:T(8,128)S(1)} all-to-all(f32[16,36,128]{2,1,0:T(8,128)S(1)} %fold.2), channel_id=1, replica_groups=mesh['gx_0'=4,'gx_1'=8,'gy_0'=4,'gy_1'=2] {'gx_0','gy_0'}, dimensions={0} | all-to-all | bytes 589824 | tf_op jit(solution)/shard_map/all_to_all | solution.py:734
  97.4 11.4 %all_to_all.11.table = f32[8,36,128]{2,1,0:T(8,128)S(1)} all-to-all(f32[8,36,128]{2,1,0:T(8,128)S(1)} %fold.3), channel_id=1, replica_groups=mesh['gx_0'=4,'gx_1'=8,'gy_0'=4,'gy_1'=2] {'gx_1'}, dimensions={0} | all-to-all | bytes 294912 | tf_op jit(solution)/shard_map/all_to_all | solution.py:735
  108.8 6.2 %finish.1 = (f32[2,16,3,4,128]{4,3,2,1,0:T(4,128)}, f32[2,16,3,4,128]{4,3,2,1,0:T(4,128)}) custom-call(f32[8,36,128]{2,1,0:T(8,128)S(1)} %all_to_all.11.table, f32[2,8,128]{2,1,0:T(8,128)S(1)} %get-tuple-element.45.interval.before.scale_far, f32[16,3,8,128]{3,2,1,0:T(8,128)S(1)} %get-tuple-element.48.own.refs_0_.first, ...), custom_call_target="tpu_custom_call" | custom-call | tf_op jit(solution)/shard_map/finish/pallas_call | solution.py:608
  (27 shorter events, 0.3 us)
Async XLA Ops:
  0.7 4.3 %copy-start.3 = (f32[27,3,3]{0,2,1:T(4,128)S(1)}, f32[27,3,3]{0,2,1:T(4,128)}, u32[]{:S(2)}) copy-start(f32[27,3,3]{0,2,1:T(4,128)} %param.8) | copy-start | bytes 2920
  1.9 6.3 %collective-permute-start = (f32[400,128]{1,0:T(8,128)S(1)}, f32[400,128]{1,0:T(8,128)S(1)}, u32[]{:S(2)}, u32[]{:S(2)}) collective-permute-start(f32[400,128]{1,0:T(8,128)S(1)} %get-tuple-element.46), channel_id=1, source_target_pairs={{0,8},{8,0},{16,24},{24,16},{32,40},{40,32},{48,56},{56,48},{64,72... | collective-permute-start | bytes 614408 | tf_op jit(solution)/shard_map/ppermute | solution.py:624
  4.4 3.8 %collective-permute-start.1 = (f32[400,128]{1,0:T(8,128)S(1)}, f32[400,128]{1,0:T(8,128)S(1)}, u32[]{:S(2)}, u32[]{:S(2)}) collective-permute-start(f32[400,128]{1,0:T(8,128)S(1)} %get-tuple-element.47), channel_id=1, source_target_pairs={{8,16},{16,8},{24,32},{32,24},{40,48},{48,40},{56,64},{64,56},{72,... | collective-permute-start | bytes 614408 | tf_op jit(solution)/shard_map/ppermute | solution.py:624
  5.2 0.7 copy-start.2
  8.3 5.4 %copy-start = (s32[2,16,3,128]{3,1,2,0:T(8,128)S(1)}, s32[2,16,3,128]{3,1,2,0:T(8,128)}, u32[]{:S(2)}) copy-start(s32[2,16,3,128]{3,1,2,0:T(8,128)} %param.12) | copy-start | bytes 147460
  8.3 9.9 %collective-permute-start.3 = (f32[152,128]{1,0:T(8,128)S(1)}, f32[152,128]{1,0:T(8,128)S(1)}, u32[]{:S(2)}, u32[]{:S(2)}) collective-permute-start(f32[152,128]{1,0:T(8,128)S(1)} %get-tuple-element.112), channel_id=1, source_target_pairs={{1,2},{2,1},{3,4},{4,3},{5,6},{6,5},{9,10},{10,9},{11,12},{12,11},... | collective-permute-start | bytes 233480 | tf_op jit(solution)/shard_map/ppermute | solution.py:624
  13.6 4.6 %collective-permute-start.2 = (f32[152,128]{1,0:T(8,128)S(1)}, f32[152,128]{1,0:T(8,128)S(1)}, u32[]{:S(2)}, u32[]{:S(2)}) collective-permute-start(f32[152,128]{1,0:T(8,128)S(1)} %get-tuple-element.113), channel_id=1, source_target_pairs={{0,1},{1,0},{2,3},{3,2},{4,5},{5,4},{6,7},{7,6},{8,9},{9,8},{10,11... | collective-permute-start | bytes 233480 | tf_op jit(solution)/shard_map/ppermute | solution.py:624
  13.7 0.7 copy-start.1
  19.4 10.8 %collective-permute-start.5 = (f32[16,3,8,128]{3,2,1,0:T(8,128)S(1)}, f32[16,3,8,128]{3,2,1,0:T(8,128)S(1)}, u32[]{:S(2)}, u32[]{:S(2)}) collective-permute-start(f32[16,3,8,128]{3,2,1,0:T(8,128)S(1)} %get-tuple-element.56.refs_2_.own.l0), channel_id=1, source_target_pairs={{8,16},{16,8},{24,32},{32,24},{40,48},{48,40},{56,64},{64,56},{72,... | collective-permute-start | bytes 589832 | tf_op jit(solution)/shard_map/ppermute | solution.py:624
  20.1 12.4 %collective-permute-start.4 = (f32[16,3,8,128]{3,2,1,0:T(8,128)S(1)}, f32[16,3,8,128]{3,2,1,0:T(8,128)S(1)}, u32[]{:S(2)}, u32[]{:S(2)}) collective-permute-start(f32[16,3,8,128]{3,2,1,0:T(8,128)S(1)} %get-tuple-element.56.refs_2_.own.l0), channel_id=1, source_target_pairs={{0,8},{8,0},{16,24},{24,16},{32,40},{40,32},{48,56},{56,48},{64,72... | collective-permute-start | bytes 589832 | tf_op jit(solution)/shard_map/ppermute | solution.py:624
  32.6 7.0 %collective-permute-start.7 = (f32[3,2,3,8,128]{4,3,2,1,0:T(8,128)S(1)}, f32[3,2,3,8,128]{4,3,2,1,0:T(8,128)S(1)}, u32[]{:S(2)}, u32[]{:S(2)}) collective-permute-start(f32[3,2,3,8,128]{4,3,2,1,0:T(8,128)S(1)} %get-tuple-element.118), channel_id=1, source_target_pairs={{1,2},{2,1},{3,4},{4,3},{5,6},{6,5},{9,10},{10,9},{11,12},{12,11},... | collective-permute-start | bytes 221192 | tf_op jit(solution)/shard_map/ppermute | solution.py:624
  36.9 2.6 %collective-permute-start.6 = (f32[3,2,3,8,128]{4,3,2,1,0:T(8,128)S(1)}, f32[3,2,3,8,128]{4,3,2,1,0:T(8,128)S(1)}, u32[]{:S(2)}, u32[]{:S(2)}) collective-permute-start(f32[3,2,3,8,128]{4,3,2,1,0:T(8,128)S(1)} %get-tuple-element.119), channel_id=1, source_target_pairs={{0,1},{1,0},{2,3},{3,2},{4,5},{5,4},{6,7},{7,6},{8,9},{9,8},{10,11... | collective-permute-start | bytes 221192 | tf_op jit(solution)/shard_map/ppermute | solution.py:624
  40.7 9.0 %collective-permute-start.9 = (f32[16,3,8,128]{3,2,1,0:T(8,128)S(1)}, f32[16,3,8,128]{3,2,1,0:T(8,128)S(1)}, u32[]{:S(2)}, u32[]{:S(2)}) collective-permute-start(f32[16,3,8,128]{3,2,1,0:T(8,128)S(1)} %get-tuple-element.64.refs_1_.own.l1), channel_id=1, source_target_pairs={{8,16},{16,8},{24,32},{32,24},{40,48},{48,40},{56,64},{64,56},{72,... | collective-permute-start | bytes 589832 | tf_op jit(solution)/shard_map/ppermute | solution.py:624
  41.4 10.6 %collective-permute-start.8 = (f32[16,3,8,128]{3,2,1,0:T(8,128)S(1)}, f32[16,3,8,128]{3,2,1,0:T(8,128)S(1)}, u32[]{:S(2)}, u32[]{:S(2)}) collective-permute-start(f32[16,3,8,128]{3,2,1,0:T(8,128)S(1)} %get-tuple-element.64.refs_1_.own.l1), channel_id=1, source_target_pairs={{0,8},{8,0},{16,24},{24,16},{32,40},{40,32},{48,56},{56,48},{64,72... | collective-permute-start | bytes 589832 | tf_op jit(solution)/shard_map/ppermute | solution.py:624
  52.1 6.7 %collective-permute-start.11 = (f32[3,2,3,8,128]{4,3,2,1,0:T(8,128)S(1)}, f32[3,2,3,8,128]{4,3,2,1,0:T(8,128)S(1)}, u32[]{:S(2)}, u32[]{:S(2)}) collective-permute-start(f32[3,2,3,8,128]{4,3,2,1,0:T(8,128)S(1)} %get-tuple-element.116), channel_id=1, source_target_pairs={{1,2},{2,1},{3,4},{4,3},{5,6},{6,5},{9,10},{10,9},{11,12},{12,11},... | collective-permute-start | bytes 221192 | tf_op jit(solution)/shard_map/ppermute | solution.py:624
  56.2 2.6 %collective-permute-start.10 = (f32[3,2,3,8,128]{4,3,2,1,0:T(8,128)S(1)}, f32[3,2,3,8,128]{4,3,2,1,0:T(8,128)S(1)}, u32[]{:S(2)}, u32[]{:S(2)}) collective-permute-start(f32[3,2,3,8,128]{4,3,2,1,0:T(8,128)S(1)} %get-tuple-element.117), channel_id=1, source_target_pairs={{0,1},{1,0},{2,3},{3,2},{4,5},{5,4},{6,7},{7,6},{8,9},{9,8},{10,11... | collective-permute-start | bytes 221192 | tf_op jit(solution)/shard_map/ppermute | solution.py:624
  60.0 6.7 %collective-permute-start.13 = (f32[16,3,8,128]{3,2,1,0:T(8,128)S(1)}, f32[16,3,8,128]{3,2,1,0:T(8,128)S(1)}, u32[]{:S(2)}, u32[]{:S(2)}) collective-permute-start(f32[16,3,8,128]{3,2,1,0:T(8,128)S(1)} %get-tuple-element.71.refs_1_.own.l2), channel_id=1, source_target_pairs={{8,16},{16,8},{24,32},{32,24},{40,48},{48,40},{56,64},{64,56},{72,... | collective-permute-start | bytes 589832 | tf_op jit(solution)/shard_map/ppermute | solution.py:624
  60.7 8.4 %collective-permute-start.12 = (f32[16,3,8,128]{3,2,1,0:T(8,128)S(1)}, f32[16,3,8,128]{3,2,1,0:T(8,128)S(1)}, u32[]{:S(2)}, u32[]{:S(2)}) collective-permute-start(f32[16,3,8,128]{3,2,1,0:T(8,128)S(1)} %get-tuple-element.71.refs_1_.own.l2), channel_id=1, source_target_pairs={{0,8},{8,0},{16,24},{24,16},{32,40},{40,32},{48,56},{56,48},{64,72... | collective-permute-start | bytes 589832 | tf_op jit(solution)/shard_map/ppermute | solution.py:624
  69.1 6.0 %collective-permute-start.15 = (f32[3,2,3,8,128]{4,3,2,1,0:T(8,128)S(1)}, f32[3,2,3,8,128]{4,3,2,1,0:T(8,128)S(1)}, u32[]{:S(2)}, u32[]{:S(2)}) collective-permute-start(f32[3,2,3,8,128]{4,3,2,1,0:T(8,128)S(1)} %get-tuple-element.114), channel_id=1, source_target_pairs={{1,2},{2,1},{3,4},{4,3},{5,6},{6,5},{9,10},{10,9},{11,12},{12,11},... | collective-permute-start | bytes 221192 | tf_op jit(solution)/shard_map/ppermute | solution.py:624
  72.5 2.6 %collective-permute-start.14 = (f32[3,2,3,8,128]{4,3,2,1,0:T(8,128)S(1)}, f32[3,2,3,8,128]{4,3,2,1,0:T(8,128)S(1)}, u32[]{:S(2)}, u32[]{:S(2)}) collective-permute-start(f32[3,2,3,8,128]{4,3,2,1,0:T(8,128)S(1)} %get-tuple-element.115), channel_id=1, source_target_pairs={{0,1},{1,0},{2,3},{3,2},{4,5},{5,4},{6,7},{7,6},{8,9},{9,8},{10,11... | collective-permute-start | bytes 221192 | tf_op jit(solution)/shard_map/ppermute | solution.py:624
  77.3 1.3 %collective-permute-start.16 = (f32[36,128]{1,0:T(8,128)S(1)}, f32[36,128]{1,0:T(8,128)S(1)}, u32[]{:S(2)}, u32[]{:S(2)}) collective-permute-start(f32[36,128]{1,0:T(8,128)S(1)} %get-tuple-element.81.refs_0_), channel_id=1, source_target_pairs={{0,1},{1,0},{2,3},{3,2},{4,5},{5,4},{6,7},{7,6},{8,9},{9,8},{10,11... | collective-permute-start | bytes 55304 | tf_op jit(solution)/shard_map/ppermute | solution.py:733

commit v5 on v4

--- a/solution.py
+++ b/solution.py
@@ -9,8 +9,8 @@
 from jax.sharding import PartitionSpec as P
 
 STEPS = 8
-AXES = ("gx_0", "gx_1", "gy_0", "gy_1")
-GX = ("gx_0", "gx_1")
+AXES = ("gx_0", "gx_1", "gx_2", "gy_0", "gy_1")
+GX = ("gx_0", "gx_1", "gx_2")
 GY = ("gy_0", "gy_1")
 
 VMEM = pl.BlockSpec(memory_space=pltpu.VMEM)
@@ -505,50 +505,52 @@
         )
 
     rhs = jnp.where(live, table[0:8], 0.0)
-    norms = jnp.sqrt(sum_lanes(rhs * rhs) + 1e-06)
-    basis = rhs / norms
-    coords = jnp.where(live & (lane == row), 1.0, 0.0) / norms
+    tall_row = lax.broadcasted_iota(jnp.int32, (40, 128), 0)
+    tall_lane = lax.broadcasted_iota(jnp.int32, (40, 128), 1)
+    lower = jnp.concatenate([table[4:8], table[0:36]], axis=0)
+    upper = jnp.concatenate([table[4:40], table[0:4]], axis=0)
+    vectors = shift[0:1] * table + (0.5 * reach[0:1]) * (lower + upper)
+    rhs_rows = jnp.concatenate([rhs, rhs, rhs, rhs, rhs], axis=0)
+    vectors = jnp.where(tall_row < 32, vectors, rhs_rows)
+
+    image_table = jnp.where(tall_row < 32, vectors, 0.0)
+    scaling = lax.rsqrt(sum_lanes(rhs * rhs) + 1e-06)
+    basis = rhs * scaling
+    coords = jnp.where(live & (lane == row), 1.0, 0.0) * scaling
     leading = jnp.sum(jnp.where(lane == row, coords, 0.0), axis=0, keepdims=True)
     for k in range(STEPS - 1):
-        moved = move(coords)
-        image = dot(moved[:, 0:40], table)
-        rest, next_coords = image, moved
+        image = dot(coords[:, 0:40], image_table)
+        rest, next_coords = image, move(coords)
         for i in range(4):
             weight = sum_lanes(image * basis[i : i + 1])
             rest = rest - weight * basis[i : i + 1]
             next_coords = next_coords - weight * coords[i : i + 1]
-        norms = jnp.sqrt(sum_lanes(rest * rest) + 1e-06)
-        basis = rest / norms
-        coords = next_coords / norms
+        scaling = lax.rsqrt(sum_lanes(rest * rest) + 1e-06)
+        basis = rest * scaling
+        coords = next_coords * scaling
         leading = leading + jnp.sum(
             jnp.where(live & (lane == row + 4 * (k + 1)), coords, 0.0), axis=0, keepdims=True
         )
 
-    tall_row = lax.broadcasted_iota(jnp.int32, (40, 128), 0)
-    tall_lane = lax.broadcasted_iota(jnp.int32, (40, 128), 1)
-    wide = shift[0:1]
-    part = 0.5 * reach[0:1]
-    lower = jnp.concatenate([table[4:8], table[0:36]], axis=0)
-    upper = jnp.concatenate([table[4:40], table[0:4]], axis=0)
-    vectors = wide * table + part * (lower + upper)
-    rhs_rows = jnp.concatenate([rhs, rhs, rhs, rhs, rhs], axis=0)
-    vectors = jnp.where(tall_row < 32, vectors, rhs_rows)
-
     combos = jnp.where(tall_row == tall_lane, 1.0, 0.0)
     found = jnp.zeros((8, 128), F32)
-    sizes = jnp.zeros((1, 128), F32)
+    sizes = jnp.ones((1, 128), F32)
     for j in range(4 * STEPS):
         pivot = vectors[j : j + 1]
         products = sum_lanes(vectors * pivot)
         size = products[j : j + 1]
-        ratio = products / (size + 1e-37)
+        ratio = products * (1.0 / (size + 1e-37))
         found = jnp.where(lane == j, ratio[32:40], found)
         sizes = jnp.where(lane[0:1] == j, size, sizes)
-        later = jnp.where(tall_row > j, ratio, 0.0)
-        vectors = vectors - later * pivot
-        combos = combos - later * combos[j : j + 1]
+        tail = j // 8 * 8
+        later = jnp.where(tall_row[tail:] > j, ratio[tail:], 0.0)
+        rest = vectors[tail:] - later * pivot
+        more = combos[tail:] - later * combos[j : j + 1]
+        vectors = jnp.concatenate([vectors[:tail], rest], axis=0) if tail else rest
+        combos = jnp.concatenate([combos[:tail], more], axis=0) if tail else more
     scaled = sizes * leading * leading
-    found = jnp.where(live, found * (scaled / (scaled + 1e-06)), 0.0)
+    shrink = scaled / (scaled + 1e-06)
+    found = jnp.where(live & (lane < 4 * STEPS), found * shrink, 0.0)
     return move, dot(found[:, 0:40], combos)
 
 
@@ -579,6 +581,8 @@
 
     refs = [(first, 0), (m0, 1), (l0, 0), (m1, 1), (l1, 0), (m2, 1), (l2, 0), (m3, 1), (l3, 0)]
 
+    turns = [row - sub + (sub + r) % 4 for r in range(4)]
+
     def one_row(y, carry):
         for c in range(3):
             total = None
@@ -586,12 +590,7 @@
             for k, (ref, kind) in enumerate(refs):
                 tile = ref[y + 1, 1, c] if kind else ref[y, c]
                 for r in range(4):
-                    if r:
-                        turned = jnp.where(
-                            sub < 4 - r, pltpu.roll(tile, 8 - r, 0), pltpu.roll(tile, 4 - r, 0)
-                        )
-                    else:
-                        turned = tile
+                    turned = jnp.take_along_axis(tile, turns[r], axis=0) if r else tile
                     if k < STEPS:
                         part = mix[0, k * 4 + r] * turned
                         total = part if total is None else total + part
@@ -730,15 +729,19 @@
         blocks += done[:2]
 
     table = done[2]
-    other = lax.ppermute(table, "gy_1", [(0, 1), (1, 0)])
-    copies = lax.all_to_all(fold(16, table, other), ("gx_0", "gy_0"), 0, 0, tiled=True)
-    copies = lax.all_to_all(fold(8, copies), ("gx_1",), 0, 0, tiled=True)
+    for axis in ("gy_1", "gx_2"):
+        other = lax.ppermute(table, axis, [(0, 1), (1, 0)])
+        count = 1 if axis == "gy_1" else 16
+        copies = fold(count, table, other)
+        table = copies.reshape(table.shape) if count == 1 else copies
+    copies = lax.all_to_all(table, ("gx_0", "gy_0"), 0, 0, tiled=True)
+    copies = lax.all_to_all(fold(4, copies), ("gx_1",), 0, 0, tiled=True)
     iterate, remainder = finish(copies, interval, blocks)
     return iterate.transpose(0, 1, 3, 2, 4), remainder.transpose(0, 1, 3, 2, 4)
 
 
 def solution(mesh):
-    split = Mesh(mesh.devices.reshape(4, 8, 4, 2), AXES)
+    split = Mesh(mesh.devices.reshape(4, 4, 2, 4, 2), AXES)
     return jax.shard_map(
         cycle,
         mesh=split,

time: 116 us -> 118 us (1.017)
  the two profiles are of different devices: /device:TPU:1 before, /device:TPU:32 now
where the time goes in v5:
time: 118 us; the launch traced here: 117 us
  Pallas kernels  32.4 us (27%)
  starting transfers between devices  32 us (27%)
  blocking collectives  30.6 us (26%)
  waiting for transfers between devices  19.5 us (17%)
  local copies, waits for them, and re-layouts  1.61 us (1%)
    ppermute x16, starting transfers between devices, swap(): out.append(lax.ppermute(operand, axis, pairs))  31.7 us
    all_to_all x1, blocking collectives, cycle(): copies = lax.all_to_all(table, ('gx_0', 'gy_0'), 0, 0, tiled=True)  17.7 us
    ppermute x16, waiting for transfers between devices, swap(): out.append(lax.ppermute(operand, axis, pairs))  14.8 us
    all_to_all x1, blocking collectives, cycle(): copies = lax.all_to_all(fold(4, copies), ('gx_1',), 0, 0, tiled=True)  12.9 us
    pallas_call x4, Pallas kernels, middle(): pl.pallas_call(make_middle_kernel(first_round), out_shape=(shaped(18, 3,...  9.93 us
    pallas_call x4, Pallas kernels, outer(): pl.pallas_call(make_outer_kernel(first_round, len(tail)), out_shape=(shap...  5.85 us
    pallas_call x1, Pallas kernels, finish(): pl.pallas_call(finish_kernel, out_shape=(shaped(2, 16, 3, 4, 128), shaped...  5.51 us
    pallas_call x4, Pallas kernels, inner(): pl.pallas_call(inner_kernel, out_shape=shaped(14, 3, 3, 8, 128), in_specs...  4.69 us
  transfers between devices with their start and end apart: 18, of which 9 were waited for; matrix products, arithmetic and copies ran while one was open for 0% of the time, Pallas kernels for 17%

profile of v5, /device:TPU:32, one launch (start us, length us, event | category | flops | bytes accessed | tf_op | source)
XLA Modules:
  0.0 117.2 jit_solution(11151594351303135775)
XLA Ops:
  0.7 0.1 stack.97.parity
  0.7 1.1 prepare.1
  1.9 1.9 %collective-permute-start = (f32[400,128]{1,0:T(8,128)S(1)}, f32[400,128]{1,0:T(8,128)S(1)}, u32[]{:S(2)}, u32[]{:S(2)}) collective-permute-start(f32[400,128]{1,0:T(8,128)S(1)} %get-tuple-element.46), channel_id=1, source_target_pairs={{0,8},{8,0},{16,24},{24,16},{32,40},{40,32},{48,56},{56,48},{64,72... | collective-permute-start | bytes 614408 | tf_op jit(solution)/shard_map/ppermute | solution.py:623
  3.8 3.9 %collective-permute-start.1 = (f32[400,128]{1,0:T(8,128)S(1)}, f32[400,128]{1,0:T(8,128)S(1)}, u32[]{:S(2)}, u32[]{:S(2)}) collective-permute-start(f32[400,128]{1,0:T(8,128)S(1)} %get-tuple-element.47), channel_id=1, source_target_pairs={{8,16},{16,8},{24,32},{32,24},{40,48},{48,40},{56,64},{64,56},{72,... | collective-permute-start | bytes 614408 | tf_op jit(solution)/shard_map/ppermute | solution.py:623
  7.7 0.1 copy.20
  7.8 0.0 copy-start.2
  7.8 0.2 reshape.120.stencil
  8.0 0.5 copy-done.2
  8.5 1.0 setup.1
  9.5 1.2 inner.4.part
  10.7 0.0 collective-permute-done
  10.7 1.8 %collective-permute-done.1 = f32[400,128]{1,0:T(8,128)S(1)} collective-permute-done((f32[400,128]{1,0:T(8,128)S(1)}, f32[400,128]{1,0:T(8,128)S(1)}, u32[]{:S(2)}, u32[]{:S(2)}) %collective-permute-start.1) | collective-permute-done | bytes 204832 | tf_op jit(solution)/shard_map/ppermute | solution.py:623
  12.6 0.0 copy-start
  12.6 0.7 collective-permute-start.3
  13.3 2.9 %collective-permute-start.2 = (f32[152,128]{1,0:T(8,128)S(1)}, f32[152,128]{1,0:T(8,128)S(1)}, u32[]{:S(2)}, u32[]{:S(2)}) collective-permute-start(f32[152,128]{1,0:T(8,128)S(1)} %get-tuple-element.113), channel_id=1, source_target_pairs={{0,1},{1,0},{2,3},{3,2},{4,5},{5,4},{6,7},{7,6},{8,9},{9,8},{10,11... | collective-permute-start | bytes 233480 | tf_op jit(solution)/shard_map/ppermute | solution.py:623
  16.2 0.7 copy-done.1
  16.9 1.2 %signs.1.refs_1_ = f32[64,8,128]{2,1,0:T(8,128)S(1)} custom-call(s32[128]{0:T(128)S(1)} %bitcast.93, s32[2,3,16,128]{3,2,1,0:T(8,128)S(1)} %bitcast.92), custom_call_target="tpu_custom_call" | custom-call | tf_op jit(solution)/shard_map/signs/pallas_call | solution.py:148
  18.2 2.5 %middle.4 = (f32[18,3,3,8,128]{4,3,2,1,0:T(8,128)S(1)}, f32[16,3,8,128]{3,2,1,0:T(8,128)S(1)}) custom-call(f32[243,8,128]{2,1,0:T(8,128)S(1)} %get-tuple-element.44.coef, f32[2,8,128]{2,1,0:T(8,128)S(1)} %get-tuple-element.45.interval.before.scale_far, f32[2,8,128]{2,1,0:T(8,128)S(1)} %stack.97.parity, f32[16,3,8,128]{3,2,1,0:T(8,128)S(1)} %bitcast.87, ...), custom_call_target="tpu_custom_call" | custom-call | tf_op jit(solution)/shard_map/middle/pallas_call | solution.py:314
  20.7 0.0 collective-permute-done.3.swap_d
  20.7 0.0 collective-permute-done.2.swap_c
  20.7 1.2 %outer.4 = (f32[18,3,3,8,128]{4,3,2,1,0:T(8,128)S(1)}, f32[16,3,8,128]{3,2,1,0:T(8,128)S(1)}, f32[2,2,8,128]{3,2,1,0:T(8,128)S(1)}) custom-call(f32[243,8,128]{2,1,0:T(8,128)S(1)} %get-tuple-element.44.coef, f32[2,8,128]{2,1,0:T(8,128)S(1)} %get-tuple-element.45.interval.before.scale_far, ...), custom_call_target="tpu_custom_call", output_to_operand_aliasing={{0}: (12, {}), {1}: (13, {})} | custom-call | tf_op jit(solution)/shard_map/outer/pallas_call | solution.py:421
  21.9 3.6 %collective-permute-start.5 = (f32[16,3,8,128]{3,2,1,0:T(8,128)S(1)}, f32[16,3,8,128]{3,2,1,0:T(8,128)S(1)}, u32[]{:S(2)}, u32[]{:S(2)}) collective-permute-start(f32[16,3,8,128]{3,2,1,0:T(8,128)S(1)} %get-tuple-element.56.refs_2_.own.l0), channel_id=1, source_target_pairs={{8,16},{16,8},{24,32},{32,24},{40,48},{48,40},{56,64},{64,56},{72,... | collective-permute-start | bytes 589832 | tf_op jit(solution)/shard_map/ppermute | solution.py:623
  25.6 0.1 collective-permute-start.4
  25.7 1.2 %inner.5.part = f32[14,3,3,8,128]{4,3,2,1,0:T(8,128)S(1)} custom-call(f32[243,8,128]{2,1,0:T(8,128)S(1)} %get-tuple-element.44.coef, f32[16,3,8,128]{3,2,1,0:T(8,128)S(1)} %get-tuple-element.56.refs_2_.own.l0), custom_call_target="tpu_custom_call" | custom-call | tf_op jit(solution)/shard_map/inner/pallas_call | solution.py:223
  26.8 1.1 sketch.3.refs_2_
  27.9 2.7 %collective-permute-done.5.swap_b = f32[16,3,8,128]{3,2,1,0:T(8,128)S(1)} collective-permute-done((f32[16,3,8,128]{3,2,1,0:T(8,128)S(1)}, f32[16,3,8,128]{3,2,1,0:T(8,128)S(1)}, u32[]{:S(2)}, u32[]{:S(2)}) %collective-permute-start.5) | collective-permute-done | bytes 196640 | tf_op jit(solution)/shard_map/ppermute | solution.py:623
  30.6 1.6 %collective-permute-done.4.swap_a = f32[16,3,8,128]{3,2,1,0:T(8,128)S(1)} collective-permute-done((f32[16,3,8,128]{3,2,1,0:T(8,128)S(1)}, f32[16,3,8,128]{3,2,1,0:T(8,128)S(1)}, u32[]{:S(2)}, u32[]{:S(2)}) %collective-permute-start.4) | collective-permute-done | bytes 196640 | tf_op jit(solution)/shard_map/ppermute | solution.py:623
  32.2 0.7 collective-permute-start.7
  32.9 2.9 %collective-permute-start.6 = (f32[3,2,3,8,128]{4,3,2,1,0:T(8,128)S(1)}, f32[3,2,3,8,128]{4,3,2,1,0:T(8,128)S(1)}, u32[]{:S(2)}, u32[]{:S(2)}) collective-permute-start(f32[3,2,3,8,128]{4,3,2,1,0:T(8,128)S(1)} %get-tuple-element.119), channel_id=1, source_target_pairs={{0,1},{1,0},{2,3},{3,2},{4,5},{5,4},{6,7},{7,6},{8,9},{9,8},{10,11... | collective-permute-start | bytes 221192 | tf_op jit(solution)/shard_map/ppermute | solution.py:623
  35.8 2.5 %middle.5 = (f32[18,3,3,8,128]{4,3,2,1,0:T(8,128)S(1)}, f32[16,3,8,128]{3,2,1,0:T(8,128)S(1)}) custom-call(f32[243,8,128]{2,1,0:T(8,128)S(1)} %get-tuple-element.44.coef, f32[2,8,128]{2,1,0:T(8,128)S(1)} %get-tuple-element.45.interval.before.scale_far, f32[2,8,128]{2,1,0:T(8,128)S(1)} %stack.97.parity, f32[16,3,8,128]{3,2,1,0:T(8,128)S(1)} %collective-permute-done.4.swap_a, ...), custom_call_target="tpu_custom_call" | custom-call | tf_op jit(solution)/shard_map/middle/pallas_call | solution.py:314
  38.3 0.0 collective-permute-done.7.swap_d
  38.3 0.0 collective-permute-done.6.swap_c
  38.3 1.2 %outer.5 = (f32[18,3,3,8,128]{4,3,2,1,0:T(8,128)S(1)}, f32[16,3,8,128]{3,2,1,0:T(8,128)S(1)}) custom-call(f32[243,8,128]{2,1,0:T(8,128)S(1)} %get-tuple-element.44.coef, f32[2,8,128]{2,1,0:T(8,128)S(1)} %get-tuple-element.45.interval.before.scale_far, f32[2,8,128]{2,1,0:T(8,128)S(1)} %stack.97.parity, ...), custom_call_target="tpu_custom_call", output_to_operand_aliasing={{0}: (12, {}), {1}: (13, {})} | custom-call | tf_op jit(solution)/shard_map/outer/pallas_call | solution.py:421
  39.6 5.5 %collective-permute-start.9 = (f32[16,3,8,128]{3,2,1,0:T(8,128)S(1)}, f32[16,3,8,128]{3,2,1,0:T(8,128)S(1)}, u32[]{:S(2)}, u32[]{:S(2)}) collective-permute-start(f32[16,3,8,128]{3,2,1,0:T(8,128)S(1)} %get-tuple-element.64.refs_1_.own.l1), channel_id=1, source_target_pairs={{8,16},{16,8},{24,32},{32,24},{40,48},{48,40},{56,64},{64,56},{72,... | collective-permute-start | bytes 589832 | tf_op jit(solution)/shard_map/ppermute | solution.py:623
  45.1 0.1 collective-permute-start.8
  45.2 1.2 %inner.6.part = f32[14,3,3,8,128]{4,3,2,1,0:T(8,128)S(1)} custom-call(f32[243,8,128]{2,1,0:T(8,128)S(1)} %get-tuple-element.44.coef, f32[16,3,8,128]{3,2,1,0:T(8,128)S(1)} %get-tuple-element.64.refs_1_.own.l1), custom_call_target="tpu_custom_call" | custom-call | tf_op jit(solution)/shard_map/inner/pallas_call | solution.py:223
  46.4 1.0 sketch.4.refs_3_
  47.4 2.8 %collective-permute-done.9.swap_b = f32[16,3,8,128]{3,2,1,0:T(8,128)S(1)} collective-permute-done((f32[16,3,8,128]{3,2,1,0:T(8,128)S(1)}, f32[16,3,8,128]{3,2,1,0:T(8,128)S(1)}, u32[]{:S(2)}, u32[]{:S(2)}) %collective-permute-start.9) | collective-permute-done | bytes 196640 | tf_op jit(solution)/shard_map/ppermute | solution.py:623
  50.2 1.6 %collective-permute-done.8.swap_a = f32[16,3,8,128]{3,2,1,0:T(8,128)S(1)} collective-permute-done((f32[16,3,8,128]{3,2,1,0:T(8,128)S(1)}, f32[16,3,8,128]{3,2,1,0:T(8,128)S(1)}, u32[]{:S(2)}, u32[]{:S(2)}) %collective-permute-start.8) | collective-permute-done | bytes 196640 | tf_op jit(solution)/shard_map/ppermute | solution.py:623
  51.8 0.7 collective-permute-start.11
  52.4 2.6 %collective-permute-start.10 = (f32[3,2,3,8,128]{4,3,2,1,0:T(8,128)S(1)}, f32[3,2,3,8,128]{4,3,2,1,0:T(8,128)S(1)}, u32[]{:S(2)}, u32[]{:S(2)}) collective-permute-start(f32[3,2,3,8,128]{4,3,2,1,0:T(8,128)S(1)} %get-tuple-element.117), channel_id=1, source_target_pairs={{0,1},{1,0},{2,3},{3,2},{4,5},{5,4},{6,7},{7,6},{8,9},{9,8},{10,11... | collective-permute-start | bytes 221192 | tf_op jit(solution)/shard_map/ppermute | solution.py:623
  55.1 2.5 %middle.6 = (f32[18,3,3,8,128]{4,3,2,1,0:T(8,128)S(1)}, f32[16,3,8,128]{3,2,1,0:T(8,128)S(1)}) custom-call(f32[243,8,128]{2,1,0:T(8,128)S(1)} %get-tuple-element.44.coef, f32[2,8,128]{2,1,0:T(8,128)S(1)} %get-tuple-element.45.interval.before.scale_far, f32[2,8,128]{2,1,0:T(8,128)S(1)} %stack.97.parity, f32[16,3,8,128]{3,2,1,0:T(8,128)S(1)} %collective-permute-done.8.swap_a, ...), custom_call_target="tpu_custom_call" | custom-call | tf_op jit(solution)/shard_map/middle/pallas_call | solution.py:314
  57.6 0.0 collective-permute-done.11.swap_d
  57.6 0.0 collective-permute-done.10.swap_c
  57.6 1.2 %outer.6 = (f32[18,3,3,8,128]{4,3,2,1,0:T(8,128)S(1)}, f32[16,3,8,128]{3,2,1,0:T(8,128)S(1)}) custom-call(f32[243,8,128]{2,1,0:T(8,128)S(1)} %get-tuple-element.44.coef, f32[2,8,128]{2,1,0:T(8,128)S(1)} %get-tuple-element.45.interval.before.scale_far, f32[2,8,128]{2,1,0:T(8,128)S(1)} %stack.97.parity, ...), custom_call_target="tpu_custom_call", output_to_operand_aliasing={{0}: (12, {}), {1}: (13, {})} | custom-call | tf_op jit(solution)/shard_map/outer/pallas_call | solution.py:421
  58.8 3.3 %collective-permute-start.13 = (f32[16,3,8,128]{3,2,1,0:T(8,128)S(1)}, f32[16,3,8,128]{3,2,1,0:T(8,128)S(1)}, u32[]{:S(2)}, u32[]{:S(2)}) collective-permute-start(f32[16,3,8,128]{3,2,1,0:T(8,128)S(1)} %get-tuple-element.71.refs_1_.own.l2), channel_id=1, source_target_pairs={{8,16},{16,8},{24,32},{32,24},{40,48},{48,40},{56,64},{64,56},{72,... | collective-permute-start | bytes 589832 | tf_op jit(solution)/shard_map/ppermute | solution.py:623
  62.1 0.1 collective-permute-start.12
  62.2 1.2 inner.7.part
  63.4 1.0 sketch.5.refs_4_
  64.4 3.2 %collective-permute-done.13.swap_b = f32[16,3,8,128]{3,2,1,0:T(8,128)S(1)} collective-permute-done((f32[16,3,8,128]{3,2,1,0:T(8,128)S(1)}, f32[16,3,8,128]{3,2,1,0:T(8,128)S(1)}, u32[]{:S(2)}, u32[]{:S(2)}) %collective-permute-start.13) | collective-permute-done | bytes 196640 | tf_op jit(solution)/shard_map/ppermute | solution.py:623
  67.5 1.2 %collective-permute-done.12.swap_a = f32[16,3,8,128]{3,2,1,0:T(8,128)S(1)} collective-permute-done((f32[16,3,8,128]{3,2,1,0:T(8,128)S(1)}, f32[16,3,8,128]{3,2,1,0:T(8,128)S(1)}, u32[]{:S(2)}, u32[]{:S(2)}) %collective-permute-start.12) | collective-permute-done | bytes 196640 | tf_op jit(solution)/shard_map/ppermute | solution.py:623
  68.8 0.7 collective-permute-start.15
  69.5 1.9 %collective-permute-start.14 = (f32[3,2,3,8,128]{4,3,2,1,0:T(8,128)S(1)}, f32[3,2,3,8,128]{4,3,2,1,0:T(8,128)S(1)}, u32[]{:S(2)}, u32[]{:S(2)}) collective-permute-start(f32[3,2,3,8,128]{4,3,2,1,0:T(8,128)S(1)} %get-tuple-element.115), channel_id=1, source_target_pairs={{0,1},{1,0},{2,3},{3,2},{4,5},{5,4},{6,7},{7,6},{8,9},{9,8},{10,11... | collective-permute-start | bytes 221192 | tf_op jit(solution)/shard_map/ppermute | solution.py:623
  71.4 2.5 %middle.7 = (f32[18,3,3,8,128]{4,3,2,1,0:T(8,128)S(1)}, f32[16,3,8,128]{3,2,1,0:T(8,128)S(1)}) custom-call(f32[243,8,128]{2,1,0:T(8,128)S(1)} %get-tuple-element.44.coef, f32[2,8,128]{2,1,0:T(8,128)S(1)} %get-tuple-element.45.interval.before.scale_far, f32[2,8,128]{2,1,0:T(8,128)S(1)} %stack.97.parity, f32[16,3,8,128]{3,2,1,0:T(8,128)S(1)} %collective-permute-done.12.swap_a, ...), custom_call_target="tpu_custom_call" | custom-call | tf_op jit(solution)/shard_map/middle/pallas_call | solution.py:314
  73.9 0.0 collective-permute-done.15.swap_d
  73.9 0.0 collective-permute-done.14.swap_c
  73.9 2.2 %outer.7 = (f32[18,3,3,8,128]{4,3,2,1,0:T(8,128)S(1)}, f32[16,3,8,128]{3,2,1,0:T(8,128)S(1)}, f32[36,128]{1,0:T(8,128)S(1)}) custom-call(f32[243,8,128]{2,1,0:T(8,128)S(1)} %get-tuple-element.44.coef, f32[2,8,128]{2,1,0:T(8,128)S(1)} %get-tuple-element.45.interval.before.scale_far, ...), custom_call_target="tpu_custom_call", output_to_operand_aliasing={{0}: (12, {}), {1}: (13, {})} | custom-call | tf_op jit(solution)/shard_map/outer/pallas_call | solution.py:421
  76.1 0.0 collective-permute-start.16
  76.1 1.2 collective-permute-done.16.refs_1_
  77.3 0.3 collective-permute-start.17
  77.6 3.5 %collective-permute-done.17.refs_1_ = f32[36,128]{1,0:T(8,128)S(1)} collective-permute-done((f32[36,128]{1,0:T(8,128)S(1)}, f32[36,128]{1,0:T(8,128)S(1)}, u32[]{:S(2)}, u32[]{:S(2)}) %collective-permute-start.17) | collective-permute-done | bytes 18464 | tf_op jit(solution)/shard_map/ppermute | solution.py:733
  81.1 17.7 %all_to_all.10.refs_0_ = f32[16,36,128]{2,1,0:T(8,128)S(1)} all-to-all(f32[16,36,128]{2,1,0:T(8,128)S(1)} %fold.4), channel_id=1, replica_groups=mesh['gx_0'=4,'gx_1'=4,'gx_2'=2,'gy_0'=4,'gy_1'=2] {'gx_0','gy_0'}, dimensions={0} | all-to-all | bytes 589824 | tf_op jit(solution)/shard_map/all_to_all | solution.py:737
  98.8 12.9 %all_to_all.11.table = f32[4,36,128]{2,1,0:T(8,128)S(1)} all-to-all(f32[4,36,128]{2,1,0:T(8,128)S(1)} %fold.5), channel_id=1, replica_groups=mesh['gx_0'=4,'gx_1'=4,'gx_2'=2,'gy_0'=4,'gy_1'=2] {'gx_1'}, dimensions={0} | all-to-all | bytes 147456 | tf_op jit(solution)/shard_map/all_to_all | solution.py:738
  111.7 5.5 %finish.1 = (f32[2,16,3,4,128]{4,3,2,1,0:T(4,128)}, f32[2,16,3,4,128]{4,3,2,1,0:T(4,128)}) custom-call(f32[4,36,128]{2,1,0:T(8,128)S(1)} %all_to_all.11.table, f32[2,8,128]{2,1,0:T(8,128)S(1)} %get-tuple-element.45.interval.before.scale_far, f32[16,3,8,128]{3,2,1,0:T(8,128)S(1)} %get-tuple-element.48.own.refs_0_.first, ...), custom_call_target="tpu_custom_call" | custom-call | tf_op jit(solution)/shard_map/finish/pallas_call | solution.py:607
  (30 shorter events, 0.3 us)
Async XLA Ops:
  0.7 7.0 %copy-start.3 = (f32[27,3,3]{0,2,1:T(4,128)S(1)}, f32[27,3,3]{0,2,1:T(4,128)}, u32[]{:S(2)}) copy-start(f32[27,3,3]{0,2,1:T(4,128)} %param.8) | copy-start | bytes 2920
  1.9 8.8 %collective-permute-start = (f32[400,128]{1,0:T(8,128)S(1)}, f32[400,128]{1,0:T(8,128)S(1)}, u32[]{:S(2)}, u32[]{:S(2)}) collective-permute-start(f32[400,128]{1,0:T(8,128)S(1)} %get-tuple-element.46), channel_id=1, source_target_pairs={{0,8},{8,0},{16,24},{24,16},{32,40},{40,32},{48,56},{56,48},{64,72... | collective-permute-start | bytes 614408 | tf_op jit(solution)/shard_map/ppermute | solution.py:623
  3.8 8.7 %collective-permute-start.1 = (f32[400,128]{1,0:T(8,128)S(1)}, f32[400,128]{1,0:T(8,128)S(1)}, u32[]{:S(2)}, u32[]{:S(2)}) collective-permute-start(f32[400,128]{1,0:T(8,128)S(1)} %get-tuple-element.47), channel_id=1, source_target_pairs={{8,16},{16,8},{24,32},{32,24},{40,48},{48,40},{56,64},{64,56},{72,... | collective-permute-start | bytes 614408 | tf_op jit(solution)/shard_map/ppermute | solution.py:623
  7.8 0.7 copy-start.2
  12.6 3.6 %copy-start = (s32[2,16,3,128]{3,1,2,0:T(8,128)S(1)}, s32[2,16,3,128]{3,1,2,0:T(8,128)}, u32[]{:S(2)}) copy-start(s32[2,16,3,128]{3,1,2,0:T(8,128)} %param.12) | copy-start | bytes 147460
  12.6 8.1 %collective-permute-start.3 = (f32[152,128]{1,0:T(8,128)S(1)}, f32[152,128]{1,0:T(8,128)S(1)}, u32[]{:S(2)}, u32[]{:S(2)}) collective-permute-start(f32[152,128]{1,0:T(8,128)S(1)} %get-tuple-element.112), channel_id=1, source_target_pairs={{1,2},{2,1},{3,4},{4,3},{5,6},{6,5},{9,10},{10,9},{11,12},{12,11},... | collective-permute-start | bytes 233480 | tf_op jit(solution)/shard_map/ppermute | solution.py:623
  13.3 7.4 %collective-permute-start.2 = (f32[152,128]{1,0:T(8,128)S(1)}, f32[152,128]{1,0:T(8,128)S(1)}, u32[]{:S(2)}, u32[]{:S(2)}) collective-permute-start(f32[152,128]{1,0:T(8,128)S(1)} %get-tuple-element.113), channel_id=1, source_target_pairs={{0,1},{1,0},{2,3},{3,2},{4,5},{5,4},{6,7},{7,6},{8,9},{9,8},{10,11... | collective-permute-start | bytes 233480 | tf_op jit(solution)/shard_map/ppermute | solution.py:623
  16.2 0.7 copy-start.1
  21.9 8.7 %collective-permute-start.5 = (f32[16,3,8,128]{3,2,1,0:T(8,128)S(1)}, f32[16,3,8,128]{3,2,1,0:T(8,128)S(1)}, u32[]{:S(2)}, u32[]{:S(2)}) collective-permute-start(f32[16,3,8,128]{3,2,1,0:T(8,128)S(1)} %get-tuple-element.56.refs_2_.own.l0), channel_id=1, source_target_pairs={{8,16},{16,8},{24,32},{32,24},{40,48},{48,40},{56,64},{64,56},{72,... | collective-permute-start | bytes 589832 | tf_op jit(solution)/shard_map/ppermute | solution.py:623
  25.6 6.6 %collective-permute-start.4 = (f32[16,3,8,128]{3,2,1,0:T(8,128)S(1)}, f32[16,3,8,128]{3,2,1,0:T(8,128)S(1)}, u32[]{:S(2)}, u32[]{:S(2)}) collective-permute-start(f32[16,3,8,128]{3,2,1,0:T(8,128)S(1)} %get-tuple-element.56.refs_2_.own.l0), channel_id=1, source_target_pairs={{0,8},{8,0},{16,24},{24,16},{32,40},{40,32},{48,56},{56,48},{64,72... | collective-permute-start | bytes 589832 | tf_op jit(solution)/shard_map/ppermute | solution.py:623
  32.2 6.1 %collective-permute-start.7 = (f32[3,2,3,8,128]{4,3,2,1,0:T(8,128)S(1)}, f32[3,2,3,8,128]{4,3,2,1,0:T(8,128)S(1)}, u32[]{:S(2)}, u32[]{:S(2)}) collective-permute-start(f32[3,2,3,8,128]{4,3,2,1,0:T(8,128)S(1)} %get-tuple-element.118), channel_id=1, source_target_pairs={{1,2},{2,1},{3,4},{4,3},{5,6},{6,5},{9,10},{10,9},{11,12},{12,11},... | collective-permute-start | bytes 221192 | tf_op jit(solution)/shard_map/ppermute | solution.py:623
  32.9 5.4 %collective-permute-start.6 = (f32[3,2,3,8,128]{4,3,2,1,0:T(8,128)S(1)}, f32[3,2,3,8,128]{4,3,2,1,0:T(8,128)S(1)}, u32[]{:S(2)}, u32[]{:S(2)}) collective-permute-start(f32[3,2,3,8,128]{4,3,2,1,0:T(8,128)S(1)} %get-tuple-element.119), channel_id=1, source_target_pairs={{0,1},{1,0},{2,3},{3,2},{4,5},{5,4},{6,7},{7,6},{8,9},{9,8},{10,11... | collective-permute-start | bytes 221192 | tf_op jit(solution)/shard_map/ppermute | solution.py:623
  39.6 10.6 %collective-permute-start.9 = (f32[16,3,8,128]{3,2,1,0:T(8,128)S(1)}, f32[16,3,8,128]{3,2,1,0:T(8,128)S(1)}, u32[]{:S(2)}, u32[]{:S(2)}) collective-permute-start(f32[16,3,8,128]{3,2,1,0:T(8,128)S(1)} %get-tuple-element.64.refs_1_.own.l1), channel_id=1, source_target_pairs={{8,16},{16,8},{24,32},{32,24},{40,48},{48,40},{56,64},{64,56},{72,... | collective-permute-start | bytes 589832 | tf_op jit(solution)/shard_map/ppermute | solution.py:623
  45.1 6.6 %collective-permute-start.8 = (f32[16,3,8,128]{3,2,1,0:T(8,128)S(1)}, f32[16,3,8,128]{3,2,1,0:T(8,128)S(1)}, u32[]{:S(2)}, u32[]{:S(2)}) collective-permute-start(f32[16,3,8,128]{3,2,1,0:T(8,128)S(1)} %get-tuple-element.64.refs_1_.own.l1), channel_id=1, source_target_pairs={{0,8},{8,0},{16,24},{24,16},{32,40},{40,32},{48,56},{56,48},{64,72... | collective-permute-start | bytes 589832 | tf_op jit(solution)/shard_map/ppermute | solution.py:623
  51.8 5.8 %collective-permute-start.11 = (f32[3,2,3,8,128]{4,3,2,1,0:T(8,128)S(1)}, f32[3,2,3,8,128]{4,3,2,1,0:T(8,128)S(1)}, u32[]{:S(2)}, u32[]{:S(2)}) collective-permute-start(f32[3,2,3,8,128]{4,3,2,1,0:T(8,128)S(1)} %get-tuple-element.116), channel_id=1, source_target_pairs={{1,2},{2,1},{3,4},{4,3},{5,6},{6,5},{9,10},{10,9},{11,12},{12,11},... | collective-permute-start | bytes 221192 | tf_op jit(solution)/shard_map/ppermute | solution.py:623
  52.4 5.1 %collective-permute-start.10 = (f32[3,2,3,8,128]{4,3,2,1,0:T(8,128)S(1)}, f32[3,2,3,8,128]{4,3,2,1,0:T(8,128)S(1)}, u32[]{:S(2)}, u32[]{:S(2)}) collective-permute-start(f32[3,2,3,8,128]{4,3,2,1,0:T(8,128)S(1)} %get-tuple-element.117), channel_id=1, source_target_pairs={{0,1},{1,0},{2,3},{3,2},{4,5},{5,4},{6,7},{7,6},{8,9},{9,8},{10,11... | collective-permute-start | bytes 221192 | tf_op jit(solution)/shard_map/ppermute | solution.py:623
  58.8 8.7 %collective-permute-start.13 = (f32[16,3,8,128]{3,2,1,0:T(8,128)S(1)}, f32[16,3,8,128]{3,2,1,0:T(8,128)S(1)}, u32[]{:S(2)}, u32[]{:S(2)}) collective-permute-start(f32[16,3,8,128]{3,2,1,0:T(8,128)S(1)} %get-tuple-element.71.refs_1_.own.l2), channel_id=1, source_target_pairs={{8,16},{16,8},{24,32},{32,24},{40,48},{48,40},{56,64},{64,56},{72,... | collective-permute-start | bytes 589832 | tf_op jit(solution)/shard_map/ppermute | solution.py:623
  62.1 6.6 %collective-permute-start.12 = (f32[16,3,8,128]{3,2,1,0:T(8,128)S(1)}, f32[16,3,8,128]{3,2,1,0:T(8,128)S(1)}, u32[]{:S(2)}, u32[]{:S(2)}) collective-permute-start(f32[16,3,8,128]{3,2,1,0:T(8,128)S(1)} %get-tuple-element.71.refs_1_.own.l2), channel_id=1, source_target_pairs={{0,8},{8,0},{16,24},{24,16},{32,40},{40,32},{48,56},{56,48},{64,72... | collective-permute-start | bytes 589832 | tf_op jit(solution)/shard_map/ppermute | solution.py:623
  68.8 5.1 %collective-permute-start.15 = (f32[3,2,3,8,128]{4,3,2,1,0:T(8,128)S(1)}, f32[3,2,3,8,128]{4,3,2,1,0:T(8,128)S(1)}, u32[]{:S(2)}, u32[]{:S(2)}) collective-permute-start(f32[3,2,3,8,128]{4,3,2,1,0:T(8,128)S(1)} %get-tuple-element.114), channel_id=1, source_target_pairs={{1,2},{2,1},{3,4},{4,3},{5,6},{6,5},{9,10},{10,9},{11,12},{12,11},... | collective-permute-start | bytes 221192 | tf_op jit(solution)/shard_map/ppermute | solution.py:623
  69.5 4.4 %collective-permute-start.14 = (f32[3,2,3,8,128]{4,3,2,1,0:T(8,128)S(1)}, f32[3,2,3,8,128]{4,3,2,1,0:T(8,128)S(1)}, u32[]{:S(2)}, u32[]{:S(2)}) collective-permute-start(f32[3,2,3,8,128]{4,3,2,1,0:T(8,128)S(1)} %get-tuple-element.115), channel_id=1, source_target_pairs={{0,1},{1,0},{2,3},{3,2},{4,5},{5,4},{6,7},{7,6},{8,9},{9,8},{10,11... | collective-permute-start | bytes 221192 | tf_op jit(solution)/shard_map/ppermute | solution.py:623
  76.1 1.2 %collective-permute-start.16 = (f32[36,128]{1,0:T(8,128)S(1)}, f32[36,128]{1,0:T(8,128)S(1)}, u32[]{:S(2)}, u32[]{:S(2)}) collective-permute-start(f32[36,128]{1,0:T(8,128)S(1)} %get-tuple-element.81.refs_0_), channel_id=1, source_target_pairs={{0,1},{1,0},{2,3},{3,2},{4,5},{5,4},{6,7},{7,6},{8,9},{9,8},{10,11... | collective-permute-start | bytes 55304 | tf_op jit(solution)/shard_map/ppermute | solution.py:733
  77.3 3.8 %collective-permute-start.17 = (f32[36,128]{1,0:T(8,128)S(1)}, f32[36,128]{1,0:T(8,128)S(1)}, u32[]{:S(2)}, u32[]{:S(2)}) collective-permute-start(f32[36,128]{1,0:T(8,128)S(1)} %bitcast.89), channel_id=1, source_target_pairs={{0,8},{8,0},{1,9},{9,1},{2,10},{10,2},{3,11},{11,3},{4,12},{12,4},... | collective-permute-start | bytes 55304 | tf_op jit(solution)/shard_map/ppermute | solution.py:733

commit v6 on v5

--- a/solution.py
+++ b/solution.py
@@ -9,8 +9,8 @@
 from jax.sharding import PartitionSpec as P
 
 STEPS = 8
-AXES = ("gx_0", "gx_1", "gx_2", "gy_0", "gy_1")
-GX = ("gx_0", "gx_1", "gx_2")
+AXES = ("gx_0", "gx_1", "gy_0", "gy_1")
+GX = ("gx_0", "gx_1")
 GY = ("gy_0", "gy_1")
 
 VMEM = pl.BlockSpec(memory_space=pltpu.VMEM)
@@ -600,7 +600,7 @@
                 remainder[x, y, c] = image[4 * x : 4 * x + 4]
         return carry
 
-    lax.fori_loop(0, 16, one_row, 0)
+    lax.fori_loop(0, 16, one_row, 0, unroll=2)
 
 
 def finish(table, interval, blocks):
@@ -729,19 +729,23 @@
         blocks += done[:2]
 
     table = done[2]
-    for axis in ("gy_1", "gx_2"):
-        other = lax.ppermute(table, axis, [(0, 1), (1, 0)])
-        count = 1 if axis == "gy_1" else 16
-        copies = fold(count, table, other)
-        table = copies.reshape(table.shape) if count == 1 else copies
+    stages = (
+        ("gy_1", ((0, 1),)),
+        ("gx_1", ((0, 1), (2, 3), (4, 5), (6, 7))),
+        ("gx_1", ((1, 2), (3, 4), (5, 6), (7, 0))),
+        ("gx_1", ((1, 6), (2, 5), (3, 0), (4, 7))),
+    )
+    for n, (axis, pairs) in enumerate(stages):
+        both_ways = [pair for a, b in pairs for pair in ((a, b), (b, a))]
+        other = lax.ppermute(table, axis, both_ways)
+        table = fold(1, table, other)[0] if n < 3 else fold(16, table, other)
     copies = lax.all_to_all(table, ("gx_0", "gy_0"), 0, 0, tiled=True)
-    copies = lax.all_to_all(fold(4, copies), ("gx_1",), 0, 0, tiled=True)
     iterate, remainder = finish(copies, interval, blocks)
     return iterate.transpose(0, 1, 3, 2, 4), remainder.transpose(0, 1, 3, 2, 4)
 
 
 def solution(mesh):
-    split = Mesh(mesh.devices.reshape(4, 4, 2, 4, 2), AXES)
+    split = Mesh(mesh.devices.reshape(4, 8, 4, 2), AXES)
     return jax.shard_map(
         cycle,
         mesh=split,

time: 118 us -> 116 us (0.983)
  the two profiles are of different devices: /device:TPU:32 before, /device:TPU:2 now
where the time goes in v6:
time: 116 us
  starting transfers between devices  45.7 us (39%)
  Pallas kernels  32.2 us (28%)
  waiting for transfers between devices  19.8 us (17%)
  blocking collectives  15.1 us (13%)
  local copies, waits for them, and re-layouts  1.61 us (1%)
    ppermute x16, starting transfers between devices, swap(): out.append(lax.ppermute(operand, axis, pairs))  36.6 us
    all_to_all x1, blocking collectives, cycle(): copies = lax.all_to_all(table, ('gx_0', 'gy_0'), 0, 0, tiled=True)  15.1 us
    ppermute x4, waiting for transfers between devices, cycle(): other = lax.ppermute(table, axis, both_ways)  10 us
    pallas_call x4, Pallas kernels, middle(): pl.pallas_call(make_middle_kernel(first_round), out_shape=(shaped(18, 3,...  9.93 us
    ppermute x16, waiting for transfers between devices, swap(): out.append(lax.ppermute(operand, axis, pairs))  9.73 us
    ppermute x4, starting transfers between devices, cycle(): other = lax.ppermute(table, axis, both_ways)  9.1 us
    pallas_call x4, Pallas kernels, outer(): pl.pallas_call(make_outer_kernel(first_round, len(tail)), out_shape=(shap...  5.84 us
    pallas_call x1, Pallas kernels, finish(): pl.pallas_call(finish_kernel, out_shape=(shaped(2, 16, 3, 4, 128), shaped...  5.46 us
  transfers between devices with their start and end apart: 20, of which 10 were waited for; matrix products, arithmetic and copies ran while one was open for 0% of the time, Pallas kernels for 17%

profile of v6, /device:TPU:2, one launch (start us, length us, event | category | flops | bytes accessed | tf_op | source)
XLA Modules:
  0.0 115.5 jit_solution(17577543146557290300)
XLA Ops:
  0.7 0.1 stack.97.parity
  0.7 1.1 prepare.1
  1.9 2.0 %collective-permute-start = (f32[400,128]{1,0:T(8,128)S(1)}, f32[400,128]{1,0:T(8,128)S(1)}, u32[]{:S(2)}, u32[]{:S(2)}) collective-permute-start(f32[400,128]{1,0:T(8,128)S(1)} %get-tuple-element.46), channel_id=1, source_target_pairs={{0,8},{8,0},{16,24},{24,16},{32,40},{40,32},{48,56},{56,48},{64,72... | collective-permute-start | bytes 614408 | tf_op jit(solution)/shard_map/ppermute | solution.py:623
  3.9 0.7 collective-permute-start.1
  4.5 0.1 copy.20
  4.7 0.0 copy-start.2
  4.7 0.2 reshape.117.stencil
  4.8 0.5 copy-done.2
  5.3 1.0 setup.1
  6.3 1.2 %inner.4.part = f32[14,3,3,8,128]{4,3,2,1,0:T(8,128)S(1)} custom-call(f32[243,8,128]{2,1,0:T(8,128)S(1)} %get-tuple-element.44.coef, f32[16,3,8,128]{3,2,1,0:T(8,128)S(1)} %get-tuple-element.48.own.refs_0_.first), custom_call_target="tpu_custom_call" | custom-call | tf_op jit(solution)/shard_map/inner/pallas_call | solution.py:223
  7.5 1.4 %collective-permute-done = f32[400,128]{1,0:T(8,128)S(1)} collective-permute-done((f32[400,128]{1,0:T(8,128)S(1)}, f32[400,128]{1,0:T(8,128)S(1)}, u32[]{:S(2)}, u32[]{:S(2)}) %collective-permute-start) | collective-permute-done | bytes 204832 | tf_op jit(solution)/shard_map/ppermute | solution.py:623
  8.9 0.0 collective-permute-done.1
  9.1 0.0 copy-start
  9.1 1.9 %collective-permute-start.3 = (f32[152,128]{1,0:T(8,128)S(1)}, f32[152,128]{1,0:T(8,128)S(1)}, u32[]{:S(2)}, u32[]{:S(2)}) collective-permute-start(f32[152,128]{1,0:T(8,128)S(1)} %get-tuple-element.112), channel_id=1, source_target_pairs={{1,2},{2,1},{3,4},{4,3},{5,6},{6,5},{9,10},{10,9},{11,12},{12,11},... | collective-permute-start | bytes 233480 | tf_op jit(solution)/shard_map/ppermute | solution.py:623
  11.0 1.7 %collective-permute-start.2 = (f32[152,128]{1,0:T(8,128)S(1)}, f32[152,128]{1,0:T(8,128)S(1)}, u32[]{:S(2)}, u32[]{:S(2)}) collective-permute-start(f32[152,128]{1,0:T(8,128)S(1)} %get-tuple-element.113), channel_id=1, source_target_pairs={{0,1},{1,0},{2,3},{3,2},{4,5},{5,4},{6,7},{7,6},{8,9},{9,8},{10,11... | collective-permute-start | bytes 233480 | tf_op jit(solution)/shard_map/ppermute | solution.py:623
  12.7 0.7 copy-done.1
  13.4 1.2 %signs.1.refs_1_ = f32[64,8,128]{2,1,0:T(8,128)S(1)} custom-call(s32[128]{0:T(128)S(1)} %bitcast.99, s32[2,3,16,128]{3,2,1,0:T(8,128)S(1)} %bitcast.98), custom_call_target="tpu_custom_call" | custom-call | tf_op jit(solution)/shard_map/signs/pallas_call | solution.py:148
  14.7 2.5 %middle.4 = (f32[18,3,3,8,128]{4,3,2,1,0:T(8,128)S(1)}, f32[16,3,8,128]{3,2,1,0:T(8,128)S(1)}) custom-call(f32[243,8,128]{2,1,0:T(8,128)S(1)} %get-tuple-element.44.coef, f32[2,8,128]{2,1,0:T(8,128)S(1)} %get-tuple-element.45.interval.before.scale_far, f32[2,8,128]{2,1,0:T(8,128)S(1)} %stack.97.parity, f32[16,3,8,128]{3,2,1,0:T(8,128)S(1)} %bitcast.89, ...), custom_call_target="tpu_custom_call" | custom-call | tf_op jit(solution)/shard_map/middle/pallas_call | solution.py:314
  17.2 0.0 collective-permute-done.3.swap_d
  17.2 0.0 collective-permute-done.2.swap_c
  17.2 1.2 %outer.4 = (f32[18,3,3,8,128]{4,3,2,1,0:T(8,128)S(1)}, f32[16,3,8,128]{3,2,1,0:T(8,128)S(1)}, f32[2,2,8,128]{3,2,1,0:T(8,128)S(1)}) custom-call(f32[243,8,128]{2,1,0:T(8,128)S(1)} %get-tuple-element.44.coef, f32[2,8,128]{2,1,0:T(8,128)S(1)} %get-tuple-element.45.interval.before.scale_far, ...), custom_call_target="tpu_custom_call", output_to_operand_aliasing={{0}: (12, {}), {1}: (13, {})} | custom-call | tf_op jit(solution)/shard_map/outer/pallas_call | solution.py:421
  18.4 0.7 collective-permute-start.5
  19.1 8.5 %collective-permute-start.4 = (f32[16,3,8,128]{3,2,1,0:T(8,128)S(1)}, f32[16,3,8,128]{3,2,1,0:T(8,128)S(1)}, u32[]{:S(2)}, u32[]{:S(2)}) collective-permute-start(f32[16,3,8,128]{3,2,1,0:T(8,128)S(1)} %get-tuple-element.56.refs_2_.own.l0), channel_id=1, source_target_pairs={{0,8},{8,0},{16,24},{24,16},{32,40},{40,32},{48,56},{56,48},{64,72... | collective-permute-start | bytes 589832 | tf_op jit(solution)/shard_map/ppermute | solution.py:623
  27.6 1.2 %inner.5.part = f32[14,3,3,8,128]{4,3,2,1,0:T(8,128)S(1)} custom-call(f32[243,8,128]{2,1,0:T(8,128)S(1)} %get-tuple-element.44.coef, f32[16,3,8,128]{3,2,1,0:T(8,128)S(1)} %get-tuple-element.56.refs_2_.own.l0), custom_call_target="tpu_custom_call" | custom-call | tf_op jit(solution)/shard_map/inner/pallas_call | solution.py:223
  28.7 1.1 sketch.3.refs_2_
  29.8 0.0 collective-permute-done.5.swap_b
  29.8 2.6 %collective-permute-done.4.swap_a = f32[16,3,8,128]{3,2,1,0:T(8,128)S(1)} collective-permute-done((f32[16,3,8,128]{3,2,1,0:T(8,128)S(1)}, f32[16,3,8,128]{3,2,1,0:T(8,128)S(1)}, u32[]{:S(2)}, u32[]{:S(2)}) %collective-permute-start.4) | collective-permute-done | bytes 196640 | tf_op jit(solution)/shard_map/ppermute | solution.py:623
  32.4 1.9 %collective-permute-start.7 = (f32[3,2,3,8,128]{4,3,2,1,0:T(8,128)S(1)}, f32[3,2,3,8,128]{4,3,2,1,0:T(8,128)S(1)}, u32[]{:S(2)}, u32[]{:S(2)}) collective-permute-start(f32[3,2,3,8,128]{4,3,2,1,0:T(8,128)S(1)} %get-tuple-element.118), channel_id=1, source_target_pairs={{1,2},{2,1},{3,4},{4,3},{5,6},{6,5},{9,10},{10,9},{11,12},{12,11},... | collective-permute-start | bytes 221192 | tf_op jit(solution)/shard_map/ppermute | solution.py:623
  34.3 1.4 %collective-permute-start.6 = (f32[3,2,3,8,128]{4,3,2,1,0:T(8,128)S(1)}, f32[3,2,3,8,128]{4,3,2,1,0:T(8,128)S(1)}, u32[]{:S(2)}, u32[]{:S(2)}) collective-permute-start(f32[3,2,3,8,128]{4,3,2,1,0:T(8,128)S(1)} %get-tuple-element.119), channel_id=1, source_target_pairs={{0,1},{1,0},{2,3},{3,2},{4,5},{5,4},{6,7},{7,6},{8,9},{9,8},{10,11... | collective-permute-start | bytes 221192 | tf_op jit(solution)/shard_map/ppermute | solution.py:623
  35.7 2.5 %middle.5 = (f32[18,3,3,8,128]{4,3,2,1,0:T(8,128)S(1)}, f32[16,3,8,128]{3,2,1,0:T(8,128)S(1)}) custom-call(f32[243,8,128]{2,1,0:T(8,128)S(1)} %get-tuple-element.44.coef, f32[2,8,128]{2,1,0:T(8,128)S(1)} %get-tuple-element.45.interval.before.scale_far, f32[2,8,128]{2,1,0:T(8,128)S(1)} %stack.97.parity, f32[16,3,8,128]{3,2,1,0:T(8,128)S(1)} %collective-permute-done.4.swap_a, ...), custom_call_target="tpu_custom_call" | custom-call | tf_op jit(solution)/shard_map/middle/pallas_call | solution.py:314
  38.2 0.0 collective-permute-done.7.swap_d
  38.2 0.0 collective-permute-done.6.swap_c
  38.2 1.2 %outer.5 = (f32[18,3,3,8,128]{4,3,2,1,0:T(8,128)S(1)}, f32[16,3,8,128]{3,2,1,0:T(8,128)S(1)}) custom-call(f32[243,8,128]{2,1,0:T(8,128)S(1)} %get-tuple-element.44.coef, f32[2,8,128]{2,1,0:T(8,128)S(1)} %get-tuple-element.45.interval.before.scale_far, f32[2,8,128]{2,1,0:T(8,128)S(1)} %stack.97.parity, ...), custom_call_target="tpu_custom_call", output_to_operand_aliasing={{0}: (12, {}), {1}: (13, {})} | custom-call | tf_op jit(solution)/shard_map/outer/pallas_call | solution.py:421
  39.4 0.7 collective-permute-start.9
  40.1 6.7 %collective-permute-start.8 = (f32[16,3,8,128]{3,2,1,0:T(8,128)S(1)}, f32[16,3,8,128]{3,2,1,0:T(8,128)S(1)}, u32[]{:S(2)}, u32[]{:S(2)}) collective-permute-start(f32[16,3,8,128]{3,2,1,0:T(8,128)S(1)} %get-tuple-element.64.refs_1_.own.l1), channel_id=1, source_target_pairs={{0,8},{8,0},{16,24},{24,16},{32,40},{40,32},{48,56},{56,48},{64,72... | collective-permute-start | bytes 589832 | tf_op jit(solution)/shard_map/ppermute | solution.py:623
  46.8 1.2 %inner.6.part = f32[14,3,3,8,128]{4,3,2,1,0:T(8,128)S(1)} custom-call(f32[243,8,128]{2,1,0:T(8,128)S(1)} %get-tuple-element.44.coef, f32[16,3,8,128]{3,2,1,0:T(8,128)S(1)} %get-tuple-element.64.refs_1_.own.l1), custom_call_target="tpu_custom_call" | custom-call | tf_op jit(solution)/shard_map/inner/pallas_call | solution.py:223
  48.0 1.0 sketch.4.refs_3_
  49.0 2.6 %collective-permute-done.8.swap_a = f32[16,3,8,128]{3,2,1,0:T(8,128)S(1)} collective-permute-done((f32[16,3,8,128]{3,2,1,0:T(8,128)S(1)}, f32[16,3,8,128]{3,2,1,0:T(8,128)S(1)}, u32[]{:S(2)}, u32[]{:S(2)}) %collective-permute-start.8) | collective-permute-done | bytes 196640 | tf_op jit(solution)/shard_map/ppermute | solution.py:623
  51.6 1.9 %collective-permute-start.11 = (f32[3,2,3,8,128]{4,3,2,1,0:T(8,128)S(1)}, f32[3,2,3,8,128]{4,3,2,1,0:T(8,128)S(1)}, u32[]{:S(2)}, u32[]{:S(2)}) collective-permute-start(f32[3,2,3,8,128]{4,3,2,1,0:T(8,128)S(1)} %get-tuple-element.116), channel_id=1, source_target_pairs={{1,2},{2,1},{3,4},{4,3},{5,6},{6,5},{9,10},{10,9},{11,12},{12,11},... | collective-permute-start | bytes 221192 | tf_op jit(solution)/shard_map/ppermute | solution.py:623
  53.6 0.7 collective-permute-start.10
  54.3 2.5 %middle.6 = (f32[18,3,3,8,128]{4,3,2,1,0:T(8,128)S(1)}, f32[16,3,8,128]{3,2,1,0:T(8,128)S(1)}) custom-call(f32[243,8,128]{2,1,0:T(8,128)S(1)} %get-tuple-element.44.coef, f32[2,8,128]{2,1,0:T(8,128)S(1)} %get-tuple-element.45.interval.before.scale_far, f32[2,8,128]{2,1,0:T(8,128)S(1)} %stack.97.parity, f32[16,3,8,128]{3,2,1,0:T(8,128)S(1)} %collective-permute-done.8.swap_a, ...), custom_call_target="tpu_custom_call" | custom-call | tf_op jit(solution)/shard_map/middle/pallas_call | solution.py:314
  56.7 0.6 collective-permute-done.11.swap_d
  57.3 0.0 collective-permute-done.10.swap_c
  57.3 1.2 %outer.6 = (f32[18,3,3,8,128]{4,3,2,1,0:T(8,128)S(1)}, f32[16,3,8,128]{3,2,1,0:T(8,128)S(1)}) custom-call(f32[243,8,128]{2,1,0:T(8,128)S(1)} %get-tuple-element.44.coef, f32[2,8,128]{2,1,0:T(8,128)S(1)} %get-tuple-element.45.interval.before.scale_far, f32[2,8,128]{2,1,0:T(8,128)S(1)} %stack.97.parity, ...), custom_call_target="tpu_custom_call", output_to_operand_aliasing={{0}: (12, {}), {1}: (13, {})} | custom-call | tf_op jit(solution)/shard_map/outer/pallas_call | solution.py:421
  58.5 0.7 collective-permute-start.13
  59.2 4.4 %collective-permute-start.12 = (f32[16,3,8,128]{3,2,1,0:T(8,128)S(1)}, f32[16,3,8,128]{3,2,1,0:T(8,128)S(1)}, u32[]{:S(2)}, u32[]{:S(2)}) collective-permute-start(f32[16,3,8,128]{3,2,1,0:T(8,128)S(1)} %get-tuple-element.71.refs_1_.own.l2), channel_id=1, source_target_pairs={{0,8},{8,0},{16,24},{24,16},{32,40},{40,32},{48,56},{56,48},{64,72... | collective-permute-start | bytes 589832 | tf_op jit(solution)/shard_map/ppermute | solution.py:623
  63.7 1.2 %inner.7.part = f32[14,3,3,8,128]{4,3,2,1,0:T(8,128)S(1)} custom-call(f32[243,8,128]{2,1,0:T(8,128)S(1)} %get-tuple-element.44.coef, f32[16,3,8,128]{3,2,1,0:T(8,128)S(1)} %get-tuple-element.71.refs_1_.own.l2), custom_call_target="tpu_custom_call" | custom-call | tf_op jit(solution)/shard_map/inner/pallas_call | solution.py:223
  64.8 1.0 sketch.5.refs_4_
  65.8 2.1 %collective-permute-done.12.swap_a = f32[16,3,8,128]{3,2,1,0:T(8,128)S(1)} collective-permute-done((f32[16,3,8,128]{3,2,1,0:T(8,128)S(1)}, f32[16,3,8,128]{3,2,1,0:T(8,128)S(1)}, u32[]{:S(2)}, u32[]{:S(2)}) %collective-permute-start.12) | collective-permute-done | bytes 196640 | tf_op jit(solution)/shard_map/ppermute | solution.py:623
  68.0 2.2 %collective-permute-start.15 = (f32[3,2,3,8,128]{4,3,2,1,0:T(8,128)S(1)}, f32[3,2,3,8,128]{4,3,2,1,0:T(8,128)S(1)}, u32[]{:S(2)}, u32[]{:S(2)}) collective-permute-start(f32[3,2,3,8,128]{4,3,2,1,0:T(8,128)S(1)} %get-tuple-element.114), channel_id=1, source_target_pairs={{1,2},{2,1},{3,4},{4,3},{5,6},{6,5},{9,10},{10,9},{11,12},{12,11},... | collective-permute-start | bytes 221192 | tf_op jit(solution)/shard_map/ppermute | solution.py:623
  70.2 0.6 collective-permute-start.14
  70.8 2.5 %middle.7 = (f32[18,3,3,8,128]{4,3,2,1,0:T(8,128)S(1)}, f32[16,3,8,128]{3,2,1,0:T(8,128)S(1)}) custom-call(f32[243,8,128]{2,1,0:T(8,128)S(1)} %get-tuple-element.44.coef, f32[2,8,128]{2,1,0:T(8,128)S(1)} %get-tuple-element.45.interval.before.scale_far, f32[2,8,128]{2,1,0:T(8,128)S(1)} %stack.97.parity, f32[16,3,8,128]{3,2,1,0:T(8,128)S(1)} %collective-permute-done.12.swap_a, ...), custom_call_target="tpu_custom_call" | custom-call | tf_op jit(solution)/shard_map/middle/pallas_call | solution.py:314
  73.2 0.4 collective-permute-done.15.swap_d
  73.6 2.2 %outer.7 = (f32[18,3,3,8,128]{4,3,2,1,0:T(8,128)S(1)}, f32[16,3,8,128]{3,2,1,0:T(8,128)S(1)}, f32[36,128]{1,0:T(8,128)S(1)}) custom-call(f32[243,8,128]{2,1,0:T(8,128)S(1)} %get-tuple-element.44.coef, f32[2,8,128]{2,1,0:T(8,128)S(1)} %get-tuple-element.45.interval.before.scale_far, ...), custom_call_target="tpu_custom_call", output_to_operand_aliasing={{0}: (12, {}), {1}: (13, {})} | custom-call | tf_op jit(solution)/shard_map/outer/pallas_call | solution.py:421
  75.8 0.0 collective-permute-start.16
  75.8 1.2 %collective-permute-done.16.refs_1_ = f32[36,128]{1,0:T(8,128)S(1)} collective-permute-done((f32[36,128]{1,0:T(8,128)S(1)}, f32[36,128]{1,0:T(8,128)S(1)}, u32[]{:S(2)}, u32[]{:S(2)}) %collective-permute-start.16) | collective-permute-done | bytes 18464 | tf_op jit(solution)/shard_map/ppermute | solution.py:740
  77.0 1.7 %collective-permute-start.17 = (f32[36,128]{1,0:T(8,128)S(1)}, f32[36,128]{1,0:T(8,128)S(1)}, u32[]{:S(2)}, u32[]{:S(2)}) collective-permute-start(f32[36,128]{1,0:T(8,128)S(1)} %bitcast.93), channel_id=1, source_target_pairs={{0,8},{8,0},{16,24},{24,16},{32,40},{40,32},{48,56},{56,48},{1,9},... | collective-permute-start | bytes 55304 | tf_op jit(solution)/shard_map/ppermute | solution.py:740
  78.8 2.0 %collective-permute-done.17.refs_1_ = f32[36,128]{1,0:T(8,128)S(1)} collective-permute-done((f32[36,128]{1,0:T(8,128)S(1)}, f32[36,128]{1,0:T(8,128)S(1)}, u32[]{:S(2)}, u32[]{:S(2)}) %collective-permute-start.17) | collective-permute-done | bytes 18464 | tf_op jit(solution)/shard_map/ppermute | solution.py:740
  80.8 6.8 %collective-permute-start.18 = (f32[36,128]{1,0:T(8,128)S(1)}, f32[36,128]{1,0:T(8,128)S(1)}, u32[]{:S(2)}, u32[]{:S(2)}) collective-permute-start(f32[36,128]{1,0:T(8,128)S(1)} %bitcast.95), channel_id=1, source_target_pairs={{8,16},{16,8},{24,32},{32,24},{40,48},{48,40},{56,0},{0,56},{9,17}... | collective-permute-start | bytes 55304 | tf_op jit(solution)/shard_map/ppermute | solution.py:740
  87.6 1.8 %collective-permute-done.18.refs_1_ = f32[36,128]{1,0:T(8,128)S(1)} collective-permute-done((f32[36,128]{1,0:T(8,128)S(1)}, f32[36,128]{1,0:T(8,128)S(1)}, u32[]{:S(2)}, u32[]{:S(2)}) %collective-permute-start.18) | collective-permute-done | bytes 18464 | tf_op jit(solution)/shard_map/ppermute | solution.py:740
  89.4 0.5 collective-permute-start.19
  89.9 5.1 %collective-permute-done.19.refs_1_ = f32[36,128]{1,0:T(8,128)S(1)} collective-permute-done((f32[36,128]{1,0:T(8,128)S(1)}, f32[36,128]{1,0:T(8,128)S(1)}, u32[]{:S(2)}, u32[]{:S(2)}) %collective-permute-start.19) | collective-permute-done | bytes 18464 | tf_op jit(solution)/shard_map/ppermute | solution.py:740
  95.0 15.1 %all_to_all.5.table = f32[16,36,128]{2,1,0:T(8,128)S(1)} all-to-all(f32[16,36,128]{2,1,0:T(8,128)S(1)} %fold.7), channel_id=1, replica_groups=mesh['gx_0'=4,'gx_1'=8,'gy_0'=4,'gy_1'=2] {'gx_0','gy_0'}, dimensions={0} | all-to-all | bytes 589824 | tf_op jit(solution)/shard_map/all_to_all | solution.py:742
  110.1 5.5 %finish.1 = (f32[2,16,3,4,128]{4,3,2,1,0:T(4,128)}, f32[2,16,3,4,128]{4,3,2,1,0:T(4,128)}) custom-call(f32[16,36,128]{2,1,0:T(8,128)S(1)} %all_to_all.5.table, f32[2,8,128]{2,1,0:T(8,128)S(1)} %get-tuple-element.45.interval.before.scale_far, f32[16,3,8,128]{3,2,1,0:T(8,128)S(1)} %get-tuple-element.48.own.refs_0_.first, ...), custom_call_target="tpu_custom_call" | custom-call | tf_op jit(solution)/shard_map/finish/pallas_call | solution.py:607
  (34 shorter events, 0.3 us)
Async XLA Ops:
  0.7 3.8 %copy-start.3 = (f32[27,3,3]{0,2,1:T(4,128)S(1)}, f32[27,3,3]{0,2,1:T(4,128)}, u32[]{:S(2)}) copy-start(f32[27,3,3]{0,2,1:T(4,128)} %param.8) | copy-start | bytes 2920
  1.9 7.1 %collective-permute-start = (f32[400,128]{1,0:T(8,128)S(1)}, f32[400,128]{1,0:T(8,128)S(1)}, u32[]{:S(2)}, u32[]{:S(2)}) collective-permute-start(f32[400,128]{1,0:T(8,128)S(1)} %get-tuple-element.46), channel_id=1, source_target_pairs={{0,8},{8,0},{16,24},{24,16},{32,40},{40,32},{48,56},{56,48},{64,72... | collective-permute-start | bytes 614408 | tf_op jit(solution)/shard_map/ppermute | solution.py:623
  3.9 5.1 %collective-permute-start.1 = (f32[400,128]{1,0:T(8,128)S(1)}, f32[400,128]{1,0:T(8,128)S(1)}, u32[]{:S(2)}, u32[]{:S(2)}) collective-permute-start(f32[400,128]{1,0:T(8,128)S(1)} %get-tuple-element.47), channel_id=1, source_target_pairs={{8,16},{16,8},{24,32},{32,24},{40,48},{48,40},{56,64},{64,56},{72,... | collective-permute-start | bytes 614408 | tf_op jit(solution)/shard_map/ppermute | solution.py:623
  4.7 0.7 copy-start.2
  9.1 3.6 %copy-start = (s32[2,16,3,128]{3,1,2,0:T(8,128)S(1)}, s32[2,16,3,128]{3,1,2,0:T(8,128)}, u32[]{:S(2)}) copy-start(s32[2,16,3,128]{3,1,2,0:T(8,128)} %param.12) | copy-start | bytes 147460
  9.1 8.1 %collective-permute-start.3 = (f32[152,128]{1,0:T(8,128)S(1)}, f32[152,128]{1,0:T(8,128)S(1)}, u32[]{:S(2)}, u32[]{:S(2)}) collective-permute-start(f32[152,128]{1,0:T(8,128)S(1)} %get-tuple-element.112), channel_id=1, source_target_pairs={{1,2},{2,1},{3,4},{4,3},{5,6},{6,5},{9,10},{10,9},{11,12},{12,11},... | collective-permute-start | bytes 233480 | tf_op jit(solution)/shard_map/ppermute | solution.py:623
  11.0 6.2 %collective-permute-start.2 = (f32[152,128]{1,0:T(8,128)S(1)}, f32[152,128]{1,0:T(8,128)S(1)}, u32[]{:S(2)}, u32[]{:S(2)}) collective-permute-start(f32[152,128]{1,0:T(8,128)S(1)} %get-tuple-element.113), channel_id=1, source_target_pairs={{0,1},{1,0},{2,3},{3,2},{4,5},{5,4},{6,7},{7,6},{8,9},{9,8},{10,11... | collective-permute-start | bytes 233480 | tf_op jit(solution)/shard_map/ppermute | solution.py:623
  12.7 0.7 copy-start.1
  18.4 11.4 %collective-permute-start.5 = (f32[16,3,8,128]{3,2,1,0:T(8,128)S(1)}, f32[16,3,8,128]{3,2,1,0:T(8,128)S(1)}, u32[]{:S(2)}, u32[]{:S(2)}) collective-permute-start(f32[16,3,8,128]{3,2,1,0:T(8,128)S(1)} %get-tuple-element.56.refs_2_.own.l0), channel_id=1, source_target_pairs={{8,16},{16,8},{24,32},{32,24},{40,48},{48,40},{56,64},{64,56},{72,... | collective-permute-start | bytes 589832 | tf_op jit(solution)/shard_map/ppermute | solution.py:623
  19.1 13.3 %collective-permute-start.4 = (f32[16,3,8,128]{3,2,1,0:T(8,128)S(1)}, f32[16,3,8,128]{3,2,1,0:T(8,128)S(1)}, u32[]{:S(2)}, u32[]{:S(2)}) collective-permute-start(f32[16,3,8,128]{3,2,1,0:T(8,128)S(1)} %get-tuple-element.56.refs_2_.own.l0), channel_id=1, source_target_pairs={{0,8},{8,0},{16,24},{24,16},{32,40},{40,32},{48,56},{56,48},{64,72... | collective-permute-start | bytes 589832 | tf_op jit(solution)/shard_map/ppermute | solution.py:623
  32.4 5.8 %collective-permute-start.7 = (f32[3,2,3,8,128]{4,3,2,1,0:T(8,128)S(1)}, f32[3,2,3,8,128]{4,3,2,1,0:T(8,128)S(1)}, u32[]{:S(2)}, u32[]{:S(2)}) collective-permute-start(f32[3,2,3,8,128]{4,3,2,1,0:T(8,128)S(1)} %get-tuple-element.118), channel_id=1, source_target_pairs={{1,2},{2,1},{3,4},{4,3},{5,6},{6,5},{9,10},{10,9},{11,12},{12,11},... | collective-permute-start | bytes 221192 | tf_op jit(solution)/shard_map/ppermute | solution.py:623
  34.3 3.9 %collective-permute-start.6 = (f32[3,2,3,8,128]{4,3,2,1,0:T(8,128)S(1)}, f32[3,2,3,8,128]{4,3,2,1,0:T(8,128)S(1)}, u32[]{:S(2)}, u32[]{:S(2)}) collective-permute-start(f32[3,2,3,8,128]{4,3,2,1,0:T(8,128)S(1)} %get-tuple-element.119), channel_id=1, source_target_pairs={{0,1},{1,0},{2,3},{3,2},{4,5},{5,4},{6,7},{7,6},{8,9},{9,8},{10,11... | collective-permute-start | bytes 221192 | tf_op jit(solution)/shard_map/ppermute | solution.py:623
  39.4 9.5 %collective-permute-start.9 = (f32[16,3,8,128]{3,2,1,0:T(8,128)S(1)}, f32[16,3,8,128]{3,2,1,0:T(8,128)S(1)}, u32[]{:S(2)}, u32[]{:S(2)}) collective-permute-start(f32[16,3,8,128]{3,2,1,0:T(8,128)S(1)} %get-tuple-element.64.refs_1_.own.l1), channel_id=1, source_target_pairs={{8,16},{16,8},{24,32},{32,24},{40,48},{48,40},{56,64},{64,56},{72,... | collective-permute-start | bytes 589832 | tf_op jit(solution)/shard_map/ppermute | solution.py:623
  40.1 11.5 %collective-permute-start.8 = (f32[16,3,8,128]{3,2,1,0:T(8,128)S(1)}, f32[16,3,8,128]{3,2,1,0:T(8,128)S(1)}, u32[]{:S(2)}, u32[]{:S(2)}) collective-permute-start(f32[16,3,8,128]{3,2,1,0:T(8,128)S(1)} %get-tuple-element.64.refs_1_.own.l1), channel_id=1, source_target_pairs={{0,8},{8,0},{16,24},{24,16},{32,40},{40,32},{48,56},{56,48},{64,72... | collective-permute-start | bytes 589832 | tf_op jit(solution)/shard_map/ppermute | solution.py:623
  51.6 5.7 %collective-permute-start.11 = (f32[3,2,3,8,128]{4,3,2,1,0:T(8,128)S(1)}, f32[3,2,3,8,128]{4,3,2,1,0:T(8,128)S(1)}, u32[]{:S(2)}, u32[]{:S(2)}) collective-permute-start(f32[3,2,3,8,128]{4,3,2,1,0:T(8,128)S(1)} %get-tuple-element.116), channel_id=1, source_target_pairs={{1,2},{2,1},{3,4},{4,3},{5,6},{6,5},{9,10},{10,9},{11,12},{12,11},... | collective-permute-start | bytes 221192 | tf_op jit(solution)/shard_map/ppermute | solution.py:623
  53.6 3.7 %collective-permute-start.10 = (f32[3,2,3,8,128]{4,3,2,1,0:T(8,128)S(1)}, f32[3,2,3,8,128]{4,3,2,1,0:T(8,128)S(1)}, u32[]{:S(2)}, u32[]{:S(2)}) collective-permute-start(f32[3,2,3,8,128]{4,3,2,1,0:T(8,128)S(1)} %get-tuple-element.117), channel_id=1, source_target_pairs={{0,1},{1,0},{2,3},{3,2},{4,5},{5,4},{6,7},{7,6},{8,9},{9,8},{10,11... | collective-permute-start | bytes 221192 | tf_op jit(solution)/shard_map/ppermute | solution.py:623
  58.5 7.3 %collective-permute-start.13 = (f32[16,3,8,128]{3,2,1,0:T(8,128)S(1)}, f32[16,3,8,128]{3,2,1,0:T(8,128)S(1)}, u32[]{:S(2)}, u32[]{:S(2)}) collective-permute-start(f32[16,3,8,128]{3,2,1,0:T(8,128)S(1)} %get-tuple-element.71.refs_1_.own.l2), channel_id=1, source_target_pairs={{8,16},{16,8},{24,32},{32,24},{40,48},{48,40},{56,64},{64,56},{72,... | collective-permute-start | bytes 589832 | tf_op jit(solution)/shard_map/ppermute | solution.py:623
  59.2 8.7 %collective-permute-start.12 = (f32[16,3,8,128]{3,2,1,0:T(8,128)S(1)}, f32[16,3,8,128]{3,2,1,0:T(8,128)S(1)}, u32[]{:S(2)}, u32[]{:S(2)}) collective-permute-start(f32[16,3,8,128]{3,2,1,0:T(8,128)S(1)} %get-tuple-element.71.refs_1_.own.l2), channel_id=1, source_target_pairs={{0,8},{8,0},{16,24},{24,16},{32,40},{40,32},{48,56},{56,48},{64,72... | collective-permute-start | bytes 589832 | tf_op jit(solution)/shard_map/ppermute | solution.py:623
  68.0 5.7 %collective-permute-start.15 = (f32[3,2,3,8,128]{4,3,2,1,0:T(8,128)S(1)}, f32[3,2,3,8,128]{4,3,2,1,0:T(8,128)S(1)}, u32[]{:S(2)}, u32[]{:S(2)}) collective-permute-start(f32[3,2,3,8,128]{4,3,2,1,0:T(8,128)S(1)} %get-tuple-element.114), channel_id=1, source_target_pairs={{1,2},{2,1},{3,4},{4,3},{5,6},{6,5},{9,10},{10,9},{11,12},{12,11},... | collective-permute-start | bytes 221192 | tf_op jit(solution)/shard_map/ppermute | solution.py:623
  70.2 3.5 %collective-permute-start.14 = (f32[3,2,3,8,128]{4,3,2,1,0:T(8,128)S(1)}, f32[3,2,3,8,128]{4,3,2,1,0:T(8,128)S(1)}, u32[]{:S(2)}, u32[]{:S(2)}) collective-permute-start(f32[3,2,3,8,128]{4,3,2,1,0:T(8,128)S(1)} %get-tuple-element.115), channel_id=1, source_target_pairs={{0,1},{1,0},{2,3},{3,2},{4,5},{5,4},{6,7},{7,6},{8,9},{9,8},{10,11... | collective-permute-start | bytes 221192 | tf_op jit(solution)/shard_map/ppermute | solution.py:623
  75.8 1.2 %collective-permute-start.16 = (f32[36,128]{1,0:T(8,128)S(1)}, f32[36,128]{1,0:T(8,128)S(1)}, u32[]{:S(2)}, u32[]{:S(2)}) collective-permute-start(f32[36,128]{1,0:T(8,128)S(1)} %get-tuple-element.81.refs_0_), channel_id=1, source_target_pairs={{0,1},{1,0},{2,3},{3,2},{4,5},{5,4},{6,7},{7,6},{8,9},{9,8},{10,11... | collective-permute-start | bytes 55304 | tf_op jit(solution)/shard_map/ppermute | solution.py:740
  77.0 3.8 %collective-permute-start.17 = (f32[36,128]{1,0:T(8,128)S(1)}, f32[36,128]{1,0:T(8,128)S(1)}, u32[]{:S(2)}, u32[]{:S(2)}) collective-permute-start(f32[36,128]{1,0:T(8,128)S(1)} %bitcast.93), channel_id=1, source_target_pairs={{0,8},{8,0},{16,24},{24,16},{32,40},{40,32},{48,56},{56,48},{1,9},... | collective-permute-start | bytes 55304 | tf_op jit(solution)/shard_map/ppermute | solution.py:740
  80.8 8.6 %collective-permute-start.18 = (f32[36,128]{1,0:T(8,128)S(1)}, f32[36,128]{1,0:T(8,128)S(1)}, u32[]{:S(2)}, u32[]{:S(2)}) collective-permute-start(f32[36,128]{1,0:T(8,128)S(1)} %bitcast.95), channel_id=1, source_target_pairs={{8,16},{16,8},{24,32},{32,24},{40,48},{48,40},{56,0},{0,56},{9,17}... | collective-permute-start | bytes 55304 | tf_op jit(solution)/shard_map/ppermute | solution.py:740
  89.4 5.6 %collective-permute-start.19 = (f32[36,128]{1,0:T(8,128)S(1)}, f32[36,128]{1,0:T(8,128)S(1)}, u32[]{:S(2)}, u32[]{:S(2)}) collective-permute-start(f32[36,128]{1,0:T(8,128)S(1)} %bitcast.91), channel_id=1, source_target_pairs={{8,48},{48,8},{16,40},{40,16},{24,0},{0,24},{32,56},{56,32},{9,49}... | collective-permute-start | bytes 55304 | tf_op jit(solution)/shard_map/ppermute | solution.py:740
